TPU v7x, 256 devices: a whole 4x4x8 slice. The times are simulated.
256 devices in a mesh: row: 16 (over z_lo, x, core), col: 16 (over y, z_hi).
Axes of the slice: x: 4, y: 4, z: 8 (z_hi: 4, z_lo: 2; z = z_hi * 2 + z_lo), core: 2. Of those that a mesh axis runs over, the one named last changes fastest.
Arguments:
- eigenvectors: float32 [8192, 2048], P('row', 'col'), may hold values from -6 to 6
- householder: float32 [3, 32, 512, 256], P(None, 'row', None, 'col'), may hold values from -6 to 6
Outputs:
- transformed: float32 [8192, 2048], P('row', 'col')
All inputs are finite; a program needn't handle non-finite values.
Results may differ from a plain program's by a relative error of at most 0.0003.
Values sent between devices are 32-bit elements; how exact they have to be, the bound alone decides.
No kernel may reach another device: no remote copies, remote signals or barrier semaphores. Data moves between devices by JAX's collectives and lax.ppermute only.
A program may use at most 192 MiB of HBM per device.

v0:
```python
import functools

import jax
import jax.numpy as jnp
from jax import lax
from jax.experimental import pallas as pl
from jax.experimental.pallas import tpu as pltpu
from jax.sharding import Mesh
from jax.sharding import PartitionSpec as P

ROW = ("zl", "x", "core")
CHIP = ("zl", "x")
COL = ("y", "zh")
SUBS = 2
INTERPRET = False

NN = (((1,), (0,)), ((), ()))
NT = (((1,), (1,)), ((), ()))


def split(value):
    high = value.astype(jnp.bfloat16)
    low = (value - high.astype(jnp.float32)).astype(jnp.bfloat16)
    return high, low


def dot3(left, right, dims=NN):
    (on_left,), (on_right,) = dims[0]
    long_left = jnp.concatenate([left[0], left[0], left[1]], axis=on_left)
    long_right = jnp.concatenate([right[0], right[1], right[0]], axis=on_right)
    return lax.dot_general(long_left, long_right, dims, preferred_element_type=jnp.float32)


def prepare_body(outer_y, index_ref, near_ref, after_ref, before_ref, far0_ref, far1_ref, high_ref, low_ref, v_ref, g_ref, p_ref):
    blocks, quarter, m = near_ref.shape
    n = 4 * quarter
    half = n // 2
    piece = quarter // 4
    at_y = index_ref[0]
    at_z = index_ref[1]
    for outer in range(4):
        for inner in range(4):
            dy, dz = (outer, inner) if outer_y else (inner, outer)
            start = lax.rem(at_y + dy, 4) * quarter + lax.rem(at_z + dz, 4) * piece
            at = pl.ds(inner * piece, piece)
            for block in range(blocks):
                if outer == 0:
                    part = near_ref[block, at, :]
                elif outer == 1:
                    part = after_ref[block, at, :]
                elif outer == 3:
                    part = before_ref[block, at, :]
                elif inner < 2:
                    part = far0_ref[block, at, :]
                else:
                    part = far1_ref[block, pl.ds((inner - 2) * piece, piece), :]
                v_ref[block, pl.ds(start, piece), :] = part
    rows = lax.broadcasted_iota(jnp.int32, (half, half), 0)
    cols = lax.broadcasted_iota(jnp.int32, (half, half), 1)
    eye = rows == cols
    pair = (rows // 2 == cols // 2) & (rows < cols)
    for block in range(blocks):
        vectors = split(v_ref[block])
        g_ref[block] = dot3(vectors, vectors, NT)
    problems = [(block, side) for block in range(blocks) for side in range(2)]
    for at, (block, side) in enumerate(problems):
        lo = side * half
        gram = g_ref[block, lo : lo + half, lo : lo + half]
        on_diagonal = jnp.where(eye, gram, 0.0)
        col_inverse = 1.0 / (0.5 * jnp.sum(on_diagonal, axis=1, keepdims=True))
        row_inverse = 1.0 / (0.5 * jnp.sum(on_diagonal, axis=0, keepdims=True))
        inverse = jnp.where(eye, col_inverse, 0.0)
        p_ref[at] = inverse - jnp.where(pair, gram * col_inverse * row_inverse, 0.0)

    levels = half.bit_length() - 1

    def level(power, carry):
        old_rows = jnp.right_shift(rows, power)
        old_cols = jnp.right_shift(cols, power)
        corner = (jnp.right_shift(old_rows, 1) == jnp.right_shift(old_cols, 1)) & (old_rows < old_cols)
        first = []
        for at, (block, side) in enumerate(problems):
            lo = side * half
            edge = split(jnp.where(corner, g_ref[block, lo : lo + half, lo : lo + half], 0.0))
            first.append(dot3(split(p_ref[at]), edge))
        for at in range(len(problems)):
            old = p_ref[at]
            p_ref[at] = old - dot3(split(first[at]), split(old))
        return carry

    lax.fori_loop(1, levels, level, 0)
    eye = lax.broadcasted_iota(jnp.int32, (m, m), 0) == lax.broadcasted_iota(jnp.int32, (m, m), 1)
    unit = jnp.where(eye, 1.0, 0.0)
    first = [
        dot3(split(p_ref[2 * block]), split(g_ref[block, :half, half:])) for block in range(blocks)
    ]
    corners = [dot3(split(first[block]), split(p_ref[2 * block + 1])) for block in range(blocks)]
    for block in range(blocks):
        vectors = split(v_ref[block])
        top = split(jnp.concatenate([p_ref[2 * block], -corners[block]], axis=1))
        low = split(p_ref[2 * block + 1])
        upper = dot3(top, vectors)
        lower = dot3(low, (vectors[0][half:], vectors[1][half:]))
        scaled = split(jnp.concatenate([upper, lower], axis=0).T)
        whole = unit - dot3(scaled, vectors)
        whole = jnp.where(index_ref[2 + block] == 1, whole, unit)
        high, low = split(whole)
        high_ref[block] = high
        low_ref[block] = low


def prepare(outer_y, index, near, after, before, far0, far1):
    blocks, quarter, m = near.shape
    n = 4 * quarter
    out = jax.ShapeDtypeStruct((blocks, m, m), jnp.bfloat16)
    vmem = pl.BlockSpec(memory_space=pltpu.VMEM)
    return pl.pallas_call(
        functools.partial(prepare_body, outer_y),
        out_shape=(out, out),
        in_specs=[pl.BlockSpec(memory_space=pltpu.SMEM)] + [vmem] * 5,
        out_specs=(vmem, vmem),
        scratch_shapes=[
            pltpu.VMEM((blocks, n, m), jnp.float32),
            pltpu.VMEM((blocks, n, n), jnp.float32),
            pltpu.VMEM((2 * blocks, n // 2, n // 2), jnp.float32),
        ],
        compiler_params=pltpu.CompilerParams(vmem_limit_bytes=14 * 1024 * 1024),
        cost_estimate=pl.CostEstimate(flops=2_000_000_000, bytes_accessed=1_000_000, transcendentals=0),
        interpret=INTERPRET,
        name="prepare",
    )(index, near, after, before, far0, far1)


PAIRS = ((0, 0), (0, 1), (0, 2), (1, 1), (1, 2), (2, 2))


def operate_body(ends_ref, data_ref, own_ref, ah, al, bh, bl, step_ref, rest_ref, add_ref):
    n = ah.shape[1] // 2
    first = ends_ref[0] == 1
    last = ends_ref[1] == 1
    width = data_ref.shape[1]
    held = {(0, 0): (ah, al, 0), (0, 1): (bh, bl, 0), (1, 0): (ah, al, 1), (1, 1): (ah, al, 2), (2, 0): (bh, bl, 1), (2, 1): (ah, al, 3)}

    def part(sweep, block, side=None):
        high, low, at = held[sweep, block]
        if side is None:
            return high[at], low[at]
        rows = pl.ds(side * n, n)
        return high[at, rows, :], low[at, rows, :]

    for sweep in range(3):
        a_top = part(sweep, 0, 0)
        b_top = part(sweep, 1, 0)
        b_low = part(sweep, 1, 1)
        fresh = a_top[0].astype(jnp.float32) + a_top[1].astype(jnp.float32)
        if sweep == 0:
            own = own_ref[...].T
            arriving = jnp.where(first, own[:, :n], 0.0)
            mid = dot3(split(jnp.concatenate([arriving, own[:, n:]], axis=1)), part(0, 0))
            mid = jnp.concatenate([fresh, mid], axis=0)
            v = data_ref[...].T
            done = dot3(split(mid[:, n:]), b_top)
            done = jnp.concatenate([done[:n], done[n:] + dot3(split(v), b_low)], axis=0)
            v = jnp.concatenate([jnp.zeros((n, n), jnp.float32), v], axis=0)
            done = jnp.where(last, jnp.concatenate([mid[:, n:], v], axis=1), done)
        else:
            mid = dot3(split(u), part(sweep, 0, 1))
            mid = jnp.concatenate([mid[:-width], fresh, mid[-width:]], axis=0)
            done = dot3(split(mid[:, n:]), b_top)
            more = dot3(split(v), b_low)
            early = sweep * n
            done = jnp.concatenate(
                [done[:early] + more[:early], done[early : early + n], done[early + n :] + more[early:]], axis=0
            )
        known = (sweep + 1) * n
        u, v = mid[:, :n], done[:, :n]
        out = done[:, n:]
        for k in range(sweep + 1):
            step_ref[PAIRS.index((k, sweep))] = out[k * n : (k + 1) * n]
        add_ref[:, sweep * n : (sweep + 1) * n] = out[known:]
    rest_ref[:, 0:n] = u[: 3 * n]
    rest_ref[:, n : 2 * n] = v[: 3 * n]
    add_ref[:, 3 * n : 4 * n] = u[3 * n :]
    add_ref[:, 4 * n : 5 * n] = v[3 * n :]

    @pl.when(last)
    def _():
        high, low = bh[0], bl[0]
        for k in range(4):
            if k < 3:
                upper = step_ref[PAIRS.index((k, 2))]
                lower = step_ref[PAIRS.index((k, 1))] if k < 2 else jnp.zeros((n, n), jnp.float32)
            else:
                upper = add_ref[:, 2 * n : 3 * n]
                lower = add_ref[:, n : 2 * n]
            result = dot3(split(jnp.concatenate([upper, lower], axis=1)), (high, low))
            if k < 3:
                rest_ref[k * n : (k + 1) * n, 2 * n :] = result
            else:
                add_ref[:, 5 * n :] = result

    @pl.when(jnp.logical_not(last))
    def _():
        rest_ref[:, 2 * n :] = jnp.zeros((3 * n, 2 * n), jnp.float32)
        add_ref[:, 5 * n :] = jnp.zeros((width, 2 * n), jnp.float32)


def operate(ends, data, own, parts):
    m, width = own.shape
    n = m // 2
    vmem = pl.BlockSpec(memory_space=pltpu.VMEM)
    return pl.pallas_call(
        operate_body,
        out_shape=(
            jax.ShapeDtypeStruct((6, n, n), jnp.float32),
            jax.ShapeDtypeStruct((3 * n, 4 * n), jnp.float32),
            jax.ShapeDtypeStruct((width, 7 * n), jnp.float32),
        ),
        in_specs=[pl.BlockSpec(memory_space=pltpu.SMEM)] + [vmem] * 6,
        out_specs=(vmem,) * 3,
        compiler_params=pltpu.CompilerParams(vmem_limit_bytes=20 * 1024 * 1024),
        interpret=INTERPRET,
        name="operate",
    )(ends, data, own, *parts)


def merge_body(odd_ref, mine_ref, other_ref, keep_ref, got_ref, high_ref, low_ref, add_ref):
    n = mine_ref.shape[1]
    odd = odd_ref[0] == 1
    keep = keep_ref[...]
    got = got_ref[...]
    even_parts = [split(jnp.where(odd, other_ref[k], mine_ref[k])) for k in range(6)]
    odd_parts = [split(jnp.where(odd, mine_ref[k], other_ref[k])) for k in range(6)]
    odd_add = jnp.where(odd, keep, got)
    add_parts = split(jnp.where(odd, got, keep))
    for s in range(3):
        total = odd_add[:, s * n : (s + 1) * n]
        for j in range(s + 1):
            columns = slice(j * n, (j + 1) * n)
            total = total + dot3((add_parts[0][:, columns], add_parts[1][:, columns]), odd_parts[PAIRS.index((j, s))])
        add_ref[:, s * n : (s + 1) * n] = total
        for k in range(s + 1):
            total = None
            for j in range(k, s + 1):
                term = dot3(even_parts[PAIRS.index((k, j))], odd_parts[PAIRS.index((j, s))])
                total = term if total is None else total + term
            high_ref[PAIRS.index((k, s))], low_ref[PAIRS.index((k, s))] = split(total)


def merge(odd, mine, other, keep, got):
    n = mine.shape[1]
    half = keep.shape[0]
    vmem = pl.BlockSpec(memory_space=pltpu.VMEM)
    packed = jax.ShapeDtypeStruct((6, n, n), jnp.bfloat16)
    return pl.pallas_call(
        merge_body,
        out_shape=(packed, packed, jax.ShapeDtypeStruct((half, 3 * n), jnp.float32)),
        in_specs=[pl.BlockSpec(memory_space=pltpu.SMEM)] + [vmem] * 4,
        out_specs=(vmem,) * 3,
        compiler_params=pltpu.CompilerParams(vmem_limit_bytes=20 * 1024 * 1024),
        interpret=INTERPRET,
        name="merge",
    )(odd, mine, other, keep, got)


def hop_body(state_ref, high_ref, low_ref, add_ref, out_ref):
    n = high_ref.shape[1]
    high, low = split(state_ref[...])
    count = high.shape[0]
    both = jnp.concatenate([high, low], axis=0)
    for s in range(3):
        total = add_ref[:, s * n : (s + 1) * n]
        for k in range(s + 1):
            at = PAIRS.index((k, s))
            columns = slice(k * n, (k + 1) * n)
            main = lax.dot_general(both[:, columns], high_ref[at], NN, preferred_element_type=jnp.float32)
            side = lax.dot_general(high[:, columns], low_ref[at], NN, preferred_element_type=jnp.float32)
            total = total + (main[:count] + (main[count:] + side))
        out_ref[:, s * n : (s + 1) * n] = total


def hop_on(state, high, low, add):
    vmem = pl.BlockSpec(memory_space=pltpu.VMEM)
    return pl.pallas_call(
        hop_body,
        out_shape=jax.ShapeDtypeStruct(state.shape, jnp.float32),
        in_specs=[vmem] * 4,
        out_specs=vmem,
        compiler_params=pltpu.CompilerParams(vmem_limit_bytes=8 * 1024 * 1024),
        interpret=INTERPRET,
        name="hop",
    )(state, high, low, add)


def ending_body(odd_ref, mine_ref, other_ref, rest_ref, other_rest_ref, keep_ref, got_ref, high_ref, low_ref, add_ref):
    n = mine_ref.shape[1]
    odd = odd_ref[0] == 1
    for k in range(3):
        rows = slice(k * n, (k + 1) * n)
        even_rest = jnp.where(odd, other_rest_ref[rows, : 2 * n], rest_ref[rows, : 2 * n])
        high_ref[rows, : 2 * n], low_ref[rows, : 2 * n] = split(even_rest)
    odd_parts = []
    for k in range(3):
        rows = slice(k * n, (k + 1) * n)
        odd_parts.append(split(jnp.where(odd, rest_ref[rows, :], other_rest_ref[rows, :])))
    for k in range(3):
        total = None
        for j in range(k, 3):
            at = PAIRS.index((k, j))
            term = dot3(split(jnp.where(odd, other_ref[at], mine_ref[at])), odd_parts[j])
            total = term if total is None else total + term
        rows = slice(k * n, (k + 1) * n)
        high_ref[rows, 2 * n :], low_ref[rows, 2 * n :] = split(total)
    even_add = jnp.where(odd, got_ref[...], keep_ref[...])
    odd_add = jnp.where(odd, keep_ref[...], got_ref[...])
    total = odd_add[:, 3 * n :]
    for j in range(3):
        total = total + dot3(split(even_add[:, j * n : (j + 1) * n]), odd_parts[j])
    add_ref[:, : 2 * n] = even_add[:, 3 * n : 5 * n]
    add_ref[:, 2 * n :] = total


def ending(odd, mine, other, rest, other_rest, keep, got):
    n = mine.shape[1]
    vmem = pl.BlockSpec(memory_space=pltpu.VMEM)
    wide = jax.ShapeDtypeStruct((3 * n, 6 * n), jnp.bfloat16)
    return pl.pallas_call(
        ending_body,
        out_shape=(wide, wide, jax.ShapeDtypeStruct((keep.shape[0], 6 * n), jnp.float32)),
        in_specs=[pl.BlockSpec(memory_space=pltpu.SMEM)] + [vmem] * 6,
        out_specs=(vmem,) * 3,
        compiler_params=pltpu.CompilerParams(vmem_limit_bytes=16 * 1024 * 1024),
        interpret=INTERPRET,
        name="ending",
    )(odd, mine, other, rest, other_rest, keep, got)


def finish_body(*refs):
    *state_refs, high_ref, low_ref, add_ref, out_ref = refs
    hops = len(state_refs) // SUBS
    rows = []
    for k in range(SUBS):
        total = state_refs[k * hops][...]
        for ref in state_refs[k * hops + 1 : (k + 1) * hops]:
            total = total + ref[...]
        rows.append(total)
    state = split(jnp.concatenate(rows, axis=0))
    out_ref[...] = dot3(state, (high_ref[...], low_ref[...])) + add_ref[...]


def finish(arrived, high, low, add):
    vmem = pl.BlockSpec(memory_space=pltpu.VMEM)
    states = [value for values in arrived for value in values]
    return pl.pallas_call(
        finish_body,
        out_shape=jax.ShapeDtypeStruct(add.shape, jnp.float32),
        in_specs=[vmem] * (len(states) + 3),
        out_specs=vmem,
        compiler_params=pltpu.CompilerParams(vmem_limit_bytes=16 * 1024 * 1024),
        interpret=INTERPRET,
        name="finish",
    )(*states, high, low, add)


def ring(value, axis, step):
    count = lax.axis_size(axis)
    return lax.ppermute(value, axis, [(k, (k + step) % count) for k in range(count)])


def shifted(value, step):
    count = lax.axis_size(ROW)
    return lax.ppermute(value, ROW, [(k, k + step) for k in range(max(0, -step), min(count, count - step))])


def after_these(value, others):
    return lax.optimization_barrier((value, *others))[0]


def shards(eigenvectors, householder):
    local = jnp.swapaxes(householder, 2, 3)
    position = lax.axis_index(ROW)
    count = lax.axis_size(ROW)
    chips = lax.axis_size(CHIP)
    is_first = position == 0
    is_last = position == count - 1
    is_odd = lax.axis_index("core") == 1
    flipped = lax.axis_index(CHIP) % 2 == 1
    takes_second = is_odd != flipped
    on_last = lax.axis_index(CHIP) == chips - 1
    at = [lax.axis_index("y"), lax.axis_index("zh")]
    one = jnp.int32(1)
    held = jnp.where(is_first, 0, 1)
    index_a = jnp.stack([*at, one, held, one, held]).astype(jnp.int32)
    index_b = jnp.stack([*at, one, held]).astype(jnp.int32)
    ends = jnp.stack([is_first, is_last]).astype(jnp.int32)
    odd = is_odd.astype(jnp.int32).reshape(1)
    local, is_last, is_odd, flipped, takes_second, on_last, index_a, index_b, ends, odd = lax.optimization_barrier(
        (local, is_last, is_odd, flipped, takes_second, on_last, index_a, index_b, ends, odd)
    )
    n = eigenvectors.shape[0] // 2
    stay = jnp.stack([local[0, 1], local[1, 0], local[1, 1], local[2, 0]])
    half = 2 * stay.shape[1]
    before = ring(stay, "zh", 1)
    after = ring(stay, "zh", -1)
    from_next = shifted(local[0, 0], -1)
    from_prior = shifted(local[2, 1], 1)
    far = ring(before, "zh", 1)
    near_a = jnp.concatenate([stay, after, far, before], axis=1)
    moved = jnp.stack([jnp.where(is_last, local[2, 1], from_next), from_prior])
    before = ring(moved, "y", 1)
    after = ring(moved, "y", -1)
    far = ring(moved, "y", 2)
    near_b = jnp.concatenate([moved, after, far, before], axis=1)
    near_a = after_these(near_a, (before, after, far))
    before_a = ring(near_a, "y", 1)
    after_a = ring(near_a, "y", -1)
    give_a = (before_a[:, :half], after_a[:, half:])
    far0_a = ring(give_a[0], "y", 1)
    far1_a = ring(give_a[1], "y", -1)
    before_b = ring(near_b, "zh", 1)
    after_b = ring(near_b, "zh", -1)
    give_b0 = before_b[:, :half]
    give_b1 = after_b[:, half:]
    give_b = after_these(give_b0, give_a), after_these(give_b1, give_a)
    far0_b = ring(give_b[0], "zh", 1)
    far1_b = ring(give_b[1], "zh", -1)
    data = shifted(after_these(eigenvectors[:n], (near_b,)), -1)
    far0_a = after_these(far0_a, give_b)
    parts_a = prepare(True, index_a, near_a, after_a, before_a, far0_a, far1_a)
    parts_b = prepare(False, index_b, after_these(near_b, parts_a), after_b, before_b, far0_b, far1_b)
    step, rest, add = operate(ends, data, eigenvectors, (*parts_a, *parts_b))

    swap = [(0, 1), (1, 0)]
    half = add.shape[0] // 2
    halves = add.reshape(2, half, 7 * n)
    keep = jnp.where(takes_second, halves[1], halves[0])
    give = jnp.where(takes_second, halves[0], halves[1])
    other = lax.ppermute(step, "core", swap)
    got = lax.ppermute(give, "core", swap)
    rest, other, got = lax.optimization_barrier((rest, other, got))
    high, low, chip_add = merge(odd, step, other, keep[:, : 3 * n], got[:, : 3 * n])
    other_rest = lax.ppermute(rest, "core", swap)

    sub = half // SUBS
    adds = [chip_add[k * sub : (k + 1) * sub] for k in range(SUBS)]

    def onward(value, hop):
        return lax.ppermute(value, ROW, [(2 * hop - 2 + side, 2 * hop + 1 - side) for side in range(2)])

    arrived = [[onward(part, 1)] for part in adds]
    for hop in range(2, chips):
        for k in range(SUBS):
            sent = hop_on(arrived[k][-1], high, low, adds[k])
            arrived[k].append(onward(sent, hop))
        if hop == 2:
            rest = after_these(rest, [sent])
            ended = ending(odd, step, other, rest, other_rest, keep, got)
        if hop == 3:
            *latest, high, low = lax.optimization_barrier((*[values[-1] for values in arrived], *ended, high, low))[:]
            for k in range(SUBS):
                arrived[k][-1] = latest[k]
            ended = latest[SUBS:]
    final = finish(arrived, *ended)
    for_prior, for_even, for_odd = [final[:, 2 * k * n : 2 * (k + 1) * n] for k in range(3)]
    got = lax.ppermute(jnp.where(is_odd, for_even, for_odd), "core", swap)
    handed = [
        lax.ppermute(for_prior, ROW, [(2 * (k + 1) + side, 2 * k + 1) for k in range(chips - 1)]) for side in range(2)
    ]
    got, *handed = lax.optimization_barrier((got, *handed))
    one_half = jnp.where(is_odd, jnp.where(on_last, got, handed[1]), for_even)
    other_half = jnp.where(is_odd, jnp.where(on_last, for_odd, handed[0]), got)
    upper = jnp.where(flipped, other_half, one_half)
    lower = jnp.where(flipped, one_half, other_half)
    return jnp.concatenate([upper, lower], axis=0).T


def solution(mesh):
    split_mesh = Mesh(mesh.devices.reshape(2, 4, 2, 4, 4), (*ROW, *COL))
    return jax.shard_map(
        shards,
        mesh=split_mesh,
        in_specs=(P(ROW, COL), P(None, ROW, None, COL)),
        out_specs=P(ROW, COL),
        check_vma=False,
    )
```

profile of v0, /device:TPU:101, one launch (start us, length us, event | category | flops | bytes accessed | tf_op | source)
XLA Modules:
  0.0 129.0 jit_solution(3994476066572358692)
XLA Ops:
  0.2 0.9 slice_bitcast_fusion.3
  1.1 3.4 %collective-permute-start.7 = (f32[4,16,512]{2,1,0:T(8,128)S(1)}, f32[4,16,512]{2,1,0:T(8,128)S(1)}, u32[]{:S(2)}, u32[]{:S(2)}) collective-permute-start(f32[4,16,512]{2,1,0:T(8,128)S(1)} %pad_maximum_fusion.2), channel_id=1, source_target_pairs={{0,1},{1,2},{2,3},{3,0},{4,5},{5,6},{6,7},{7,4},{8,9},{9,10},{10,1... | collective-permute-start | bytes 393224 | tf_op jit(solution)/shard_map/ppermute | solution.py:367
  4.5 2.9 %collective-permute-start = (f32[16,512]{1,0:T(8,128)S(1)}, f32[16,512]{1,0:T(8,128)S(1)}, u32[]{:S(2)}, u32[]{:S(2)}) collective-permute-start(f32[16,512]{1,0:T(8,128)S(1)} %get-tuple-element.104), channel_id=1, source_target_pairs={{16,0},{32,16},{48,32},{64,48},{80,64},{96,80},{112,96},{128,112},... | collective-permute-start | bytes 98312 | tf_op jit(solution)/shard_map/ppermute | solution.py:372
  7.4 2.7 %collective-permute-start.1 = (f32[16,512]{1,0:T(8,128)S(1)}, f32[16,512]{1,0:T(8,128)S(1)}, u32[]{:S(2)}, u32[]{:S(2)}) collective-permute-start(f32[16,512]{1,0:T(8,128)S(1)} %get-tuple-element.105), channel_id=1, source_target_pairs={{0,16},{16,32},{32,48},{48,64},{64,80},{80,96},{96,112},{112,128},... | collective-permute-start | bytes 98312 | tf_op jit(solution)/shard_map/ppermute | solution.py:372
  10.2 3.9 %collective-permute-start.8 = (f32[4,16,512]{2,1,0:T(8,128)S(1)}, f32[4,16,512]{2,1,0:T(8,128)S(1)}, u32[]{:S(2)}, u32[]{:S(2)}) collective-permute-start(f32[4,16,512]{2,1,0:T(8,128)S(1)} %collective-permute-done.7), channel_id=1, source_target_pairs={{0,1},{1,2},{2,3},{3,0},{4,5},{5,6},{6,7},{7,4},{8,9},{9,10},{10,1... | collective-permute-start | bytes 393224 | tf_op jit(solution)/shard_map/ppermute | solution.py:367
  14.1 0.8 select_bitcast_fusion
  14.9 2.8 %collective-permute-start.2 = (f32[2,16,512]{2,1,0:T(8,128)S(1)}, f32[2,16,512]{2,1,0:T(8,128)S(1)}, u32[]{:S(2)}, u32[]{:S(2)}) collective-permute-start(f32[2,16,512]{2,1,0:T(8,128)S(1)} %pad_maximum_fusion.3), channel_id=1, source_target_pairs={{0,12},{4,0},{8,4},{12,8},{1,13},{5,1},{9,5},{13,9},{2,14},{6,2},{... | collective-permute-start | bytes 196616 | tf_op jit(solution)/shard_map/ppermute | solution.py:367
  17.7 0.4 collective-permute-start.3
  18.0 0.7 collective-permute-start.4
  18.7 0.2 collective-permute-done.8
  19.0 1.7 %collective-permute-done.2 = f32[2,16,512]{2,1,0:T(8,128)S(1)} collective-permute-done((f32[2,16,512]{2,1,0:T(8,128)S(1)}, f32[2,16,512]{2,1,0:T(8,128)S(1)}, u32[]{:S(2)}, u32[]{:S(2)}) %collective-permute-start.2) | collective-permute-done | bytes 65568 | tf_op jit(solution)/shard_map/ppermute | solution.py:367
  20.7 2.2 %collective-permute-done.3 = f32[2,16,512]{2,1,0:T(8,128)S(1)} collective-permute-done((f32[2,16,512]{2,1,0:T(8,128)S(1)}, f32[2,16,512]{2,1,0:T(8,128)S(1)}, u32[]{:S(2)}, u32[]{:S(2)}) %collective-permute-start.3) | collective-permute-done | bytes 65568 | tf_op jit(solution)/shard_map/ppermute | solution.py:367
  22.9 1.8 %collective-permute-done.4 = f32[2,16,512]{2,1,0:T(8,128)S(1)} collective-permute-done((f32[2,16,512]{2,1,0:T(8,128)S(1)}, f32[2,16,512]{2,1,0:T(8,128)S(1)}, u32[]{:S(2)}, u32[]{:S(2)}) %collective-permute-start.4) | collective-permute-done | bytes 65568 | tf_op jit(solution)/shard_map/ppermute | solution.py:367
  24.6 2.7 %collective-permute-start.9 = (f32[4,64,512]{2,1,0:T(8,128)S(1)}, f32[4,64,512]{2,1,0:T(8,128)S(1)}, u32[]{:S(2)}, u32[]{:S(2)}) collective-permute-start(f32[4,64,512]{2,1,0:T(8,128)S(1)} %pad_maximum_fusion.near_ref), channel_id=1, source_target_pairs={{0,12},{4,0},{8,4},{12,8},{1,13},{5,1},{9,5},{13,9},{2,14},{6,2},{... | collective-permute-start | bytes 1572872 | tf_op jit(solution)/shard_map/ppermute | solution.py:367
  27.4 3.6 %collective-permute-start.12 = (f32[2,64,512]{2,1,0:T(8,128)S(1)}, f32[2,64,512]{2,1,0:T(8,128)S(1)}, u32[]{:S(2)}, u32[]{:S(2)}) collective-permute-start(f32[2,64,512]{2,1,0:T(8,128)S(1)} %pad_maximum_fusion.1.near_ref), channel_id=1, source_target_pairs={{0,1},{1,2},{2,3},{3,0},{4,5},{5,6},{6,7},{7,4},{8,9},{9,10},{10,1... | collective-permute-start | bytes 786440 | tf_op jit(solution)/shard_map/ppermute | solution.py:367
  31.0 7.9 %collective-permute-done.10.before_ref = f32[4,64,512]{2,1,0:T(8,128)S(1)} collective-permute-done((f32[4,64,512]{2,1,0:T(8,128)S(1)}, f32[4,64,512]{2,1,0:T(8,128)S(1)}, u32[]{:S(2)}, u32[]{:S(2)}) %collective-permute-start.10) | collective-permute-done | bytes 524320 | tf_op jit(solution)/shard_map/ppermute | solution.py:367
  39.0 2.7 %collective-permute-start.14 = (f32[4,32,512]{2,1,0:T(8,128)S(1)}, f32[4,32,512]{2,1,0:T(8,128)S(1)}, u32[]{:S(2)}, u32[]{:S(2)}) collective-permute-start(f32[4,32,512]{2,1,0:T(8,128)S(1)} %slice.87), channel_id=1, source_target_pairs={{0,12},{4,0},{8,4},{12,8},{1,13},{5,1},{9,5},{13,9},{2,14},{6,2},{... | collective-permute-start | bytes 786440 | tf_op jit(solution)/shard_map/ppermute | solution.py:367
  41.8 3.8 %collective-permute-start.5 = (f32[256,128]{1,0:T(8,128)S(1)}, f32[256,128]{1,0:T(8,128)S(1)}, u32[]{:S(2)}, u32[]{:S(2)}) collective-permute-start(f32[256,128]{1,0:T(8,128)S(1)} %slice.65), channel_id=1, source_target_pairs={{16,0},{32,16},{48,32},{64,48},{80,64},{96,80},{112,96},{128,112},... | collective-permute-start | bytes 393224 | tf_op jit(solution)/shard_map/ppermute | solution.py:372
  45.7 3.6 %collective-permute-start.15 = (f32[2,32,512]{2,1,0:T(8,128)S(1)}, f32[2,32,512]{2,1,0:T(8,128)S(1)}, u32[]{:S(2)}, u32[]{:S(2)}) collective-permute-start(f32[2,32,512]{2,1,0:T(8,128)S(1)} %slice.86), channel_id=1, source_target_pairs={{0,1},{1,2},{2,3},{3,0},{4,5},{5,6},{6,7},{7,4},{8,9},{9,10},{10,1... | collective-permute-start | bytes 393224 | tf_op jit(solution)/shard_map/ppermute | solution.py:367
  49.3 9.2 %prepare.2 = (bf16[4,512,512]{2,1,0:T(8,128)(2,1)S(1)}, bf16[4,512,512]{2,1,0:T(8,128)(2,1)S(1)}) custom-call(s32[6]{0:T(128)S(1)} %stack.43.index_ref, f32[4,64,512]{2,1,0:T(8,128)S(1)} %pad_maximum_fusion.near_ref, f32[4,64,512]{2,1,0:T(8,128)S(1)} %collective-permute-done.9.after_ref, f32[4,64,512]{2,1,0:T(8,128)S(1)} %collective-permute-done.10.before_ref, ...), custom_call_target="tpu_custom_call" | custom-call | flops 2000000000 | bytes 1000000 | tf_op jit(solution)/shard_map/prepare/pallas_call | solution.py:117
  58.5 5.9 %prepare.3 = (bf16[2,512,512]{2,1,0:T(8,128)(2,1)S(1)}, bf16[2,512,512]{2,1,0:T(8,128)(2,1)S(1)}) custom-call(s32[4]{0:T(128)S(1)} %pad_add_fusion.index_ref, f32[2,64,512]{2,1,0:T(8,128)S(1)} %pad_maximum_fusion.1.near_ref, f32[2,64,512]{2,1,0:T(8,128)S(1)} %collective-permute-done.13.after_ref, f32[2,64,512]{2,1,0:T(8,128)S(1)} %collective-permute-done.12.before_ref, ...), custom_call_target="tpu_custom_call" | custom-call | flops 2000000000 | bytes 1000000 | tf_op jit(solution)/shard_map/prepare/pallas_call | solution.py:117
  64.4 4.5 %operate.1 = (f32[6,256,256]{2,1,0:T(8,128)S(1)}, f32[768,1024]{1,0:T(8,128)S(1)}, f32[128,1792]{1,0:T(8,128)S(1)}) custom-call(s32[2]{0:T(128)S(1)} %add_convert_fusion.ends_ref, f32[256,128]{1,0:T(8,128)S(1)} %collective-permute-done.5.data_ref, f32[512,128]{1,0:T(8,128)S(1)} %copy-done, bf16[4,512,512]{2,1,0:T(8,128)(2,1)S(1)} %get-tuple-element.61.ah, ...), custom_call_target="tpu_custom_call" | custom-call | tf_op jit(solution)/shard_map/operate/pallas_call | solution.py:212
  68.8 0.7 collective-permute-start.17
  69.6 0.1 collective-permute-start.18
  69.7 3.5 %collective-permute-done.18.got_ref = f32[64,1792]{1,0:T(8,128)S(1)} collective-permute-done((f32[64,1792]{1,0:T(8,128)S(1)}, f32[64,1792]{1,0:T(8,128)S(1)}, u32[]{:S(2)}, u32[]{:S(2)}) %collective-permute-start.18) | collective-permute-done | bytes 458784 | tf_op jit(solution)/shard_map/ppermute | solution.py:439
  73.2 0.4 collective-permute-start.25
  73.6 1.7 %merge.1 = (bf16[6,256,256]{2,1,0:T(8,128)(2,1)S(1)}, bf16[6,256,256]{2,1,0:T(8,128)(2,1)S(1)}, f32[64,768]{1,0:T(8,128)S(1)}) custom-call(s32[1]{0:T(128)} %bitcast.6.odd_ref, f32[6,256,256]{2,1,0:T(8,128)S(1)} %get-tuple-element.67.mine_ref, f32[6,256,256]{2,1,0:T(8,128)S(1)} %collective-permute-done.17.other_ref, f32[64,768]{1,0:T(8,128)S(1)} %slice.89.keep_ref, ...), custom_call_target="tpu_custom_call" | custom-call | tf_op jit(solution)/shard_map/merge/pallas_call | solution.py:255
  75.3 0.7 collective-permute-start.22
  76.0 0.7 collective-permute-start.19
  76.7 0.4 hop.14
  77.1 0.7 collective-permute-start.23
  77.7 0.4 hop.12
  78.1 0.7 collective-permute-start.20
  78.8 0.4 hop.15
  79.2 0.7 collective-permute-start.24
  79.8 0.4 hop.13
  80.2 0.7 collective-permute-start.21
  80.9 4.1 %ending.1 = (bf16[768,1536]{1,0:T(8,128)(2,1)S(1)}, bf16[768,1536]{1,0:T(8,128)(2,1)S(1)}, f32[64,1536]{1,0:T(8,128)S(1)}) custom-call(s32[1]{0:T(128)} %bitcast.6.odd_ref, f32[6,256,256]{2,1,0:T(8,128)S(1)} %get-tuple-element.67.mine_ref, f32[6,256,256]{2,1,0:T(8,128)S(1)} %collective-permute-done.17.other_ref, f32[768,1024]{1,0:T(8,128)S(1)} %get-tuple-element.77.rest_ref, ...), custom_call_target="tpu_custom_call" | custom-call | tf_op jit(solution)/shard_map/ending/pallas_call | solution.py:327
  85.0 0.4 hop.20
  85.4 0.7 collective-permute-start.30
  86.0 0.4 hop.16
  86.4 0.7 collective-permute-start.26
  87.1 0.4 hop.21
  87.4 0.7 collective-permute-start.31
  88.1 0.4 hop.17
  88.5 0.7 collective-permute-start.27
  89.2 0.4 hop.22
  89.5 1.3 collective-permute-start.32
  90.8 0.4 hop.18
  91.2 1.3 collective-permute-start.28
  92.5 19.7 %collective-permute-done.32.state_ref.refs_12_ = f32[32,768]{1,0:T(8,128)S(1)} collective-permute-done((f32[32,768]{1,0:T(8,128)S(1)}, f32[32,768]{1,0:T(8,128)S(1)}, u32[]{:S(2)}, u32[]{:S(2)}) %collective-permute-start.32) | collective-permute-done | bytes 98336 | tf_op jit(solution)/shard_map/ppermute | solution.py:448
  112.2 0.4 hop.23
  112.6 1.3 %collective-permute-start.33 = (f32[32,768]{1,0:T(8,128)S(1)}, f32[32,768]{1,0:T(8,128)S(1)}, u32[]{:S(2)}, u32[]{:S(2)}) collective-permute-start(f32[32,768]{1,0:T(8,128)S(1)} %hop.23), channel_id=1, source_target_pairs={{192,240},{208,224},{193,241},{209,225},{194,242},{210,226},{195,2... | collective-permute-start | bytes 294920 | tf_op jit(solution)/shard_map/ppermute | solution.py:448
  113.9 0.4 hop.19
  114.2 1.3 %collective-permute-start.29 = (f32[32,768]{1,0:T(8,128)S(1)}, f32[32,768]{1,0:T(8,128)S(1)}, u32[]{:S(2)}, u32[]{:S(2)}) collective-permute-start(f32[32,768]{1,0:T(8,128)S(1)} %hop.19), channel_id=1, source_target_pairs={{192,240},{208,224},{193,241},{209,225},{194,242},{210,226},{195,2... | collective-permute-start | bytes 294920 | tf_op jit(solution)/shard_map/ppermute | solution.py:448
  115.5 0.7 collective-permute-done.33.refs_13_
  116.3 2.1 %collective-permute-done.29.refs_6_ = f32[32,768]{1,0:T(8,128)S(1)} collective-permute-done((f32[32,768]{1,0:T(8,128)S(1)}, f32[32,768]{1,0:T(8,128)S(1)}, u32[]{:S(2)}, u32[]{:S(2)}) %collective-permute-start.29) | collective-permute-done | bytes 98336 | tf_op jit(solution)/shard_map/ppermute | solution.py:448
  118.4 1.3 %finish.1 = f32[64,1536]{1,0:T(8,128)S(1)} custom-call(f32[32,768]{1,0:T(8,128)S(1)} %collective-permute-done.19.state_ref.refs_0_, f32[32,768]{1,0:T(8,128)S(1)} %collective-permute-done.20.state_ref.refs_1_, f32[32,768]{1,0:T(8,128)S(1)} %collective-permute-done.21.state_ref.refs_2_, f32[32,768]{1,0:T(8,128)S(1)} %collective-permute-done.26.state_ref.refs_3_, ...), custom_call_target="tpu_custom_call" | custom-call | tf_op jit(solution)/shard_map/finish/pallas_call | solution.py:354
  119.7 0.6 collective-permute-start.34
  120.4 1.3 collective-permute-start.35
  121.7 1.9 %collective-permute-start.36 = (f32[64,512]{1,0:T(8,128)S(1)}, f32[64,512]{1,0:T(8,128)S(1)}, u32[]{:S(2)}, u32[]{:S(2)}) collective-permute-start(f32[64,512]{1,0:T(8,128)S(1)} %get-tuple-element.96), channel_id=1, source_target_pairs={{48,16},{80,48},{112,80},{144,112},{176,144},{208,176},{240,208},{... | collective-permute-start | bytes 393224 | tf_op jit(solution)/shard_map/ppermute | solution.py:467
  123.6 3.7 %collective-permute-done.35 = f32[64,512]{1,0:T(8,128)S(1)} collective-permute-done((f32[64,512]{1,0:T(8,128)S(1)}, f32[64,512]{1,0:T(8,128)S(1)}, u32[]{:S(2)}, u32[]{:S(2)}) %collective-permute-start.35) | collective-permute-done | bytes 131104 | tf_op jit(solution)/shard_map/ppermute | solution.py:467
  127.3 0.7 collective-permute-done.36
  128.2 0.8 copy.3
  (53 shorter events, 1.0 us)
Async XLA Ops:
  0.0 41.7 %copy-start = (f32[512,128]{1,0:T(8,128)S(1)}, f32[512,128]{1,0:T(8,128)}, u32[]{:S(2)}) copy-start(f32[512,128]{1,0:T(8,128)} %own_ref.1) | copy-start | bytes 786436
  1.1 9.1 %collective-permute-start.7 = (f32[4,16,512]{2,1,0:T(8,128)S(1)}, f32[4,16,512]{2,1,0:T(8,128)S(1)}, u32[]{:S(2)}, u32[]{:S(2)}) collective-permute-start(f32[4,16,512]{2,1,0:T(8,128)S(1)} %pad_maximum_fusion.2), channel_id=1, source_target_pairs={{0,1},{1,2},{2,3},{3,0},{4,5},{5,6},{6,7},{7,4},{8,9},{9,10},{10,1... | collective-permute-start | bytes 393224 | tf_op jit(solution)/shard_map/ppermute | solution.py:367
  4.5 9.6 %collective-permute-start = (f32[16,512]{1,0:T(8,128)S(1)}, f32[16,512]{1,0:T(8,128)S(1)}, u32[]{:S(2)}, u32[]{:S(2)}) collective-permute-start(f32[16,512]{1,0:T(8,128)S(1)} %get-tuple-element.104), channel_id=1, source_target_pairs={{16,0},{32,16},{48,32},{64,48},{80,64},{96,80},{112,96},{128,112},... | collective-permute-start | bytes 98312 | tf_op jit(solution)/shard_map/ppermute | solution.py:372
  7.4 11.4 %collective-permute-start.6 = (f32[4,16,512]{2,1,0:T(8,128)S(1)}, f32[4,16,512]{2,1,0:T(8,128)S(1)}, u32[]{:S(2)}, u32[]{:S(2)}) collective-permute-start(f32[4,16,512]{2,1,0:T(8,128)S(1)} %pad_maximum_fusion.2), channel_id=1, source_target_pairs={{0,3},{1,0},{2,1},{3,2},{4,7},{5,4},{6,5},{7,6},{8,11},{9,8},{10,9... | collective-permute-start | bytes 393224 | tf_op jit(solution)/shard_map/ppermute | solution.py:367
  7.4 7.4 %collective-permute-start.1 = (f32[16,512]{1,0:T(8,128)S(1)}, f32[16,512]{1,0:T(8,128)S(1)}, u32[]{:S(2)}, u32[]{:S(2)}) collective-permute-start(f32[16,512]{1,0:T(8,128)S(1)} %get-tuple-element.105), channel_id=1, source_target_pairs={{0,16},{16,32},{32,48},{48,64},{64,80},{80,96},{96,112},{112,128},... | collective-permute-start | bytes 98312 | tf_op jit(solution)/shard_map/ppermute | solution.py:372
  10.2 8.8 %collective-permute-start.8 = (f32[4,16,512]{2,1,0:T(8,128)S(1)}, f32[4,16,512]{2,1,0:T(8,128)S(1)}, u32[]{:S(2)}, u32[]{:S(2)}) collective-permute-start(f32[4,16,512]{2,1,0:T(8,128)S(1)} %collective-permute-done.7), channel_id=1, source_target_pairs={{0,1},{1,2},{2,3},{3,0},{4,5},{5,6},{6,7},{7,4},{8,9},{9,10},{10,1... | collective-permute-start | bytes 393224 | tf_op jit(solution)/shard_map/ppermute | solution.py:367
  14.9 5.8 %collective-permute-start.2 = (f32[2,16,512]{2,1,0:T(8,128)S(1)}, f32[2,16,512]{2,1,0:T(8,128)S(1)}, u32[]{:S(2)}, u32[]{:S(2)}) collective-permute-start(f32[2,16,512]{2,1,0:T(8,128)S(1)} %pad_maximum_fusion.3), channel_id=1, source_target_pairs={{0,12},{4,0},{8,4},{12,8},{1,13},{5,1},{9,5},{13,9},{2,14},{6,2},{... | collective-permute-start | bytes 196616 | tf_op jit(solution)/shard_map/ppermute | solution.py:367
  17.7 5.2 %collective-permute-start.3 = (f32[2,16,512]{2,1,0:T(8,128)S(1)}, f32[2,16,512]{2,1,0:T(8,128)S(1)}, u32[]{:S(2)}, u32[]{:S(2)}) collective-permute-start(f32[2,16,512]{2,1,0:T(8,128)S(1)} %pad_maximum_fusion.3), channel_id=1, source_target_pairs={{0,8},{4,12},{8,0},{12,4},{1,9},{5,13},{9,1},{13,5},{2,10},{6,14},... | collective-permute-start | bytes 196616 | tf_op jit(solution)/shard_map/ppermute | solution.py:367
  18.0 6.6 %collective-permute-start.4 = (f32[2,16,512]{2,1,0:T(8,128)S(1)}, f32[2,16,512]{2,1,0:T(8,128)S(1)}, u32[]{:S(2)}, u32[]{:S(2)}) collective-permute-start(f32[2,16,512]{2,1,0:T(8,128)S(1)} %pad_maximum_fusion.3), channel_id=1, source_target_pairs={{0,4},{4,8},{8,12},{12,0},{1,5},{5,9},{9,13},{13,1},{2,6},{6,10},{... | collective-permute-start | bytes 196616 | tf_op jit(solution)/shard_map/ppermute | solution.py:367
  24.6 14.2 %collective-permute-start.10 = (f32[4,64,512]{2,1,0:T(8,128)S(1)}, f32[4,64,512]{2,1,0:T(8,128)S(1)}, u32[]{:S(2)}, u32[]{:S(2)}) collective-permute-start(f32[4,64,512]{2,1,0:T(8,128)S(1)} %pad_maximum_fusion.near_ref), channel_id=1, source_target_pairs={{0,4},{4,8},{8,12},{12,0},{1,5},{5,9},{9,13},{13,1},{2,6},{6,10},{... | collective-permute-start | bytes 1572872 | tf_op jit(solution)/shard_map/ppermute | solution.py:367
  24.6 14.3 %collective-permute-start.9 = (f32[4,64,512]{2,1,0:T(8,128)S(1)}, f32[4,64,512]{2,1,0:T(8,128)S(1)}, u32[]{:S(2)}, u32[]{:S(2)}) collective-permute-start(f32[4,64,512]{2,1,0:T(8,128)S(1)} %pad_maximum_fusion.near_ref), channel_id=1, source_target_pairs={{0,12},{4,0},{8,4},{12,8},{1,13},{5,1},{9,5},{13,9},{2,14},{6,2},{... | collective-permute-start | bytes 1572872 | tf_op jit(solution)/shard_map/ppermute | solution.py:367
  27.3 18.2 %collective-permute-start.13 = (f32[2,64,512]{2,1,0:T(8,128)S(1)}, f32[2,64,512]{2,1,0:T(8,128)S(1)}, u32[]{:S(2)}, u32[]{:S(2)}) collective-permute-start(f32[2,64,512]{2,1,0:T(8,128)S(1)} %pad_maximum_fusion.1.near_ref), channel_id=1, source_target_pairs={{0,3},{1,0},{2,1},{3,2},{4,7},{5,4},{6,5},{7,6},{8,11},{9,8},{10,9... | collective-permute-start | bytes 786440 | tf_op jit(solution)/shard_map/ppermute | solution.py:367
  27.4 18.2 %collective-permute-start.12 = (f32[2,64,512]{2,1,0:T(8,128)S(1)}, f32[2,64,512]{2,1,0:T(8,128)S(1)}, u32[]{:S(2)}, u32[]{:S(2)}) collective-permute-start(f32[2,64,512]{2,1,0:T(8,128)S(1)} %pad_maximum_fusion.1.near_ref), channel_id=1, source_target_pairs={{0,1},{1,2},{2,3},{3,0},{4,5},{5,6},{6,7},{7,4},{8,9},{9,10},{10,1... | collective-permute-start | bytes 786440 | tf_op jit(solution)/shard_map/ppermute | solution.py:367
  38.9 10.4 %collective-permute-start.11 = (f32[4,32,512]{2,1,0:T(8,128)S(1)}, f32[4,32,512]{2,1,0:T(8,128)S(1)}, u32[]{:S(2)}, u32[]{:S(2)}) collective-permute-start(f32[4,32,512]{2,1,0:T(8,128)S(1)} %slice.85), channel_id=1, source_target_pairs={{0,4},{4,8},{8,12},{12,0},{1,5},{5,9},{9,13},{13,1},{2,6},{6,10},{... | collective-permute-start | bytes 786440 | tf_op jit(solution)/shard_map/ppermute | solution.py:367
  39.0 10.3 %collective-permute-start.14 = (f32[4,32,512]{2,1,0:T(8,128)S(1)}, f32[4,32,512]{2,1,0:T(8,128)S(1)}, u32[]{:S(2)}, u32[]{:S(2)}) collective-permute-start(f32[4,32,512]{2,1,0:T(8,128)S(1)} %slice.87), channel_id=1, source_target_pairs={{0,12},{4,0},{8,4},{12,8},{1,13},{5,1},{9,5},{13,9},{2,14},{6,2},{... | collective-permute-start | bytes 786440 | tf_op jit(solution)/shard_map/ppermute | solution.py:367
  41.8 22.6 %collective-permute-start.5 = (f32[256,128]{1,0:T(8,128)S(1)}, f32[256,128]{1,0:T(8,128)S(1)}, u32[]{:S(2)}, u32[]{:S(2)}) collective-permute-start(f32[256,128]{1,0:T(8,128)S(1)} %slice.65), channel_id=1, source_target_pairs={{16,0},{32,16},{48,32},{64,48},{80,64},{96,80},{112,96},{128,112},... | collective-permute-start | bytes 393224 | tf_op jit(solution)/shard_map/ppermute | solution.py:372
  45.6 12.8 %collective-permute-start.16 = (f32[2,32,512]{2,1,0:T(8,128)S(1)}, f32[2,32,512]{2,1,0:T(8,128)S(1)}, u32[]{:S(2)}, u32[]{:S(2)}) collective-permute-start(f32[2,32,512]{2,1,0:T(8,128)S(1)} %slice.88), channel_id=1, source_target_pairs={{0,3},{1,0},{2,1},{3,2},{4,7},{5,4},{6,5},{7,6},{8,11},{9,8},{10,9... | collective-permute-start | bytes 393224 | tf_op jit(solution)/shard_map/ppermute | solution.py:367
  45.7 12.7 %collective-permute-start.15 = (f32[2,32,512]{2,1,0:T(8,128)S(1)}, f32[2,32,512]{2,1,0:T(8,128)S(1)}, u32[]{:S(2)}, u32[]{:S(2)}) collective-permute-start(f32[2,32,512]{2,1,0:T(8,128)S(1)} %slice.86), channel_id=1, source_target_pairs={{0,1},{1,2},{2,3},{3,0},{4,5},{5,6},{6,7},{7,4},{8,9},{9,10},{10,1... | collective-permute-start | bytes 393224 | tf_op jit(solution)/shard_map/ppermute | solution.py:367
  68.8 4.4 %collective-permute-start.17 = (f32[6,256,256]{2,1,0:T(8,128)S(1)}, f32[6,256,256]{2,1,0:T(8,128)S(1)}, u32[]{:S(2)}, u32[]{:S(2)}) collective-permute-start(f32[6,256,256]{2,1,0:T(8,128)S(1)} %get-tuple-element.67.mine_ref), channel_id=1, source_target_pairs={{0,16},{16,0},{1,17},{17,1},{2,18},{18,2},{3,19},{19,3},{4,20},{20... | collective-permute-start | bytes 4718600 | tf_op jit(solution)/shard_map/ppermute | solution.py:438
  69.6 3.6 %collective-permute-start.18 = (f32[64,1792]{1,0:T(8,128)S(1)}, f32[64,1792]{1,0:T(8,128)S(1)}, u32[]{:S(2)}, u32[]{:S(2)}) collective-permute-start(f32[64,1792]{1,0:T(8,128)S(1)} %get-tuple-element.95), channel_id=1, source_target_pairs={{0,16},{16,0},{1,17},{17,1},{2,18},{18,2},{3,19},{19,3},{4,20},{20... | collective-permute-start | bytes 1376264 | tf_op jit(solution)/shard_map/ppermute | solution.py:439
  73.2 7.7 %collective-permute-start.25 = (f32[768,1024]{1,0:T(8,128)S(1)}, f32[768,1024]{1,0:T(8,128)S(1)}, u32[]{:S(2)}, u32[]{:S(2)}) collective-permute-start(f32[768,1024]{1,0:T(8,128)S(1)} %get-tuple-element.77.rest_ref), channel_id=1, source_target_pairs={{0,16},{16,0},{1,17},{17,1},{2,18},{18,2},{3,19},{19,3},{4,20},{20... | collective-permute-start | bytes 9437192 | tf_op jit(solution)/shard_map/ppermute | solution.py:442
  75.3 1.4 %collective-permute-start.22 = (f32[32,768]{1,0:T(8,128)S(1)}, f32[32,768]{1,0:T(8,128)S(1)}, u32[]{:S(2)}, u32[]{:S(2)}) collective-permute-start(f32[32,768]{1,0:T(8,128)S(1)} %get-tuple-element.98.add_ref), channel_id=1, source_target_pairs={{0,48},{16,32},{1,49},{17,33},{2,50},{18,34},{3,51},{19,35},{4,52}... | collective-permute-start | bytes 294920 | tf_op jit(solution)/shard_map/ppermute | solution.py:448
  76.0 1.7 %collective-permute-start.19 = (f32[32,768]{1,0:T(8,128)S(1)}, f32[32,768]{1,0:T(8,128)S(1)}, u32[]{:S(2)}, u32[]{:S(2)}) collective-permute-start(f32[32,768]{1,0:T(8,128)S(1)} %get-tuple-element.99.add_ref), channel_id=1, source_target_pairs={{0,48},{16,32},{1,49},{17,33},{2,50},{18,34},{3,51},{19,35},{4,52}... | collective-permute-start | bytes 294920 | tf_op jit(solution)/shard_map/ppermute | solution.py:448
  77.1 1.7 %collective-permute-start.23 = (f32[32,768]{1,0:T(8,128)S(1)}, f32[32,768]{1,0:T(8,128)S(1)}, u32[]{:S(2)}, u32[]{:S(2)}) collective-permute-start(f32[32,768]{1,0:T(8,128)S(1)} %hop.14), channel_id=1, source_target_pairs={{32,80},{48,64},{33,81},{49,65},{34,82},{50,66},{35,83},{51,67},{3... | collective-permute-start | bytes 294920 | tf_op jit(solution)/shard_map/ppermute | solution.py:448
  78.1 1.7 %collective-permute-start.20 = (f32[32,768]{1,0:T(8,128)S(1)}, f32[32,768]{1,0:T(8,128)S(1)}, u32[]{:S(2)}, u32[]{:S(2)}) collective-permute-start(f32[32,768]{1,0:T(8,128)S(1)} %hop.12), channel_id=1, source_target_pairs={{32,80},{48,64},{33,81},{49,65},{34,82},{50,66},{35,83},{51,67},{3... | collective-permute-start | bytes 294920 | tf_op jit(solution)/shard_map/ppermute | solution.py:448
  79.2 5.8 %collective-permute-start.24 = (f32[32,768]{1,0:T(8,128)S(1)}, f32[32,768]{1,0:T(8,128)S(1)}, u32[]{:S(2)}, u32[]{:S(2)}) collective-permute-start(f32[32,768]{1,0:T(8,128)S(1)} %hop.15), channel_id=1, source_target_pairs={{64,112},{80,96},{65,113},{81,97},{66,114},{82,98},{67,115},{83,99... | collective-permute-start | bytes 294920 | tf_op jit(solution)/shard_map/ppermute | solution.py:448
  80.2 4.8 %collective-permute-start.21 = (f32[32,768]{1,0:T(8,128)S(1)}, f32[32,768]{1,0:T(8,128)S(1)}, u32[]{:S(2)}, u32[]{:S(2)}) collective-permute-start(f32[32,768]{1,0:T(8,128)S(1)} %hop.13), channel_id=1, source_target_pairs={{64,112},{80,96},{65,113},{81,97},{66,114},{82,98},{67,115},{83,99... | collective-permute-start | bytes 294920 | tf_op jit(solution)/shard_map/ppermute | solution.py:448
  85.4 1.7 %collective-permute-start.30 = (f32[32,768]{1,0:T(8,128)S(1)}, f32[32,768]{1,0:T(8,128)S(1)}, u32[]{:S(2)}, u32[]{:S(2)}) collective-permute-start(f32[32,768]{1,0:T(8,128)S(1)} %hop.20), channel_id=1, source_target_pairs={{96,144},{112,128},{97,145},{113,129},{98,146},{114,130},{99,147},... | collective-permute-start | bytes 294920 | tf_op jit(solution)/shard_map/ppermute | solution.py:448
  86.4 1.7 %collective-permute-start.26 = (f32[32,768]{1,0:T(8,128)S(1)}, f32[32,768]{1,0:T(8,128)S(1)}, u32[]{:S(2)}, u32[]{:S(2)}) collective-permute-start(f32[32,768]{1,0:T(8,128)S(1)} %hop.16), channel_id=1, source_target_pairs={{96,144},{112,128},{97,145},{113,129},{98,146},{114,130},{99,147},... | collective-permute-start | bytes 294920 | tf_op jit(solution)/shard_map/ppermute | solution.py:448
  87.4 1.7 %collective-permute-start.31 = (f32[32,768]{1,0:T(8,128)S(1)}, f32[32,768]{1,0:T(8,128)S(1)}, u32[]{:S(2)}, u32[]{:S(2)}) collective-permute-start(f32[32,768]{1,0:T(8,128)S(1)} %hop.21), channel_id=1, source_target_pairs={{128,176},{144,160},{129,177},{145,161},{130,178},{146,162},{131,1... | collective-permute-start | bytes 294920 | tf_op jit(solution)/shard_map/ppermute | solution.py:448
  88.5 2.3 %collective-permute-start.27 = (f32[32,768]{1,0:T(8,128)S(1)}, f32[32,768]{1,0:T(8,128)S(1)}, u32[]{:S(2)}, u32[]{:S(2)}) collective-permute-start(f32[32,768]{1,0:T(8,128)S(1)} %hop.17), channel_id=1, source_target_pairs={{128,176},{144,160},{129,177},{145,161},{130,178},{146,162},{131,1... | collective-permute-start | bytes 294920 | tf_op jit(solution)/shard_map/ppermute | solution.py:448
  89.5 22.7 %collective-permute-start.32 = (f32[32,768]{1,0:T(8,128)S(1)}, f32[32,768]{1,0:T(8,128)S(1)}, u32[]{:S(2)}, u32[]{:S(2)}) collective-permute-start(f32[32,768]{1,0:T(8,128)S(1)} %hop.22), channel_id=1, source_target_pairs={{160,208},{176,192},{161,209},{177,193},{162,210},{178,194},{163,2... | collective-permute-start | bytes 294920 | tf_op jit(solution)/shard_map/ppermute | solution.py:448
  91.2 22.7 %collective-permute-start.28 = (f32[32,768]{1,0:T(8,128)S(1)}, f32[32,768]{1,0:T(8,128)S(1)}, u32[]{:S(2)}, u32[]{:S(2)}) collective-permute-start(f32[32,768]{1,0:T(8,128)S(1)} %hop.18), channel_id=1, source_target_pairs={{160,208},{176,192},{161,209},{177,193},{162,210},{178,194},{163,2... | collective-permute-start | bytes 294920 | tf_op jit(solution)/shard_map/ppermute | solution.py:448
  112.6 3.7 %collective-permute-start.33 = (f32[32,768]{1,0:T(8,128)S(1)}, f32[32,768]{1,0:T(8,128)S(1)}, u32[]{:S(2)}, u32[]{:S(2)}) collective-permute-start(f32[32,768]{1,0:T(8,128)S(1)} %hop.23), channel_id=1, source_target_pairs={{192,240},{208,224},{193,241},{209,225},{194,242},{210,226},{195,2... | collective-permute-start | bytes 294920 | tf_op jit(solution)/shard_map/ppermute | solution.py:448
  114.2 4.1 %collective-permute-start.29 = (f32[32,768]{1,0:T(8,128)S(1)}, f32[32,768]{1,0:T(8,128)S(1)}, u32[]{:S(2)}, u32[]{:S(2)}) collective-permute-start(f32[32,768]{1,0:T(8,128)S(1)} %hop.19), channel_id=1, source_target_pairs={{192,240},{208,224},{193,241},{209,225},{194,242},{210,226},{195,2... | collective-permute-start | bytes 294920 | tf_op jit(solution)/shard_map/ppermute | solution.py:448
  119.7 3.9 %collective-permute-start.34 = (f32[64,512]{1,0:T(8,128)S(1)}, f32[64,512]{1,0:T(8,128)S(1)}, u32[]{:S(2)}, u32[]{:S(2)}) collective-permute-start(f32[64,512]{1,0:T(8,128)S(1)} %get-tuple-element.97), channel_id=1, source_target_pairs={{0,16},{16,0},{1,17},{17,1},{2,18},{18,2},{3,19},{19,3},{4,20},{20... | collective-permute-start | bytes 393224 | tf_op jit(solution)/shard_map/ppermute | solution.py:465
  120.4 6.9 %collective-permute-start.35 = (f32[64,512]{1,0:T(8,128)S(1)}, f32[64,512]{1,0:T(8,128)S(1)}, u32[]{:S(2)}, u32[]{:S(2)}) collective-permute-start(f32[64,512]{1,0:T(8,128)S(1)} %get-tuple-element.96), channel_id=1, source_target_pairs={{32,16},{64,48},{96,80},{128,112},{160,144},{192,176},{224,208},{3... | collective-permute-start | bytes 393224 | tf_op jit(solution)/shard_map/ppermute | solution.py:467
  121.7 6.4 %collective-permute-start.36 = (f32[64,512]{1,0:T(8,128)S(1)}, f32[64,512]{1,0:T(8,128)S(1)}, u32[]{:S(2)}, u32[]{:S(2)}) collective-permute-start(f32[64,512]{1,0:T(8,128)S(1)} %get-tuple-element.96), channel_id=1, source_target_pairs={{48,16},{80,48},{112,80},{144,112},{176,144},{208,176},{240,208},{... | collective-permute-start | bytes 393224 | tf_op jit(solution)/shard_map/ppermute | solution.py:467
where the time goes:
time: 129 us
  starting transfers between devices  50.2 us (39%)
  waiting for transfers between devices  44.3 us (34%)
  Pallas kernels  30.9 us (24%)
  local copies, waits for them, and re-layouts  1.89 us (1%)
    ppermute x14, starting transfers between devices, ring(): lax.ppermute(value, axis, [(k, (k + step) % count) for k in range(count)])  24 us
    ppermute x14, waiting for transfers between devices, onward(): lax.ppermute(value, ROW, [(2 * hop - 2 + side, 2 * hop + 1 - side) for si...  22.6 us
    pallas_call x2, Pallas kernels, prepare(): pl.pallas_call(functools.partial(prepare_body, outer_y), out_shape=(out,...  15 us
    ppermute x14, waiting for transfers between devices, ring(): lax.ppermute(value, axis, [(k, (k + step) % count) for k in range(count)])  13.8 us
    ppermute x14, starting transfers between devices, onward(): lax.ppermute(value, ROW, [(2 * hop - 2 + side, 2 * hop + 1 - side) for si...  11.8 us
    ppermute x3, starting transfers between devices, shifted(): lax.ppermute(value, ROW, [(k, k + step) for k in range(max(0, -step), min...  9.37 us
    pallas_call x1, Pallas kernels, operate(): pl.pallas_call(operate_body, out_shape=(jax.ShapeDtypeStruct((6, n, n), j...  4.47 us
    ppermute x2, waiting for transfers between devices, shards(): lax.ppermute(for_prior, ROW, [(2 * (k + 1) + side, 2 * k + 1) for k in ra...  4.45 us
  transfers between devices with their start and end apart: 37, of which 11 were waited for; matrix products, arithmetic and copies ran while one was open for 1% of the time, Pallas kernels for 19%

commit v1 on v0

--- a/solution.py
+++ b/solution.py
@@ -384,8 +384,6 @@
     is_first = position == 0
     is_last = position == count - 1
     is_odd = lax.axis_index("core") == 1
-    flipped = lax.axis_index(CHIP) % 2 == 1
-    takes_second = is_odd != flipped
     on_last = lax.axis_index(CHIP) == chips - 1
     at = [lax.axis_index("y"), lax.axis_index("zh")]
     one = jnp.int32(1)
@@ -394,8 +392,8 @@
     index_b = jnp.stack([*at, one, held]).astype(jnp.int32)
     ends = jnp.stack([is_first, is_last]).astype(jnp.int32)
     odd = is_odd.astype(jnp.int32).reshape(1)
-    local, is_last, is_odd, flipped, takes_second, on_last, index_a, index_b, ends, odd = lax.optimization_barrier(
-        (local, is_last, is_odd, flipped, takes_second, on_last, index_a, index_b, ends, odd)
+    local, is_last, is_odd, on_last, index_a, index_b, ends, odd = lax.optimization_barrier(
+        (local, is_last, is_odd, on_last, index_a, index_b, ends, odd)
     )
     n = eigenvectors.shape[0] // 2
     stay = jnp.stack([local[0, 1], local[1, 0], local[1, 1], local[2, 0]])
@@ -411,10 +409,11 @@
     after = ring(moved, "y", -1)
     far = ring(moved, "y", 2)
     near_b = jnp.concatenate([moved, after, far, before], axis=1)
-    near_a = after_these(near_a, (before, after, far))
     before_a = ring(near_a, "y", 1)
     after_a = ring(near_a, "y", -1)
-    give_a = (before_a[:, :half], after_a[:, half:])
+    give_a0 = before_a[:, :half]
+    give_a1 = after_a[:, half:]
+    give_a = give_a0, give_a1
     far0_a = ring(give_a[0], "y", 1)
     far1_a = ring(give_a[1], "y", -1)
     before_b = ring(near_b, "zh", 1)
@@ -433,8 +432,8 @@
     swap = [(0, 1), (1, 0)]
     half = add.shape[0] // 2
     halves = add.reshape(2, half, 7 * n)
-    keep = jnp.where(takes_second, halves[1], halves[0])
-    give = jnp.where(takes_second, halves[0], halves[1])
+    keep = jnp.where(is_odd, halves[1], halves[0])
+    give = jnp.where(is_odd, halves[0], halves[1])
     other = lax.ppermute(step, "core", swap)
     got = lax.ppermute(give, "core", swap)
     rest, other, got = lax.optimization_barrier((rest, other, got))
@@ -445,21 +444,18 @@
     adds = [chip_add[k * sub : (k + 1) * sub] for k in range(SUBS)]
 
     def onward(value, hop):
-        return lax.ppermute(value, ROW, [(2 * hop - 2 + side, 2 * hop + 1 - side) for side in range(2)])
+        return lax.ppermute(value, CHIP, [(hop - 1, hop)])
 
     arrived = [[onward(part, 1)] for part in adds]
     for hop in range(2, chips):
         for k in range(SUBS):
             sent = hop_on(arrived[k][-1], high, low, adds[k])
             arrived[k].append(onward(sent, hop))
-        if hop == 2:
-            rest = after_these(rest, [sent])
-            ended = ending(odd, step, other, rest, other_rest, keep, got)
-        if hop == 3:
-            *latest, high, low = lax.optimization_barrier((*[values[-1] for values in arrived], *ended, high, low))[:]
-            for k in range(SUBS):
-                arrived[k][-1] = latest[k]
-            ended = latest[SUBS:]
+        if hop == 4:
+            ended = ending(odd, step, other, after_these(rest, [sent]), other_rest, keep, got)
+        if hop == 5:
+            for values in arrived:
+                values[-1] = after_these(values[-1], ended)
     final = finish(arrived, *ended)
     for_prior, for_even, for_odd = [final[:, 2 * k * n : 2 * (k + 1) * n] for k in range(3)]
     got = lax.ppermute(jnp.where(is_odd, for_even, for_odd), "core", swap)
@@ -467,10 +463,8 @@
         lax.ppermute(for_prior, ROW, [(2 * (k + 1) + side, 2 * k + 1) for k in range(chips - 1)]) for side in range(2)
     ]
     got, *handed = lax.optimization_barrier((got, *handed))
-    one_half = jnp.where(is_odd, jnp.where(on_last, got, handed[1]), for_even)
-    other_half = jnp.where(is_odd, jnp.where(on_last, for_odd, handed[0]), got)
-    upper = jnp.where(flipped, other_half, one_half)
-    lower = jnp.where(flipped, one_half, other_half)
+    upper = jnp.where(is_odd, jnp.where(on_last, got, handed[0]), for_even)
+    lower = jnp.where(is_odd, jnp.where(on_last, for_odd, handed[1]), got)
     return jnp.concatenate([upper, lower], axis=0).T
 
 

time: 129 us -> 137 us (1.062)
  the two profiles are of different devices: /device:TPU:101 before, /device:TPU:45 now
where the time goes in v1:
time: 137 us; the launch traced here: 136 us
  starting transfers between devices  58.9 us (43%)
  waiting for transfers between devices  43 us (31%)
  Pallas kernels  30.9 us (23%)
  local copies, waits for them, and re-layouts  1.89 us (1%)
    ppermute x14, waiting for transfers between devices, ring(): lax.ppermute(value, axis, [(k, (k + step) % count) for k in range(count)])  19.5 us
    ppermute x14, starting transfers between devices, ring(): lax.ppermute(value, axis, [(k, (k + step) % count) for k in range(count)])  18.7 us
    ppermute x14, waiting for transfers between devices, onward(): return lax.ppermute(value, CHIP, [(hop - 1, hop)])  15.5 us
    pallas_call x2, Pallas kernels, prepare(): pl.pallas_call(functools.partial(prepare_body, outer_y), out_shape=(out,...  15 us
    ppermute x14, starting transfers between devices, onward(): return lax.ppermute(value, CHIP, [(hop - 1, hop)])  11.8 us
    ppermute x3, starting transfers between devices, shifted(): lax.ppermute(value, ROW, [(k, k + step) for k in range(max(0, -step), min...  10.6 us
    ppermute x1, starting transfers between devices, shards(): other = lax.ppermute(step, 'core', swap)  9.53 us
    ppermute x1, starting transfers between devices, shards(): got = lax.ppermute(jnp.where(is_odd, for_even, for_odd), 'core', swap)  4.53 us
  transfers between devices with their start and end apart: 37, of which 11 were waited for; matrix products, arithmetic and copies ran while one was open for 1% of the time, Pallas kernels for 18%

profile of v1, /device:TPU:45, one launch (start us, length us, event | category | flops | bytes accessed | tf_op | source)
XLA Modules:
  0.0 136.3 jit_solution(10781847643467081878)
XLA Ops:
  0.2 0.9 slice_bitcast_fusion.3
  1.1 3.1 %collective-permute-start.7 = (f32[4,16,512]{2,1,0:T(8,128)S(1)}, f32[4,16,512]{2,1,0:T(8,128)S(1)}, u32[]{:S(2)}, u32[]{:S(2)}) collective-permute-start(f32[4,16,512]{2,1,0:T(8,128)S(1)} %pad_maximum_fusion.2), channel_id=1, source_target_pairs={{0,1},{1,2},{2,3},{3,0},{4,5},{5,6},{6,7},{7,4},{8,9},{9,10},{10,1... | collective-permute-start | bytes 393224 | tf_op jit(solution)/shard_map/ppermute | solution.py:367
  4.2 2.2 %collective-permute-start.6 = (f32[4,16,512]{2,1,0:T(8,128)S(1)}, f32[4,16,512]{2,1,0:T(8,128)S(1)}, u32[]{:S(2)}, u32[]{:S(2)}) collective-permute-start(f32[4,16,512]{2,1,0:T(8,128)S(1)} %pad_maximum_fusion.2), channel_id=1, source_target_pairs={{0,3},{1,0},{2,1},{3,2},{4,7},{5,4},{6,5},{7,6},{8,11},{9,8},{10,9... | collective-permute-start | bytes 393224 | tf_op jit(solution)/shard_map/ppermute | solution.py:367
  6.4 6.2 %collective-permute-done.7 = f32[4,16,512]{2,1,0:T(8,128)S(1)} collective-permute-done((f32[4,16,512]{2,1,0:T(8,128)S(1)}, f32[4,16,512]{2,1,0:T(8,128)S(1)}, u32[]{:S(2)}, u32[]{:S(2)}) %collective-permute-start.7) | collective-permute-done | bytes 131104 | tf_op jit(solution)/shard_map/ppermute | solution.py:367
  12.9 2.7 %collective-permute-start = (f32[16,512]{1,0:T(8,128)S(1)}, f32[16,512]{1,0:T(8,128)S(1)}, u32[]{:S(2)}, u32[]{:S(2)}) collective-permute-start(f32[16,512]{1,0:T(8,128)S(1)} %get-tuple-element.87), channel_id=1, source_target_pairs={{16,0},{32,16},{48,32},{64,48},{80,64},{96,80},{112,96},{128,112},... | collective-permute-start | bytes 98312 | tf_op jit(solution)/shard_map/ppermute | solution.py:372
  15.5 2.9 %collective-permute-start.1 = (f32[16,512]{1,0:T(8,128)S(1)}, f32[16,512]{1,0:T(8,128)S(1)}, u32[]{:S(2)}, u32[]{:S(2)}) collective-permute-start(f32[16,512]{1,0:T(8,128)S(1)} %get-tuple-element.88), channel_id=1, source_target_pairs={{0,16},{16,32},{32,48},{48,64},{64,80},{80,96},{96,112},{112,128},... | collective-permute-start | bytes 98312 | tf_op jit(solution)/shard_map/ppermute | solution.py:372
  18.4 1.7 %collective-permute-done.8 = f32[4,16,512]{2,1,0:T(8,128)S(1)} collective-permute-done((f32[4,16,512]{2,1,0:T(8,128)S(1)}, f32[4,16,512]{2,1,0:T(8,128)S(1)}, u32[]{:S(2)}, u32[]{:S(2)}) %collective-permute-start.8) | collective-permute-done | bytes 131104 | tf_op jit(solution)/shard_map/ppermute | solution.py:367
  20.1 1.3 collective-permute-start.10
  21.7 0.8 select_bitcast_fusion
  22.5 1.6 %collective-permute-start.2 = (f32[2,16,512]{2,1,0:T(8,128)S(1)}, f32[2,16,512]{2,1,0:T(8,128)S(1)}, u32[]{:S(2)}, u32[]{:S(2)}) collective-permute-start(f32[2,16,512]{2,1,0:T(8,128)S(1)} %pad_maximum_fusion.3), channel_id=1, source_target_pairs={{0,12},{4,0},{8,4},{12,8},{1,13},{5,1},{9,5},{13,9},{2,14},{6,2},{... | collective-permute-start | bytes 196616 | tf_op jit(solution)/shard_map/ppermute | solution.py:367
  24.0 0.9 collective-permute-start.3
  25.0 1.6 %collective-permute-start.4 = (f32[2,16,512]{2,1,0:T(8,128)S(1)}, f32[2,16,512]{2,1,0:T(8,128)S(1)}, u32[]{:S(2)}, u32[]{:S(2)}) collective-permute-start(f32[2,16,512]{2,1,0:T(8,128)S(1)} %pad_maximum_fusion.3), channel_id=1, source_target_pairs={{0,4},{4,8},{8,12},{12,0},{1,5},{5,9},{9,13},{13,1},{2,6},{6,10},{... | collective-permute-start | bytes 196616 | tf_op jit(solution)/shard_map/ppermute | solution.py:367
  26.6 7.8 %collective-permute-done.2 = f32[2,16,512]{2,1,0:T(8,128)S(1)} collective-permute-done((f32[2,16,512]{2,1,0:T(8,128)S(1)}, f32[2,16,512]{2,1,0:T(8,128)S(1)}, u32[]{:S(2)}, u32[]{:S(2)}) %collective-permute-start.2) | collective-permute-done | bytes 65568 | tf_op jit(solution)/shard_map/ppermute | solution.py:367
  34.4 1.8 %collective-permute-done.3 = f32[2,16,512]{2,1,0:T(8,128)S(1)} collective-permute-done((f32[2,16,512]{2,1,0:T(8,128)S(1)}, f32[2,16,512]{2,1,0:T(8,128)S(1)}, u32[]{:S(2)}, u32[]{:S(2)}) %collective-permute-start.3) | collective-permute-done | bytes 65568 | tf_op jit(solution)/shard_map/ppermute | solution.py:367
  36.3 3.5 %collective-permute-start.13 = (f32[2,64,512]{2,1,0:T(8,128)S(1)}, f32[2,64,512]{2,1,0:T(8,128)S(1)}, u32[]{:S(2)}, u32[]{:S(2)}) collective-permute-start(f32[2,64,512]{2,1,0:T(8,128)S(1)} %pad_maximum_fusion.1.near_ref), channel_id=1, source_target_pairs={{0,3},{1,0},{2,1},{3,2},{4,7},{5,4},{6,5},{7,6},{8,11},{9,8},{10,9... | collective-permute-start | bytes 786440 | tf_op jit(solution)/shard_map/ppermute | solution.py:367
  39.9 1.5 %collective-permute-start.14 = (f32[4,32,512]{2,1,0:T(8,128)S(1)}, f32[4,32,512]{2,1,0:T(8,128)S(1)}, u32[]{:S(2)}, u32[]{:S(2)}) collective-permute-start(f32[4,32,512]{2,1,0:T(8,128)S(1)} %slice.87), channel_id=1, source_target_pairs={{0,12},{4,0},{8,4},{12,8},{1,13},{5,1},{9,5},{13,9},{2,14},{6,2},{... | collective-permute-start | bytes 786440 | tf_op jit(solution)/shard_map/ppermute | solution.py:367
  41.4 5.1 %collective-permute-start.5 = (f32[256,128]{1,0:T(8,128)S(1)}, f32[256,128]{1,0:T(8,128)S(1)}, u32[]{:S(2)}, u32[]{:S(2)}) collective-permute-start(f32[256,128]{1,0:T(8,128)S(1)} %slice.65), channel_id=1, source_target_pairs={{16,0},{32,16},{48,32},{64,48},{80,64},{96,80},{112,96},{128,112},... | collective-permute-start | bytes 393224 | tf_op jit(solution)/shard_map/ppermute | solution.py:372
  46.6 1.9 %collective-permute-done.12.before_ref = f32[2,64,512]{2,1,0:T(8,128)S(1)} collective-permute-done((f32[2,64,512]{2,1,0:T(8,128)S(1)}, f32[2,64,512]{2,1,0:T(8,128)S(1)}, u32[]{:S(2)}, u32[]{:S(2)}) %collective-permute-start.12) | collective-permute-done | bytes 262176 | tf_op jit(solution)/shard_map/ppermute | solution.py:367
  48.4 1.5 %collective-permute-start.16 = (f32[2,32,512]{2,1,0:T(8,128)S(1)}, f32[2,32,512]{2,1,0:T(8,128)S(1)}, u32[]{:S(2)}, u32[]{:S(2)}) collective-permute-start(f32[2,32,512]{2,1,0:T(8,128)S(1)} %slice.88), channel_id=1, source_target_pairs={{0,3},{1,0},{2,1},{3,2},{4,7},{5,4},{6,5},{7,6},{8,11},{9,8},{10,9... | collective-permute-start | bytes 393224 | tf_op jit(solution)/shard_map/ppermute | solution.py:367
  49.9 1.0 collective-permute-start.15
  50.9 9.1 %prepare.2 = (bf16[4,512,512]{2,1,0:T(8,128)(2,1)S(1)}, bf16[4,512,512]{2,1,0:T(8,128)(2,1)S(1)}) custom-call(s32[6]{0:T(128)S(1)} %stack.43.index_ref, f32[4,64,512]{2,1,0:T(8,128)S(1)} %pad_maximum_fusion.near_ref, f32[4,64,512]{2,1,0:T(8,128)S(1)} %collective-permute-done.9.after_ref, f32[4,64,512]{2,1,0:T(8,128)S(1)} %collective-permute-done.10.before_ref, ...), custom_call_target="tpu_custom_call" | custom-call | flops 2000000000 | bytes 1000000 | tf_op jit(solution)/shard_map/prepare/pallas_call | solution.py:117
  60.1 5.9 %prepare.3 = (bf16[2,512,512]{2,1,0:T(8,128)(2,1)S(1)}, bf16[2,512,512]{2,1,0:T(8,128)(2,1)S(1)}) custom-call(s32[4]{0:T(128)S(1)} %pad_add_fusion.index_ref, f32[2,64,512]{2,1,0:T(8,128)S(1)} %pad_maximum_fusion.1.near_ref, f32[2,64,512]{2,1,0:T(8,128)S(1)} %collective-permute-done.13.after_ref, f32[2,64,512]{2,1,0:T(8,128)S(1)} %collective-permute-done.12.before_ref, ...), custom_call_target="tpu_custom_call" | custom-call | flops 2000000000 | bytes 1000000 | tf_op jit(solution)/shard_map/prepare/pallas_call | solution.py:117
  66.0 4.5 %operate.1 = (f32[6,256,256]{2,1,0:T(8,128)S(1)}, f32[768,1024]{1,0:T(8,128)S(1)}, f32[128,1792]{1,0:T(8,128)S(1)}) custom-call(s32[2]{0:T(128)S(1)} %add_convert_fusion.ends_ref, f32[256,128]{1,0:T(8,128)S(1)} %collective-permute-done.5.data_ref, f32[512,128]{1,0:T(8,128)S(1)} %copy-done, bf16[4,512,512]{2,1,0:T(8,128)(2,1)S(1)} %get-tuple-element.51.ah, ...), custom_call_target="tpu_custom_call" | custom-call | tf_op jit(solution)/shard_map/operate/pallas_call | solution.py:212
  70.5 9.5 %collective-permute-start.17 = (f32[6,256,256]{2,1,0:T(8,128)S(1)}, f32[6,256,256]{2,1,0:T(8,128)S(1)}, u32[]{:S(2)}, u32[]{:S(2)}) collective-permute-start(f32[6,256,256]{2,1,0:T(8,128)S(1)} %get-tuple-element.57.mine_ref), channel_id=1, source_target_pairs={{0,16},{16,0},{1,17},{17,1},{2,18},{18,2},{3,19},{19,3},{4,20},{20... | collective-permute-start | bytes 4718600 | tf_op jit(solution)/shard_map/ppermute | solution.py:437
  80.2 3.5 %collective-permute-done.18.got_ref = f32[64,1792]{1,0:T(8,128)S(1)} collective-permute-done((f32[64,1792]{1,0:T(8,128)S(1)}, f32[64,1792]{1,0:T(8,128)S(1)}, u32[]{:S(2)}, u32[]{:S(2)}) %collective-permute-start.18) | collective-permute-done | bytes 458784 | tf_op jit(solution)/shard_map/ppermute | solution.py:438
  83.7 0.4 collective-permute-start.27
  84.1 1.7 %merge.1 = (bf16[6,256,256]{2,1,0:T(8,128)(2,1)S(1)}, bf16[6,256,256]{2,1,0:T(8,128)(2,1)S(1)}, f32[64,768]{1,0:T(8,128)S(1)}) custom-call(s32[1]{0:T(128)} %bitcast.6.odd_ref, f32[6,256,256]{2,1,0:T(8,128)S(1)} %get-tuple-element.57.mine_ref, f32[6,256,256]{2,1,0:T(8,128)S(1)} %collective-permute-done.17.other_ref, f32[64,768]{1,0:T(8,128)S(1)} %slice.89.keep_ref, ...), custom_call_target="tpu_custom_call" | custom-call | tf_op jit(solution)/shard_map/merge/pallas_call | solution.py:255
  85.8 0.7 collective-permute-start.24
  86.5 0.7 collective-permute-start.19
  87.2 0.4 hop.16
  87.5 0.7 collective-permute-start.25
  88.2 0.4 hop.12
  88.6 0.7 collective-permute-start.20
  89.3 0.4 hop.17
  89.6 0.7 collective-permute-start.26
  90.3 0.4 hop.13
  90.7 0.7 collective-permute-start.21
  91.4 0.4 hop.18
  91.7 0.7 collective-permute-start.30
  92.4 0.4 hop.14
  92.8 0.7 collective-permute-start.22
  93.4 0.4 hop.21
  93.8 0.7 collective-permute-start.31
  94.5 0.4 hop.15
  94.9 0.7 collective-permute-start.23
  95.5 4.1 %ending.1 = (bf16[768,1536]{1,0:T(8,128)(2,1)S(1)}, bf16[768,1536]{1,0:T(8,128)(2,1)S(1)}, f32[64,1536]{1,0:T(8,128)S(1)}) custom-call(s32[1]{0:T(128)} %bitcast.6.odd_ref, f32[6,256,256]{2,1,0:T(8,128)S(1)} %get-tuple-element.57.mine_ref, f32[6,256,256]{2,1,0:T(8,128)S(1)} %collective-permute-done.17.other_ref, f32[768,1024]{1,0:T(8,128)S(1)} %get-tuple-element.66.rest_ref, ...), custom_call_target="tpu_custom_call" | custom-call | tf_op jit(solution)/shard_map/ending/pallas_call | solution.py:327
  99.6 0.4 hop.22
  100.0 1.3 collective-permute-start.32
  101.3 0.4 hop.19
  101.7 1.3 collective-permute-start.28
  103.0 9.3 %collective-permute-done.32.state_ref.refs_12_ = f32[32,768]{1,0:T(8,128)S(1)} collective-permute-done((f32[32,768]{1,0:T(8,128)S(1)}, f32[32,768]{1,0:T(8,128)S(1)}, u32[]{:S(2)}, u32[]{:S(2)}) %collective-permute-start.32) | collective-permute-done | bytes 98336 | tf_op jit(solution)/shard_map/ppermute | solution.py:447
  112.3 0.4 hop.23
  112.6 1.3 collective-permute-start.33
  113.9 4.6 %collective-permute-done.28.state_ref.refs_5_ = f32[32,768]{1,0:T(8,128)S(1)} collective-permute-done((f32[32,768]{1,0:T(8,128)S(1)}, f32[32,768]{1,0:T(8,128)S(1)}, u32[]{:S(2)}, u32[]{:S(2)}) %collective-permute-start.28) | collective-permute-done | bytes 98336 | tf_op jit(solution)/shard_map/ppermute | solution.py:447
  118.5 0.4 hop.20
  118.8 1.3 collective-permute-start.29
  120.2 1.6 %collective-permute-done.29.refs_6_ = f32[32,768]{1,0:T(8,128)S(1)} collective-permute-done((f32[32,768]{1,0:T(8,128)S(1)}, f32[32,768]{1,0:T(8,128)S(1)}, u32[]{:S(2)}, u32[]{:S(2)}) %collective-permute-start.29) | collective-permute-done | bytes 98336 | tf_op jit(solution)/shard_map/ppermute | solution.py:447
  121.8 1.3 finish.1
  123.1 4.5 %collective-permute-start.34 = (f32[64,512]{1,0:T(8,128)S(1)}, f32[64,512]{1,0:T(8,128)S(1)}, u32[]{:S(2)}, u32[]{:S(2)}) collective-permute-start(f32[64,512]{1,0:T(8,128)S(1)} %get-tuple-element.80), channel_id=1, source_target_pairs={{0,16},{16,0},{1,17},{17,1},{2,18},{18,2},{3,19},{19,3},{4,20},{20... | collective-permute-start | bytes 393224 | tf_op jit(solution)/shard_map/ppermute | solution.py:461
  127.6 1.3 collective-permute-start.35
  128.9 1.9 %collective-permute-start.36 = (f32[64,512]{1,0:T(8,128)S(1)}, f32[64,512]{1,0:T(8,128)S(1)}, u32[]{:S(2)}, u32[]{:S(2)}) collective-permute-start(f32[64,512]{1,0:T(8,128)S(1)} %get-tuple-element.79), channel_id=1, source_target_pairs={{48,16},{80,48},{112,80},{144,112},{176,144},{208,176},{240,208},{... | collective-permute-start | bytes 393224 | tf_op jit(solution)/shard_map/ppermute | solution.py:463
  130.9 3.7 %collective-permute-done.35 = f32[64,512]{1,0:T(8,128)S(1)} collective-permute-done((f32[64,512]{1,0:T(8,128)S(1)}, f32[64,512]{1,0:T(8,128)S(1)}, u32[]{:S(2)}, u32[]{:S(2)}) %collective-permute-start.35) | collective-permute-done | bytes 131104 | tf_op jit(solution)/shard_map/ppermute | solution.py:463
  134.6 0.7 collective-permute-done.36
  135.4 0.8 copy.3
  (52 shorter events, 1.3 us)
Async XLA Ops:
  0.0 41.4 %copy-start = (f32[512,128]{1,0:T(8,128)S(1)}, f32[512,128]{1,0:T(8,128)}, u32[]{:S(2)}) copy-start(f32[512,128]{1,0:T(8,128)} %own_ref.1) | copy-start | bytes 786436
  1.1 11.5 %collective-permute-start.7 = (f32[4,16,512]{2,1,0:T(8,128)S(1)}, f32[4,16,512]{2,1,0:T(8,128)S(1)}, u32[]{:S(2)}, u32[]{:S(2)}) collective-permute-start(f32[4,16,512]{2,1,0:T(8,128)S(1)} %pad_maximum_fusion.2), channel_id=1, source_target_pairs={{0,1},{1,2},{2,3},{3,0},{4,5},{5,6},{6,7},{7,4},{8,9},{9,10},{10,1... | collective-permute-start | bytes 393224 | tf_op jit(solution)/shard_map/ppermute | solution.py:367
  4.2 14.2 %collective-permute-start.6 = (f32[4,16,512]{2,1,0:T(8,128)S(1)}, f32[4,16,512]{2,1,0:T(8,128)S(1)}, u32[]{:S(2)}, u32[]{:S(2)}) collective-permute-start(f32[4,16,512]{2,1,0:T(8,128)S(1)} %pad_maximum_fusion.2), channel_id=1, source_target_pairs={{0,3},{1,0},{2,1},{3,2},{4,7},{5,4},{6,5},{7,6},{8,11},{9,8},{10,9... | collective-permute-start | bytes 393224 | tf_op jit(solution)/shard_map/ppermute | solution.py:367
  12.6 7.5 %collective-permute-start.8 = (f32[4,16,512]{2,1,0:T(8,128)S(1)}, f32[4,16,512]{2,1,0:T(8,128)S(1)}, u32[]{:S(2)}, u32[]{:S(2)}) collective-permute-start(f32[4,16,512]{2,1,0:T(8,128)S(1)} %collective-permute-done.7), channel_id=1, source_target_pairs={{0,1},{1,2},{2,3},{3,0},{4,5},{5,6},{6,7},{7,4},{8,9},{9,10},{10,1... | collective-permute-start | bytes 393224 | tf_op jit(solution)/shard_map/ppermute | solution.py:367
  12.9 8.8 %collective-permute-start = (f32[16,512]{1,0:T(8,128)S(1)}, f32[16,512]{1,0:T(8,128)S(1)}, u32[]{:S(2)}, u32[]{:S(2)}) collective-permute-start(f32[16,512]{1,0:T(8,128)S(1)} %get-tuple-element.87), channel_id=1, source_target_pairs={{16,0},{32,16},{48,32},{64,48},{80,64},{96,80},{112,96},{128,112},... | collective-permute-start | bytes 98312 | tf_op jit(solution)/shard_map/ppermute | solution.py:372
  15.5 6.9 %collective-permute-start.1 = (f32[16,512]{1,0:T(8,128)S(1)}, f32[16,512]{1,0:T(8,128)S(1)}, u32[]{:S(2)}, u32[]{:S(2)}) collective-permute-start(f32[16,512]{1,0:T(8,128)S(1)} %get-tuple-element.88), channel_id=1, source_target_pairs={{0,16},{16,32},{32,48},{48,64},{64,80},{80,96},{96,112},{112,128},... | collective-permute-start | bytes 98312 | tf_op jit(solution)/shard_map/ppermute | solution.py:372
  20.1 19.6 %collective-permute-start.10 = (f32[4,64,512]{2,1,0:T(8,128)S(1)}, f32[4,64,512]{2,1,0:T(8,128)S(1)}, u32[]{:S(2)}, u32[]{:S(2)}) collective-permute-start(f32[4,64,512]{2,1,0:T(8,128)S(1)} %pad_maximum_fusion.near_ref), channel_id=1, source_target_pairs={{0,4},{4,8},{8,12},{12,0},{1,5},{5,9},{9,13},{13,1},{2,6},{6,10},{... | collective-permute-start | bytes 1572872 | tf_op jit(solution)/shard_map/ppermute | solution.py:367
  21.5 18.4 %collective-permute-start.9 = (f32[4,64,512]{2,1,0:T(8,128)S(1)}, f32[4,64,512]{2,1,0:T(8,128)S(1)}, u32[]{:S(2)}, u32[]{:S(2)}) collective-permute-start(f32[4,64,512]{2,1,0:T(8,128)S(1)} %pad_maximum_fusion.near_ref), channel_id=1, source_target_pairs={{0,12},{4,0},{8,4},{12,8},{1,13},{5,1},{9,5},{13,9},{2,14},{6,2},{... | collective-permute-start | bytes 1572872 | tf_op jit(solution)/shard_map/ppermute | solution.py:367
  22.5 12.0 %collective-permute-start.2 = (f32[2,16,512]{2,1,0:T(8,128)S(1)}, f32[2,16,512]{2,1,0:T(8,128)S(1)}, u32[]{:S(2)}, u32[]{:S(2)}) collective-permute-start(f32[2,16,512]{2,1,0:T(8,128)S(1)} %pad_maximum_fusion.3), channel_id=1, source_target_pairs={{0,12},{4,0},{8,4},{12,8},{1,13},{5,1},{9,5},{13,9},{2,14},{6,2},{... | collective-permute-start | bytes 196616 | tf_op jit(solution)/shard_map/ppermute | solution.py:367
  24.0 12.2 %collective-permute-start.3 = (f32[2,16,512]{2,1,0:T(8,128)S(1)}, f32[2,16,512]{2,1,0:T(8,128)S(1)}, u32[]{:S(2)}, u32[]{:S(2)}) collective-permute-start(f32[2,16,512]{2,1,0:T(8,128)S(1)} %pad_maximum_fusion.3), channel_id=1, source_target_pairs={{0,8},{4,12},{8,0},{12,4},{1,9},{5,13},{9,1},{13,5},{2,10},{6,14},... | collective-permute-start | bytes 196616 | tf_op jit(solution)/shard_map/ppermute | solution.py:367
  25.0 11.3 %collective-permute-start.4 = (f32[2,16,512]{2,1,0:T(8,128)S(1)}, f32[2,16,512]{2,1,0:T(8,128)S(1)}, u32[]{:S(2)}, u32[]{:S(2)}) collective-permute-start(f32[2,16,512]{2,1,0:T(8,128)S(1)} %pad_maximum_fusion.3), channel_id=1, source_target_pairs={{0,4},{4,8},{8,12},{12,0},{1,5},{5,9},{9,13},{13,1},{2,6},{6,10},{... | collective-permute-start | bytes 196616 | tf_op jit(solution)/shard_map/ppermute | solution.py:367
  36.3 10.2 %collective-permute-start.13 = (f32[2,64,512]{2,1,0:T(8,128)S(1)}, f32[2,64,512]{2,1,0:T(8,128)S(1)}, u32[]{:S(2)}, u32[]{:S(2)}) collective-permute-start(f32[2,64,512]{2,1,0:T(8,128)S(1)} %pad_maximum_fusion.1.near_ref), channel_id=1, source_target_pairs={{0,3},{1,0},{2,1},{3,2},{4,7},{5,4},{6,5},{7,6},{8,11},{9,8},{10,9... | collective-permute-start | bytes 786440 | tf_op jit(solution)/shard_map/ppermute | solution.py:367
  39.8 8.7 %collective-permute-start.12 = (f32[2,64,512]{2,1,0:T(8,128)S(1)}, f32[2,64,512]{2,1,0:T(8,128)S(1)}, u32[]{:S(2)}, u32[]{:S(2)}) collective-permute-start(f32[2,64,512]{2,1,0:T(8,128)S(1)} %pad_maximum_fusion.1.near_ref), channel_id=1, source_target_pairs={{0,1},{1,2},{2,3},{3,0},{4,5},{5,6},{6,7},{7,4},{8,9},{9,10},{10,1... | collective-permute-start | bytes 786440 | tf_op jit(solution)/shard_map/ppermute | solution.py:367
  39.8 11.1 %collective-permute-start.11 = (f32[4,32,512]{2,1,0:T(8,128)S(1)}, f32[4,32,512]{2,1,0:T(8,128)S(1)}, u32[]{:S(2)}, u32[]{:S(2)}) collective-permute-start(f32[4,32,512]{2,1,0:T(8,128)S(1)} %slice.85), channel_id=1, source_target_pairs={{0,4},{4,8},{8,12},{12,0},{1,5},{5,9},{9,13},{13,1},{2,6},{6,10},{... | collective-permute-start | bytes 786440 | tf_op jit(solution)/shard_map/ppermute | solution.py:367
  39.9 11.0 %collective-permute-start.14 = (f32[4,32,512]{2,1,0:T(8,128)S(1)}, f32[4,32,512]{2,1,0:T(8,128)S(1)}, u32[]{:S(2)}, u32[]{:S(2)}) collective-permute-start(f32[4,32,512]{2,1,0:T(8,128)S(1)} %slice.87), channel_id=1, source_target_pairs={{0,12},{4,0},{8,4},{12,8},{1,13},{5,1},{9,5},{13,9},{2,14},{6,2},{... | collective-permute-start | bytes 786440 | tf_op jit(solution)/shard_map/ppermute | solution.py:367
  41.4 24.5 %collective-permute-start.5 = (f32[256,128]{1,0:T(8,128)S(1)}, f32[256,128]{1,0:T(8,128)S(1)}, u32[]{:S(2)}, u32[]{:S(2)}) collective-permute-start(f32[256,128]{1,0:T(8,128)S(1)} %slice.65), channel_id=1, source_target_pairs={{16,0},{32,16},{48,32},{64,48},{80,64},{96,80},{112,96},{128,112},... | collective-permute-start | bytes 393224 | tf_op jit(solution)/shard_map/ppermute | solution.py:372
  48.4 11.6 %collective-permute-start.16 = (f32[2,32,512]{2,1,0:T(8,128)S(1)}, f32[2,32,512]{2,1,0:T(8,128)S(1)}, u32[]{:S(2)}, u32[]{:S(2)}) collective-permute-start(f32[2,32,512]{2,1,0:T(8,128)S(1)} %slice.88), channel_id=1, source_target_pairs={{0,3},{1,0},{2,1},{3,2},{4,7},{5,4},{6,5},{7,6},{8,11},{9,8},{10,9... | collective-permute-start | bytes 393224 | tf_op jit(solution)/shard_map/ppermute | solution.py:367
  49.9 10.2 %collective-permute-start.15 = (f32[2,32,512]{2,1,0:T(8,128)S(1)}, f32[2,32,512]{2,1,0:T(8,128)S(1)}, u32[]{:S(2)}, u32[]{:S(2)}) collective-permute-start(f32[2,32,512]{2,1,0:T(8,128)S(1)} %slice.86), channel_id=1, source_target_pairs={{0,1},{1,2},{2,3},{3,0},{4,5},{5,6},{6,7},{7,4},{8,9},{9,10},{10,1... | collective-permute-start | bytes 393224 | tf_op jit(solution)/shard_map/ppermute | solution.py:367
  70.5 13.2 %collective-permute-start.17 = (f32[6,256,256]{2,1,0:T(8,128)S(1)}, f32[6,256,256]{2,1,0:T(8,128)S(1)}, u32[]{:S(2)}, u32[]{:S(2)}) collective-permute-start(f32[6,256,256]{2,1,0:T(8,128)S(1)} %get-tuple-element.57.mine_ref), channel_id=1, source_target_pairs={{0,16},{16,0},{1,17},{17,1},{2,18},{18,2},{3,19},{19,3},{4,20},{20... | collective-permute-start | bytes 4718600 | tf_op jit(solution)/shard_map/ppermute | solution.py:437
  80.0 3.6 %collective-permute-start.18 = (f32[64,1792]{1,0:T(8,128)S(1)}, f32[64,1792]{1,0:T(8,128)S(1)}, u32[]{:S(2)}, u32[]{:S(2)}) collective-permute-start(f32[64,1792]{1,0:T(8,128)S(1)} %get-tuple-element.76), channel_id=1, source_target_pairs={{0,16},{16,0},{1,17},{17,1},{2,18},{18,2},{3,19},{19,3},{4,20},{20... | collective-permute-start | bytes 1376264 | tf_op jit(solution)/shard_map/ppermute | solution.py:438
  83.7 11.8 %collective-permute-start.27 = (f32[768,1024]{1,0:T(8,128)S(1)}, f32[768,1024]{1,0:T(8,128)S(1)}, u32[]{:S(2)}, u32[]{:S(2)}) collective-permute-start(f32[768,1024]{1,0:T(8,128)S(1)} %get-tuple-element.66.rest_ref), channel_id=1, source_target_pairs={{0,16},{16,0},{1,17},{17,1},{2,18},{18,2},{3,19},{19,3},{4,20},{20... | collective-permute-start | bytes 9437192 | tf_op jit(solution)/shard_map/ppermute | solution.py:441
  85.8 1.4 collective-permute-start.24
  86.5 1.7 %collective-permute-start.19 = (f32[32,768]{1,0:T(8,128)S(1)}, f32[32,768]{1,0:T(8,128)S(1)}, u32[]{:S(2)}, u32[]{:S(2)}) collective-permute-start(f32[32,768]{1,0:T(8,128)S(1)} %get-tuple-element.82.add_ref), channel_id=1, source_target_pairs={{0,32},{1,33},{2,34},{3,35},{4,36},{5,37},{6,38},{7,39},{8,40},{9,... | collective-permute-start | bytes 294920 | tf_op jit(solution)/shard_map/ppermute | solution.py:447
  87.5 1.7 %collective-permute-start.25 = (f32[32,768]{1,0:T(8,128)S(1)}, f32[32,768]{1,0:T(8,128)S(1)}, u32[]{:S(2)}, u32[]{:S(2)}) collective-permute-start(f32[32,768]{1,0:T(8,128)S(1)} %hop.16), channel_id=1, source_target_pairs={{32,64},{33,65},{34,66},{35,67},{36,68},{37,69},{38,70},{39,71},{4... | collective-permute-start | bytes 294920 | tf_op jit(solution)/shard_map/ppermute | solution.py:447
  88.6 1.7 %collective-permute-start.20 = (f32[32,768]{1,0:T(8,128)S(1)}, f32[32,768]{1,0:T(8,128)S(1)}, u32[]{:S(2)}, u32[]{:S(2)}) collective-permute-start(f32[32,768]{1,0:T(8,128)S(1)} %hop.12), channel_id=1, source_target_pairs={{32,64},{33,65},{34,66},{35,67},{36,68},{37,69},{38,70},{39,71},{4... | collective-permute-start | bytes 294920 | tf_op jit(solution)/shard_map/ppermute | solution.py:447
  89.6 1.7 %collective-permute-start.26 = (f32[32,768]{1,0:T(8,128)S(1)}, f32[32,768]{1,0:T(8,128)S(1)}, u32[]{:S(2)}, u32[]{:S(2)}) collective-permute-start(f32[32,768]{1,0:T(8,128)S(1)} %hop.17), channel_id=1, source_target_pairs={{64,96},{65,97},{66,98},{67,99},{68,100},{69,101},{70,102},{71,103... | collective-permute-start | bytes 294920 | tf_op jit(solution)/shard_map/ppermute | solution.py:447
  90.7 1.7 %collective-permute-start.21 = (f32[32,768]{1,0:T(8,128)S(1)}, f32[32,768]{1,0:T(8,128)S(1)}, u32[]{:S(2)}, u32[]{:S(2)}) collective-permute-start(f32[32,768]{1,0:T(8,128)S(1)} %hop.13), channel_id=1, source_target_pairs={{64,96},{65,97},{66,98},{67,99},{68,100},{69,101},{70,102},{71,103... | collective-permute-start | bytes 294920 | tf_op jit(solution)/shard_map/ppermute | solution.py:447
  91.7 1.7 %collective-permute-start.30 = (f32[32,768]{1,0:T(8,128)S(1)}, f32[32,768]{1,0:T(8,128)S(1)}, u32[]{:S(2)}, u32[]{:S(2)}) collective-permute-start(f32[32,768]{1,0:T(8,128)S(1)} %hop.18), channel_id=1, source_target_pairs={{96,128},{97,129},{98,130},{99,131},{100,132},{101,133},{102,134},... | collective-permute-start | bytes 294920 | tf_op jit(solution)/shard_map/ppermute | solution.py:447
  92.8 1.7 %collective-permute-start.22 = (f32[32,768]{1,0:T(8,128)S(1)}, f32[32,768]{1,0:T(8,128)S(1)}, u32[]{:S(2)}, u32[]{:S(2)}) collective-permute-start(f32[32,768]{1,0:T(8,128)S(1)} %hop.14), channel_id=1, source_target_pairs={{96,128},{97,129},{98,130},{99,131},{100,132},{101,133},{102,134},... | collective-permute-start | bytes 294920 | tf_op jit(solution)/shard_map/ppermute | solution.py:447
  93.8 5.8 %collective-permute-start.31 = (f32[32,768]{1,0:T(8,128)S(1)}, f32[32,768]{1,0:T(8,128)S(1)}, u32[]{:S(2)}, u32[]{:S(2)}) collective-permute-start(f32[32,768]{1,0:T(8,128)S(1)} %hop.21), channel_id=1, source_target_pairs={{128,160},{129,161},{130,162},{131,163},{132,164},{133,165},{134,1... | collective-permute-start | bytes 294920 | tf_op jit(solution)/shard_map/ppermute | solution.py:447
  94.9 6.4 %collective-permute-start.23 = (f32[32,768]{1,0:T(8,128)S(1)}, f32[32,768]{1,0:T(8,128)S(1)}, u32[]{:S(2)}, u32[]{:S(2)}) collective-permute-start(f32[32,768]{1,0:T(8,128)S(1)} %hop.15), channel_id=1, source_target_pairs={{128,160},{129,161},{130,162},{131,163},{132,164},{133,165},{134,1... | collective-permute-start | bytes 294920 | tf_op jit(solution)/shard_map/ppermute | solution.py:447
  100.0 12.3 %collective-permute-start.32 = (f32[32,768]{1,0:T(8,128)S(1)}, f32[32,768]{1,0:T(8,128)S(1)}, u32[]{:S(2)}, u32[]{:S(2)}) collective-permute-start(f32[32,768]{1,0:T(8,128)S(1)} %hop.22), channel_id=1, source_target_pairs={{160,192},{161,193},{162,194},{163,195},{164,196},{165,197},{166,1... | collective-permute-start | bytes 294920 | tf_op jit(solution)/shard_map/ppermute | solution.py:447
  101.7 16.8 %collective-permute-start.28 = (f32[32,768]{1,0:T(8,128)S(1)}, f32[32,768]{1,0:T(8,128)S(1)}, u32[]{:S(2)}, u32[]{:S(2)}) collective-permute-start(f32[32,768]{1,0:T(8,128)S(1)} %hop.19), channel_id=1, source_target_pairs={{160,192},{161,193},{162,194},{163,195},{164,196},{165,197},{166,1... | collective-permute-start | bytes 294920 | tf_op jit(solution)/shard_map/ppermute | solution.py:447
  112.6 7.5 %collective-permute-start.33 = (f32[32,768]{1,0:T(8,128)S(1)}, f32[32,768]{1,0:T(8,128)S(1)}, u32[]{:S(2)}, u32[]{:S(2)}) collective-permute-start(f32[32,768]{1,0:T(8,128)S(1)} %hop.23), channel_id=1, source_target_pairs={{192,224},{193,225},{194,226},{195,227},{196,228},{197,229},{198,2... | collective-permute-start | bytes 294920 | tf_op jit(solution)/shard_map/ppermute | solution.py:447
  118.8 2.9 %collective-permute-start.29 = (f32[32,768]{1,0:T(8,128)S(1)}, f32[32,768]{1,0:T(8,128)S(1)}, u32[]{:S(2)}, u32[]{:S(2)}) collective-permute-start(f32[32,768]{1,0:T(8,128)S(1)} %hop.20), channel_id=1, source_target_pairs={{192,224},{193,225},{194,226},{195,227},{196,228},{197,229},{198,2... | collective-permute-start | bytes 294920 | tf_op jit(solution)/shard_map/ppermute | solution.py:447
  123.1 7.7 %collective-permute-start.34 = (f32[64,512]{1,0:T(8,128)S(1)}, f32[64,512]{1,0:T(8,128)S(1)}, u32[]{:S(2)}, u32[]{:S(2)}) collective-permute-start(f32[64,512]{1,0:T(8,128)S(1)} %get-tuple-element.80), channel_id=1, source_target_pairs={{0,16},{16,0},{1,17},{17,1},{2,18},{18,2},{3,19},{19,3},{4,20},{20... | collective-permute-start | bytes 393224 | tf_op jit(solution)/shard_map/ppermute | solution.py:461
  127.6 6.9 %collective-permute-start.35 = (f32[64,512]{1,0:T(8,128)S(1)}, f32[64,512]{1,0:T(8,128)S(1)}, u32[]{:S(2)}, u32[]{:S(2)}) collective-permute-start(f32[64,512]{1,0:T(8,128)S(1)} %get-tuple-element.79), channel_id=1, source_target_pairs={{32,16},{64,48},{96,80},{128,112},{160,144},{192,176},{224,208},{3... | collective-permute-start | bytes 393224 | tf_op jit(solution)/shard_map/ppermute | solution.py:463
  128.9 6.4 %collective-permute-start.36 = (f32[64,512]{1,0:T(8,128)S(1)}, f32[64,512]{1,0:T(8,128)S(1)}, u32[]{:S(2)}, u32[]{:S(2)}) collective-permute-start(f32[64,512]{1,0:T(8,128)S(1)} %get-tuple-element.79), channel_id=1, source_target_pairs={{48,16},{80,48},{112,80},{144,112},{176,144},{208,176},{240,208},{... | collective-permute-start | bytes 393224 | tf_op jit(solution)/shard_map/ppermute | solution.py:463

commit v2 on v1

--- a/solution.py
+++ b/solution.py
@@ -336,16 +336,18 @@
 
 
 def finish_body(*refs):
-    *state_refs, high_ref, low_ref, add_ref, out_ref = refs
+    *state_refs, high_ref, low_ref, add_ref, out_ref, sum_ref = refs
     hops = len(state_refs) // SUBS
+    width = out_ref.shape[1]
     rows = []
     for k in range(SUBS):
         total = state_refs[k * hops][...]
         for ref in state_refs[k * hops + 1 : (k + 1) * hops]:
             total = total + ref[...]
         rows.append(total)
-    state = split(jnp.concatenate(rows, axis=0))
-    out_ref[...] = dot3(state, (high_ref[...], low_ref[...])) + add_ref[...]
+    state = jnp.concatenate(rows, axis=0)
+    sum_ref[...] = state
+    out_ref[...] = dot3(split(state), (high_ref[:, :width], low_ref[:, :width])) + add_ref[:, :width]
 
 
 def finish(arrived, high, low, add):
@@ -353,13 +355,38 @@
     states = [value for values in arrived for value in values]
     return pl.pallas_call(
         finish_body,
-        out_shape=jax.ShapeDtypeStruct(add.shape, jnp.float32),
+        out_shape=(
+            jax.ShapeDtypeStruct((add.shape[0], add.shape[1] // 3), jnp.float32),
+            jax.ShapeDtypeStruct((add.shape[0], high.shape[0]), jnp.float32),
+        ),
         in_specs=[vmem] * (len(states) + 3),
-        out_specs=vmem,
+        out_specs=(vmem, vmem),
         compiler_params=pltpu.CompilerParams(vmem_limit_bytes=16 * 1024 * 1024),
         interpret=INTERPRET,
         name="finish",
     )(*states, high, low, add)
+
+
+def finish_own_body(state_ref, high_ref, low_ref, add_ref, even_ref, odd_ref):
+    width = even_ref.shape[1]
+    state = split(state_ref[...])
+    for k, ref in ((1, even_ref), (2, odd_ref)):
+        at = slice(k * width, (k + 1) * width)
+        ref[...] = dot3(state, (high_ref[:, at], low_ref[:, at])) + add_ref[:, at]
+
+
+def finish_own(state, high, low, add):
+    vmem = pl.BlockSpec(memory_space=pltpu.VMEM)
+    out = jax.ShapeDtypeStruct((add.shape[0], add.shape[1] // 3), jnp.float32)
+    return pl.pallas_call(
+        finish_own_body,
+        out_shape=(out, out),
+        in_specs=[vmem] * 4,
+        out_specs=(vmem, vmem),
+        compiler_params=pltpu.CompilerParams(vmem_limit_bytes=16 * 1024 * 1024),
+        interpret=INTERPRET,
+        name="finish_own",
+    )(state, high, low, add)
 
 
 def ring(value, axis, step):
@@ -384,6 +411,10 @@
     is_first = position == 0
     is_last = position == count - 1
     is_odd = lax.axis_index("core") == 1
+    middle = chips // 2
+    flipped = lax.axis_index(CHIP) >= middle
+    flips_next = lax.axis_index(CHIP) + 1 >= middle
+    takes_second = is_odd != flipped
     on_last = lax.axis_index(CHIP) == chips - 1
     at = [lax.axis_index("y"), lax.axis_index("zh")]
     one = jnp.int32(1)
@@ -392,8 +423,8 @@
     index_b = jnp.stack([*at, one, held]).astype(jnp.int32)
     ends = jnp.stack([is_first, is_last]).astype(jnp.int32)
     odd = is_odd.astype(jnp.int32).reshape(1)
-    local, is_last, is_odd, on_last, index_a, index_b, ends, odd = lax.optimization_barrier(
-        (local, is_last, is_odd, on_last, index_a, index_b, ends, odd)
+    local, is_last, is_odd, flipped, flips_next, takes_second, on_last, index_a, index_b, ends, odd = lax.optimization_barrier(
+        (local, is_last, is_odd, flipped, flips_next, takes_second, on_last, index_a, index_b, ends, odd)
     )
     n = eigenvectors.shape[0] // 2
     stay = jnp.stack([local[0, 1], local[1, 0], local[1, 1], local[2, 0]])
@@ -432,8 +463,8 @@
     swap = [(0, 1), (1, 0)]
     half = add.shape[0] // 2
     halves = add.reshape(2, half, 7 * n)
-    keep = jnp.where(is_odd, halves[1], halves[0])
-    give = jnp.where(is_odd, halves[0], halves[1])
+    keep = jnp.where(takes_second, halves[1], halves[0])
+    give = jnp.where(takes_second, halves[0], halves[1])
     other = lax.ppermute(step, "core", swap)
     got = lax.ppermute(give, "core", swap)
     rest, other, got = lax.optimization_barrier((rest, other, got))
@@ -444,7 +475,8 @@
     adds = [chip_add[k * sub : (k + 1) * sub] for k in range(SUBS)]
 
     def onward(value, hop):
-        return lax.ppermute(value, CHIP, [(hop - 1, hop)])
+        turn = 1 if hop == middle else 0
+        return lax.ppermute(value, ROW, [(2 * hop - 2 + side, 2 * hop + (side ^ turn)) for side in range(2)])
 
     arrived = [[onward(part, 1)] for part in adds]
     for hop in range(2, chips):
@@ -456,15 +488,17 @@
         if hop == 5:
             for values in arrived:
                 values[-1] = after_these(values[-1], ended)
-    final = finish(arrived, *ended)
-    for_prior, for_even, for_odd = [final[:, 2 * k * n : 2 * (k + 1) * n] for k in range(3)]
+    for_prior, state = finish(arrived, *ended)
+    handed = []
+    for side in range(2):
+        pairs = [(2 * (k + 1) + side, 2 * k + 1) for k in range(chips - 1)]
+        handed.append(lax.ppermute(for_prior, ROW, pairs))
+    for_even, for_odd = finish_own(state, *ended)
     got = lax.ppermute(jnp.where(is_odd, for_even, for_odd), "core", swap)
-    handed = [
-        lax.ppermute(for_prior, ROW, [(2 * (k + 1) + side, 2 * k + 1) for k in range(chips - 1)]) for side in range(2)
-    ]
     got, *handed = lax.optimization_barrier((got, *handed))
-    upper = jnp.where(is_odd, jnp.where(on_last, got, handed[0]), for_even)
-    lower = jnp.where(is_odd, jnp.where(on_last, for_odd, handed[1]), got)
+    near, far = jnp.where(flips_next, handed[1], handed[0]), jnp.where(flips_next, handed[0], handed[1])
+    upper = jnp.where(is_odd, jnp.where(on_last, for_odd, near), jnp.where(flipped, got, for_even))
+    lower = jnp.where(is_odd, jnp.where(on_last, got, far), jnp.where(flipped, for_even, got))
     return jnp.concatenate([upper, lower], axis=0).T
 
 

time: 137 us -> 137 us (level)
  starting transfers between devices: 58.9 us -> 55.4 us
  waiting for transfers between devices: 43 us -> 46.5 us
    ppermute x16, waiting for transfers between devices: 19.9 us -> 23.5 us  [the longest x14 19.1 us: onward(): lax.ppermute(value, ROW, [(2 * hop - 2 + side, 2 * hop + (side ^ turn)) f...]
    ppermute x1, starting transfers between devices: 4.53 us -> 1.06 us  [shards(): got = lax.ppermute(jnp.where(is_odd, for_even, for_odd), 'core', swap)]
where the time goes in v2:
time: 137 us
  starting transfers between devices  55.4 us (40%)
  waiting for transfers between devices  46.5 us (34%)
  Pallas kernels  31.1 us (23%)
  local copies, waits for them, and re-layouts  1.89 us (1%)
    ppermute x14, waiting for transfers between devices, ring(): lax.ppermute(value, axis, [(k, (k + step) % count) for k in range(count)])  19.5 us
    ppermute x14, waiting for transfers between devices, onward(): lax.ppermute(value, ROW, [(2 * hop - 2 + side, 2 * hop + (side ^ turn)) f...  19.1 us
    ppermute x14, starting transfers between devices, ring(): lax.ppermute(value, axis, [(k, (k + step) % count) for k in range(count)])  18.7 us
    pallas_call x2, Pallas kernels, prepare(): pl.pallas_call(functools.partial(prepare_body, outer_y), out_shape=(out,...  15 us
    ppermute x14, starting transfers between devices, onward(): lax.ppermute(value, ROW, [(2 * hop - 2 + side, 2 * hop + (side ^ turn)) f...  11.8 us
    ppermute x3, starting transfers between devices, shifted(): lax.ppermute(value, ROW, [(k, k + step) for k in range(max(0, -step), min...  10.6 us
    ppermute x1, starting transfers between devices, shards(): other = lax.ppermute(step, 'core', swap)  9.53 us
    pallas_call x1, Pallas kernels, operate(): pl.pallas_call(operate_body, out_shape=(jax.ShapeDtypeStruct((6, n, n), j...  4.47 us
  transfers between devices with their start and end apart: 37, of which 11 were waited for; matrix products, arithmetic and copies ran while one was open for 1% of the time, Pallas kernels for 18%

profile of v2, /device:TPU:45, one launch (start us, length us, event | category | flops | bytes accessed | tf_op | source)
XLA Modules:
  0.0 136.5 jit_solution(1219929763028043257)
XLA Ops:
  0.2 0.9 slice_bitcast_fusion.3
  1.1 3.1 %collective-permute-start.7 = (f32[4,16,512]{2,1,0:T(8,128)S(1)}, f32[4,16,512]{2,1,0:T(8,128)S(1)}, u32[]{:S(2)}, u32[]{:S(2)}) collective-permute-start(f32[4,16,512]{2,1,0:T(8,128)S(1)} %pad_maximum_fusion.2), channel_id=1, source_target_pairs={{0,1},{1,2},{2,3},{3,0},{4,5},{5,6},{6,7},{7,4},{8,9},{9,10},{10,1... | collective-permute-start | bytes 393224 | tf_op jit(solution)/shard_map/ppermute | solution.py:394
  4.2 2.2 %collective-permute-start.6 = (f32[4,16,512]{2,1,0:T(8,128)S(1)}, f32[4,16,512]{2,1,0:T(8,128)S(1)}, u32[]{:S(2)}, u32[]{:S(2)}) collective-permute-start(f32[4,16,512]{2,1,0:T(8,128)S(1)} %pad_maximum_fusion.2), channel_id=1, source_target_pairs={{0,3},{1,0},{2,1},{3,2},{4,7},{5,4},{6,5},{7,6},{8,11},{9,8},{10,9... | collective-permute-start | bytes 393224 | tf_op jit(solution)/shard_map/ppermute | solution.py:394
  6.4 6.2 %collective-permute-done.7 = f32[4,16,512]{2,1,0:T(8,128)S(1)} collective-permute-done((f32[4,16,512]{2,1,0:T(8,128)S(1)}, f32[4,16,512]{2,1,0:T(8,128)S(1)}, u32[]{:S(2)}, u32[]{:S(2)}) %collective-permute-start.7) | collective-permute-done | bytes 131104 | tf_op jit(solution)/shard_map/ppermute | solution.py:394
  12.9 2.7 %collective-permute-start = (f32[16,512]{1,0:T(8,128)S(1)}, f32[16,512]{1,0:T(8,128)S(1)}, u32[]{:S(2)}, u32[]{:S(2)}) collective-permute-start(f32[16,512]{1,0:T(8,128)S(1)} %get-tuple-element.99), channel_id=1, source_target_pairs={{16,0},{32,16},{48,32},{64,48},{80,64},{96,80},{112,96},{128,112},... | collective-permute-start | bytes 98312 | tf_op jit(solution)/shard_map/ppermute | solution.py:399
  15.5 2.9 %collective-permute-start.1 = (f32[16,512]{1,0:T(8,128)S(1)}, f32[16,512]{1,0:T(8,128)S(1)}, u32[]{:S(2)}, u32[]{:S(2)}) collective-permute-start(f32[16,512]{1,0:T(8,128)S(1)} %get-tuple-element.100), channel_id=1, source_target_pairs={{0,16},{16,32},{32,48},{48,64},{64,80},{80,96},{96,112},{112,128},... | collective-permute-start | bytes 98312 | tf_op jit(solution)/shard_map/ppermute | solution.py:399
  18.4 1.7 %collective-permute-done.8 = f32[4,16,512]{2,1,0:T(8,128)S(1)} collective-permute-done((f32[4,16,512]{2,1,0:T(8,128)S(1)}, f32[4,16,512]{2,1,0:T(8,128)S(1)}, u32[]{:S(2)}, u32[]{:S(2)}) %collective-permute-start.8) | collective-permute-done | bytes 131104 | tf_op jit(solution)/shard_map/ppermute | solution.py:394
  20.1 1.3 collective-permute-start.10
  21.7 0.8 select_bitcast_fusion
  22.5 1.6 %collective-permute-start.2 = (f32[2,16,512]{2,1,0:T(8,128)S(1)}, f32[2,16,512]{2,1,0:T(8,128)S(1)}, u32[]{:S(2)}, u32[]{:S(2)}) collective-permute-start(f32[2,16,512]{2,1,0:T(8,128)S(1)} %pad_maximum_fusion.3), channel_id=1, source_target_pairs={{0,12},{4,0},{8,4},{12,8},{1,13},{5,1},{9,5},{13,9},{2,14},{6,2},{... | collective-permute-start | bytes 196616 | tf_op jit(solution)/shard_map/ppermute | solution.py:394
  24.0 0.9 collective-permute-start.3
  25.0 1.6 %collective-permute-start.4 = (f32[2,16,512]{2,1,0:T(8,128)S(1)}, f32[2,16,512]{2,1,0:T(8,128)S(1)}, u32[]{:S(2)}, u32[]{:S(2)}) collective-permute-start(f32[2,16,512]{2,1,0:T(8,128)S(1)} %pad_maximum_fusion.3), channel_id=1, source_target_pairs={{0,4},{4,8},{8,12},{12,0},{1,5},{5,9},{9,13},{13,1},{2,6},{6,10},{... | collective-permute-start | bytes 196616 | tf_op jit(solution)/shard_map/ppermute | solution.py:394
  26.6 7.8 %collective-permute-done.2 = f32[2,16,512]{2,1,0:T(8,128)S(1)} collective-permute-done((f32[2,16,512]{2,1,0:T(8,128)S(1)}, f32[2,16,512]{2,1,0:T(8,128)S(1)}, u32[]{:S(2)}, u32[]{:S(2)}) %collective-permute-start.2) | collective-permute-done | bytes 65568 | tf_op jit(solution)/shard_map/ppermute | solution.py:394
  34.4 1.8 %collective-permute-done.3 = f32[2,16,512]{2,1,0:T(8,128)S(1)} collective-permute-done((f32[2,16,512]{2,1,0:T(8,128)S(1)}, f32[2,16,512]{2,1,0:T(8,128)S(1)}, u32[]{:S(2)}, u32[]{:S(2)}) %collective-permute-start.3) | collective-permute-done | bytes 65568 | tf_op jit(solution)/shard_map/ppermute | solution.py:394
  36.3 3.5 %collective-permute-start.13 = (f32[2,64,512]{2,1,0:T(8,128)S(1)}, f32[2,64,512]{2,1,0:T(8,128)S(1)}, u32[]{:S(2)}, u32[]{:S(2)}) collective-permute-start(f32[2,64,512]{2,1,0:T(8,128)S(1)} %pad_maximum_fusion.1.near_ref), channel_id=1, source_target_pairs={{0,3},{1,0},{2,1},{3,2},{4,7},{5,4},{6,5},{7,6},{8,11},{9,8},{10,9... | collective-permute-start | bytes 786440 | tf_op jit(solution)/shard_map/ppermute | solution.py:394
  39.9 1.5 %collective-permute-start.14 = (f32[4,32,512]{2,1,0:T(8,128)S(1)}, f32[4,32,512]{2,1,0:T(8,128)S(1)}, u32[]{:S(2)}, u32[]{:S(2)}) collective-permute-start(f32[4,32,512]{2,1,0:T(8,128)S(1)} %slice.75), channel_id=1, source_target_pairs={{0,12},{4,0},{8,4},{12,8},{1,13},{5,1},{9,5},{13,9},{2,14},{6,2},{... | collective-permute-start | bytes 786440 | tf_op jit(solution)/shard_map/ppermute | solution.py:394
  41.4 5.1 %collective-permute-start.5 = (f32[256,128]{1,0:T(8,128)S(1)}, f32[256,128]{1,0:T(8,128)S(1)}, u32[]{:S(2)}, u32[]{:S(2)}) collective-permute-start(f32[256,128]{1,0:T(8,128)S(1)} %slice.56), channel_id=1, source_target_pairs={{16,0},{32,16},{48,32},{64,48},{80,64},{96,80},{112,96},{128,112},... | collective-permute-start | bytes 393224 | tf_op jit(solution)/shard_map/ppermute | solution.py:399
  46.6 1.9 %collective-permute-done.12.before_ref = f32[2,64,512]{2,1,0:T(8,128)S(1)} collective-permute-done((f32[2,64,512]{2,1,0:T(8,128)S(1)}, f32[2,64,512]{2,1,0:T(8,128)S(1)}, u32[]{:S(2)}, u32[]{:S(2)}) %collective-permute-start.12) | collective-permute-done | bytes 262176 | tf_op jit(solution)/shard_map/ppermute | solution.py:394
  48.4 1.5 %collective-permute-start.16 = (f32[2,32,512]{2,1,0:T(8,128)S(1)}, f32[2,32,512]{2,1,0:T(8,128)S(1)}, u32[]{:S(2)}, u32[]{:S(2)}) collective-permute-start(f32[2,32,512]{2,1,0:T(8,128)S(1)} %slice.76), channel_id=1, source_target_pairs={{0,3},{1,0},{2,1},{3,2},{4,7},{5,4},{6,5},{7,6},{8,11},{9,8},{10,9... | collective-permute-start | bytes 393224 | tf_op jit(solution)/shard_map/ppermute | solution.py:394
  49.9 1.0 collective-permute-start.15
  50.9 9.1 %prepare.2 = (bf16[4,512,512]{2,1,0:T(8,128)(2,1)S(1)}, bf16[4,512,512]{2,1,0:T(8,128)(2,1)S(1)}) custom-call(s32[6]{0:T(128)S(1)} %stack.43.index_ref, f32[4,64,512]{2,1,0:T(8,128)S(1)} %pad_maximum_fusion.near_ref, f32[4,64,512]{2,1,0:T(8,128)S(1)} %collective-permute-done.9.after_ref, f32[4,64,512]{2,1,0:T(8,128)S(1)} %collective-permute-done.10.before_ref, ...), custom_call_target="tpu_custom_call" | custom-call | flops 2000000000 | bytes 1000000 | tf_op jit(solution)/shard_map/prepare/pallas_call | solution.py:117
  60.1 5.9 %prepare.3 = (bf16[2,512,512]{2,1,0:T(8,128)(2,1)S(1)}, bf16[2,512,512]{2,1,0:T(8,128)(2,1)S(1)}) custom-call(s32[4]{0:T(128)S(1)} %pad_add_fusion.index_ref, f32[2,64,512]{2,1,0:T(8,128)S(1)} %pad_maximum_fusion.1.near_ref, f32[2,64,512]{2,1,0:T(8,128)S(1)} %collective-permute-done.13.after_ref, f32[2,64,512]{2,1,0:T(8,128)S(1)} %collective-permute-done.12.before_ref, ...), custom_call_target="tpu_custom_call" | custom-call | flops 2000000000 | bytes 1000000 | tf_op jit(solution)/shard_map/prepare/pallas_call | solution.py:117
  66.0 4.5 %operate.1 = (f32[6,256,256]{2,1,0:T(8,128)S(1)}, f32[768,1024]{1,0:T(8,128)S(1)}, f32[128,1792]{1,0:T(8,128)S(1)}) custom-call(s32[2]{0:T(128)S(1)} %add_convert_fusion.ends_ref, f32[256,128]{1,0:T(8,128)S(1)} %collective-permute-done.5.data_ref, f32[512,128]{1,0:T(8,128)S(1)} %copy-done, bf16[4,512,512]{2,1,0:T(8,128)(2,1)S(1)} %get-tuple-element.58.ah, ...), custom_call_target="tpu_custom_call" | custom-call | tf_op jit(solution)/shard_map/operate/pallas_call | solution.py:212
  70.5 9.5 %collective-permute-start.17 = (f32[6,256,256]{2,1,0:T(8,128)S(1)}, f32[6,256,256]{2,1,0:T(8,128)S(1)}, u32[]{:S(2)}, u32[]{:S(2)}) collective-permute-start(f32[6,256,256]{2,1,0:T(8,128)S(1)} %get-tuple-element.64.mine_ref), channel_id=1, source_target_pairs={{0,16},{16,0},{1,17},{17,1},{2,18},{18,2},{3,19},{19,3},{4,20},{20... | collective-permute-start | bytes 4718600 | tf_op jit(solution)/shard_map/ppermute | solution.py:468
  80.2 3.5 %collective-permute-done.18.got_ref = f32[64,1792]{1,0:T(8,128)S(1)} collective-permute-done((f32[64,1792]{1,0:T(8,128)S(1)}, f32[64,1792]{1,0:T(8,128)S(1)}, u32[]{:S(2)}, u32[]{:S(2)}) %collective-permute-start.18) | collective-permute-done | bytes 458784 | tf_op jit(solution)/shard_map/ppermute | solution.py:469
  83.7 0.4 collective-permute-start.27
  84.1 1.7 %merge.1 = (bf16[6,256,256]{2,1,0:T(8,128)(2,1)S(1)}, bf16[6,256,256]{2,1,0:T(8,128)(2,1)S(1)}, f32[64,768]{1,0:T(8,128)S(1)}) custom-call(s32[1]{0:T(128)} %bitcast.6.odd_ref, f32[6,256,256]{2,1,0:T(8,128)S(1)} %get-tuple-element.64.mine_ref, f32[6,256,256]{2,1,0:T(8,128)S(1)} %collective-permute-done.17.other_ref, f32[64,768]{1,0:T(8,128)S(1)} %slice.77.keep_ref, ...), custom_call_target="tpu_custom_call" | custom-call | tf_op jit(solution)/shard_map/merge/pallas_call | solution.py:255
  85.8 0.7 collective-permute-start.24
  86.5 0.7 collective-permute-start.19
  87.2 0.4 hop.16
  87.5 0.7 collective-permute-start.25
  88.2 0.4 hop.12
  88.6 0.7 collective-permute-start.20
  89.3 0.4 hop.17
  89.6 0.7 collective-permute-start.26
  90.3 0.4 hop.13
  90.7 0.7 collective-permute-start.21
  91.3 0.4 hop.18
  91.7 0.7 collective-permute-start.30
  92.4 0.4 hop.14
  92.8 0.7 collective-permute-start.22
  93.4 0.4 hop.21
  93.8 0.7 collective-permute-start.31
  94.5 0.4 hop.15
  94.8 0.7 collective-permute-start.23
  95.5 4.1 %ending.1 = (bf16[768,1536]{1,0:T(8,128)(2,1)S(1)}, bf16[768,1536]{1,0:T(8,128)(2,1)S(1)}, f32[64,1536]{1,0:T(8,128)S(1)}) custom-call(s32[1]{0:T(128)} %bitcast.6.odd_ref, f32[6,256,256]{2,1,0:T(8,128)S(1)} %get-tuple-element.64.mine_ref, f32[6,256,256]{2,1,0:T(8,128)S(1)} %collective-permute-done.17.other_ref, f32[768,1024]{1,0:T(8,128)S(1)} %get-tuple-element.74.rest_ref, ...), custom_call_target="tpu_custom_call" | custom-call | tf_op jit(solution)/shard_map/ending/pallas_call | solution.py:327
  99.6 0.4 hop.22
  100.0 1.3 collective-permute-start.32
  101.3 0.4 hop.19
  101.7 1.3 collective-permute-start.28
  103.0 16.0 %collective-permute-done.32.state_ref.refs_12_ = f32[32,768]{1,0:T(8,128)S(1)} collective-permute-done((f32[32,768]{1,0:T(8,128)S(1)}, f32[32,768]{1,0:T(8,128)S(1)}, u32[]{:S(2)}, u32[]{:S(2)}) %collective-permute-start.32) | collective-permute-done | bytes 98336 | tf_op jit(solution)/shard_map/ppermute | solution.py:479
  118.9 0.4 hop.23
  119.3 1.3 collective-permute-start.33
  120.6 1.1 collective-permute-done.28.state_ref.refs_5_
  122.0 1.3 collective-permute-start.29
  123.3 2.0 %collective-permute-done.29.refs_6_ = f32[32,768]{1,0:T(8,128)S(1)} collective-permute-done((f32[32,768]{1,0:T(8,128)S(1)}, f32[32,768]{1,0:T(8,128)S(1)}, u32[]{:S(2)}, u32[]{:S(2)}) %collective-permute-start.29) | collective-permute-done | bytes 98336 | tf_op jit(solution)/shard_map/ppermute | solution.py:479
  125.3 0.5 finish.1
  125.9 0.9 finish_own.1
  126.8 1.1 collective-permute-start.34
  127.9 1.3 collective-permute-start.35
  129.2 1.9 %collective-permute-start.36 = (f32[64,512]{1,0:T(8,128)S(1)}, f32[64,512]{1,0:T(8,128)S(1)}, u32[]{:S(2)}, u32[]{:S(2)}) collective-permute-start(f32[64,512]{1,0:T(8,128)S(1)} %get-tuple-element.84), channel_id=1, source_target_pairs={{48,16},{80,48},{112,80},{144,112},{176,144},{208,176},{240,208},{... | collective-permute-start | bytes 393224 | tf_op jit(solution)/shard_map/ppermute | solution.py:495
  131.1 3.7 %collective-permute-done.35 = f32[64,512]{1,0:T(8,128)S(1)} collective-permute-done((f32[64,512]{1,0:T(8,128)S(1)}, f32[64,512]{1,0:T(8,128)S(1)}, u32[]{:S(2)}, u32[]{:S(2)}) %collective-permute-start.35) | collective-permute-done | bytes 131104 | tf_op jit(solution)/shard_map/ppermute | solution.py:495
  134.8 0.7 collective-permute-done.36
  135.7 0.8 copy.3
  (53 shorter events, 1.6 us)
Async XLA Ops:
  0.0 41.4 %copy-start = (f32[512,128]{1,0:T(8,128)S(1)}, f32[512,128]{1,0:T(8,128)}, u32[]{:S(2)}) copy-start(f32[512,128]{1,0:T(8,128)} %own_ref.1) | copy-start | bytes 786436
  1.1 11.5 %collective-permute-start.7 = (f32[4,16,512]{2,1,0:T(8,128)S(1)}, f32[4,16,512]{2,1,0:T(8,128)S(1)}, u32[]{:S(2)}, u32[]{:S(2)}) collective-permute-start(f32[4,16,512]{2,1,0:T(8,128)S(1)} %pad_maximum_fusion.2), channel_id=1, source_target_pairs={{0,1},{1,2},{2,3},{3,0},{4,5},{5,6},{6,7},{7,4},{8,9},{9,10},{10,1... | collective-permute-start | bytes 393224 | tf_op jit(solution)/shard_map/ppermute | solution.py:394
  4.2 14.2 %collective-permute-start.6 = (f32[4,16,512]{2,1,0:T(8,128)S(1)}, f32[4,16,512]{2,1,0:T(8,128)S(1)}, u32[]{:S(2)}, u32[]{:S(2)}) collective-permute-start(f32[4,16,512]{2,1,0:T(8,128)S(1)} %pad_maximum_fusion.2), channel_id=1, source_target_pairs={{0,3},{1,0},{2,1},{3,2},{4,7},{5,4},{6,5},{7,6},{8,11},{9,8},{10,9... | collective-permute-start | bytes 393224 | tf_op jit(solution)/shard_map/ppermute | solution.py:394
  12.6 7.5 %collective-permute-start.8 = (f32[4,16,512]{2,1,0:T(8,128)S(1)}, f32[4,16,512]{2,1,0:T(8,128)S(1)}, u32[]{:S(2)}, u32[]{:S(2)}) collective-permute-start(f32[4,16,512]{2,1,0:T(8,128)S(1)} %collective-permute-done.7), channel_id=1, source_target_pairs={{0,1},{1,2},{2,3},{3,0},{4,5},{5,6},{6,7},{7,4},{8,9},{9,10},{10,1... | collective-permute-start | bytes 393224 | tf_op jit(solution)/shard_map/ppermute | solution.py:394
  12.9 8.8 %collective-permute-start = (f32[16,512]{1,0:T(8,128)S(1)}, f32[16,512]{1,0:T(8,128)S(1)}, u32[]{:S(2)}, u32[]{:S(2)}) collective-permute-start(f32[16,512]{1,0:T(8,128)S(1)} %get-tuple-element.99), channel_id=1, source_target_pairs={{16,0},{32,16},{48,32},{64,48},{80,64},{96,80},{112,96},{128,112},... | collective-permute-start | bytes 98312 | tf_op jit(solution)/shard_map/ppermute | solution.py:399
  15.5 6.9 %collective-permute-start.1 = (f32[16,512]{1,0:T(8,128)S(1)}, f32[16,512]{1,0:T(8,128)S(1)}, u32[]{:S(2)}, u32[]{:S(2)}) collective-permute-start(f32[16,512]{1,0:T(8,128)S(1)} %get-tuple-element.100), channel_id=1, source_target_pairs={{0,16},{16,32},{32,48},{48,64},{64,80},{80,96},{96,112},{112,128},... | collective-permute-start | bytes 98312 | tf_op jit(solution)/shard_map/ppermute | solution.py:399
  20.1 19.6 %collective-permute-start.10 = (f32[4,64,512]{2,1,0:T(8,128)S(1)}, f32[4,64,512]{2,1,0:T(8,128)S(1)}, u32[]{:S(2)}, u32[]{:S(2)}) collective-permute-start(f32[4,64,512]{2,1,0:T(8,128)S(1)} %pad_maximum_fusion.near_ref), channel_id=1, source_target_pairs={{0,4},{4,8},{8,12},{12,0},{1,5},{5,9},{9,13},{13,1},{2,6},{6,10},{... | collective-permute-start | bytes 1572872 | tf_op jit(solution)/shard_map/ppermute | solution.py:394
  21.5 18.4 %collective-permute-start.9 = (f32[4,64,512]{2,1,0:T(8,128)S(1)}, f32[4,64,512]{2,1,0:T(8,128)S(1)}, u32[]{:S(2)}, u32[]{:S(2)}) collective-permute-start(f32[4,64,512]{2,1,0:T(8,128)S(1)} %pad_maximum_fusion.near_ref), channel_id=1, source_target_pairs={{0,12},{4,0},{8,4},{12,8},{1,13},{5,1},{9,5},{13,9},{2,14},{6,2},{... | collective-permute-start | bytes 1572872 | tf_op jit(solution)/shard_map/ppermute | solution.py:394
  22.5 12.0 %collective-permute-start.2 = (f32[2,16,512]{2,1,0:T(8,128)S(1)}, f32[2,16,512]{2,1,0:T(8,128)S(1)}, u32[]{:S(2)}, u32[]{:S(2)}) collective-permute-start(f32[2,16,512]{2,1,0:T(8,128)S(1)} %pad_maximum_fusion.3), channel_id=1, source_target_pairs={{0,12},{4,0},{8,4},{12,8},{1,13},{5,1},{9,5},{13,9},{2,14},{6,2},{... | collective-permute-start | bytes 196616 | tf_op jit(solution)/shard_map/ppermute | solution.py:394
  24.0 12.2 %collective-permute-start.3 = (f32[2,16,512]{2,1,0:T(8,128)S(1)}, f32[2,16,512]{2,1,0:T(8,128)S(1)}, u32[]{:S(2)}, u32[]{:S(2)}) collective-permute-start(f32[2,16,512]{2,1,0:T(8,128)S(1)} %pad_maximum_fusion.3), channel_id=1, source_target_pairs={{0,8},{4,12},{8,0},{12,4},{1,9},{5,13},{9,1},{13,5},{2,10},{6,14},... | collective-permute-start | bytes 196616 | tf_op jit(solution)/shard_map/ppermute | solution.py:394
  25.0 11.3 %collective-permute-start.4 = (f32[2,16,512]{2,1,0:T(8,128)S(1)}, f32[2,16,512]{2,1,0:T(8,128)S(1)}, u32[]{:S(2)}, u32[]{:S(2)}) collective-permute-start(f32[2,16,512]{2,1,0:T(8,128)S(1)} %pad_maximum_fusion.3), channel_id=1, source_target_pairs={{0,4},{4,8},{8,12},{12,0},{1,5},{5,9},{9,13},{13,1},{2,6},{6,10},{... | collective-permute-start | bytes 196616 | tf_op jit(solution)/shard_map/ppermute | solution.py:394
  36.3 10.2 %collective-permute-start.13 = (f32[2,64,512]{2,1,0:T(8,128)S(1)}, f32[2,64,512]{2,1,0:T(8,128)S(1)}, u32[]{:S(2)}, u32[]{:S(2)}) collective-permute-start(f32[2,64,512]{2,1,0:T(8,128)S(1)} %pad_maximum_fusion.1.near_ref), channel_id=1, source_target_pairs={{0,3},{1,0},{2,1},{3,2},{4,7},{5,4},{6,5},{7,6},{8,11},{9,8},{10,9... | collective-permute-start | bytes 786440 | tf_op jit(solution)/shard_map/ppermute | solution.py:394
  39.8 8.7 %collective-permute-start.12 = (f32[2,64,512]{2,1,0:T(8,128)S(1)}, f32[2,64,512]{2,1,0:T(8,128)S(1)}, u32[]{:S(2)}, u32[]{:S(2)}) collective-permute-start(f32[2,64,512]{2,1,0:T(8,128)S(1)} %pad_maximum_fusion.1.near_ref), channel_id=1, source_target_pairs={{0,1},{1,2},{2,3},{3,0},{4,5},{5,6},{6,7},{7,4},{8,9},{9,10},{10,1... | collective-permute-start | bytes 786440 | tf_op jit(solution)/shard_map/ppermute | solution.py:394
  39.8 11.1 %collective-permute-start.11 = (f32[4,32,512]{2,1,0:T(8,128)S(1)}, f32[4,32,512]{2,1,0:T(8,128)S(1)}, u32[]{:S(2)}, u32[]{:S(2)}) collective-permute-start(f32[4,32,512]{2,1,0:T(8,128)S(1)} %slice.73), channel_id=1, source_target_pairs={{0,4},{4,8},{8,12},{12,0},{1,5},{5,9},{9,13},{13,1},{2,6},{6,10},{... | collective-permute-start | bytes 786440 | tf_op jit(solution)/shard_map/ppermute | solution.py:394
  39.9 11.0 %collective-permute-start.14 = (f32[4,32,512]{2,1,0:T(8,128)S(1)}, f32[4,32,512]{2,1,0:T(8,128)S(1)}, u32[]{:S(2)}, u32[]{:S(2)}) collective-permute-start(f32[4,32,512]{2,1,0:T(8,128)S(1)} %slice.75), channel_id=1, source_target_pairs={{0,12},{4,0},{8,4},{12,8},{1,13},{5,1},{9,5},{13,9},{2,14},{6,2},{... | collective-permute-start | bytes 786440 | tf_op jit(solution)/shard_map/ppermute | solution.py:394
  41.4 24.5 %collective-permute-start.5 = (f32[256,128]{1,0:T(8,128)S(1)}, f32[256,128]{1,0:T(8,128)S(1)}, u32[]{:S(2)}, u32[]{:S(2)}) collective-permute-start(f32[256,128]{1,0:T(8,128)S(1)} %slice.56), channel_id=1, source_target_pairs={{16,0},{32,16},{48,32},{64,48},{80,64},{96,80},{112,96},{128,112},... | collective-permute-start | bytes 393224 | tf_op jit(solution)/shard_map/ppermute | solution.py:399
  48.4 11.6 %collective-permute-start.16 = (f32[2,32,512]{2,1,0:T(8,128)S(1)}, f32[2,32,512]{2,1,0:T(8,128)S(1)}, u32[]{:S(2)}, u32[]{:S(2)}) collective-permute-start(f32[2,32,512]{2,1,0:T(8,128)S(1)} %slice.76), channel_id=1, source_target_pairs={{0,3},{1,0},{2,1},{3,2},{4,7},{5,4},{6,5},{7,6},{8,11},{9,8},{10,9... | collective-permute-start | bytes 393224 | tf_op jit(solution)/shard_map/ppermute | solution.py:394
  49.9 10.2 %collective-permute-start.15 = (f32[2,32,512]{2,1,0:T(8,128)S(1)}, f32[2,32,512]{2,1,0:T(8,128)S(1)}, u32[]{:S(2)}, u32[]{:S(2)}) collective-permute-start(f32[2,32,512]{2,1,0:T(8,128)S(1)} %slice.74), channel_id=1, source_target_pairs={{0,1},{1,2},{2,3},{3,0},{4,5},{5,6},{6,7},{7,4},{8,9},{9,10},{10,1... | collective-permute-start | bytes 393224 | tf_op jit(solution)/shard_map/ppermute | solution.py:394
  70.5 13.2 %collective-permute-start.17 = (f32[6,256,256]{2,1,0:T(8,128)S(1)}, f32[6,256,256]{2,1,0:T(8,128)S(1)}, u32[]{:S(2)}, u32[]{:S(2)}) collective-permute-start(f32[6,256,256]{2,1,0:T(8,128)S(1)} %get-tuple-element.64.mine_ref), channel_id=1, source_target_pairs={{0,16},{16,0},{1,17},{17,1},{2,18},{18,2},{3,19},{19,3},{4,20},{20... | collective-permute-start | bytes 4718600 | tf_op jit(solution)/shard_map/ppermute | solution.py:468
  80.0 3.6 %collective-permute-start.18 = (f32[64,1792]{1,0:T(8,128)S(1)}, f32[64,1792]{1,0:T(8,128)S(1)}, u32[]{:S(2)}, u32[]{:S(2)}) collective-permute-start(f32[64,1792]{1,0:T(8,128)S(1)} %get-tuple-element.90), channel_id=1, source_target_pairs={{0,16},{16,0},{1,17},{17,1},{2,18},{18,2},{3,19},{19,3},{4,20},{20... | collective-permute-start | bytes 1376264 | tf_op jit(solution)/shard_map/ppermute | solution.py:469
  83.7 11.8 %collective-permute-start.27 = (f32[768,1024]{1,0:T(8,128)S(1)}, f32[768,1024]{1,0:T(8,128)S(1)}, u32[]{:S(2)}, u32[]{:S(2)}) collective-permute-start(f32[768,1024]{1,0:T(8,128)S(1)} %get-tuple-element.74.rest_ref), channel_id=1, source_target_pairs={{0,16},{16,0},{1,17},{17,1},{2,18},{18,2},{3,19},{19,3},{4,20},{20... | collective-permute-start | bytes 9437192 | tf_op jit(solution)/shard_map/ppermute | solution.py:472
  85.8 1.4 collective-permute-start.24
  86.5 1.7 %collective-permute-start.19 = (f32[32,768]{1,0:T(8,128)S(1)}, f32[32,768]{1,0:T(8,128)S(1)}, u32[]{:S(2)}, u32[]{:S(2)}) collective-permute-start(f32[32,768]{1,0:T(8,128)S(1)} %get-tuple-element.94.add_ref), channel_id=1, source_target_pairs={{0,32},{16,48},{1,33},{17,49},{2,34},{18,50},{3,35},{19,51},{4,36}... | collective-permute-start | bytes 294920 | tf_op jit(solution)/shard_map/ppermute | solution.py:479
  87.5 1.7 %collective-permute-start.25 = (f32[32,768]{1,0:T(8,128)S(1)}, f32[32,768]{1,0:T(8,128)S(1)}, u32[]{:S(2)}, u32[]{:S(2)}) collective-permute-start(f32[32,768]{1,0:T(8,128)S(1)} %hop.16), channel_id=1, source_target_pairs={{32,64},{48,80},{33,65},{49,81},{34,66},{50,82},{35,67},{51,83},{3... | collective-permute-start | bytes 294920 | tf_op jit(solution)/shard_map/ppermute | solution.py:479
  88.6 1.7 %collective-permute-start.20 = (f32[32,768]{1,0:T(8,128)S(1)}, f32[32,768]{1,0:T(8,128)S(1)}, u32[]{:S(2)}, u32[]{:S(2)}) collective-permute-start(f32[32,768]{1,0:T(8,128)S(1)} %hop.12), channel_id=1, source_target_pairs={{32,64},{48,80},{33,65},{49,81},{34,66},{50,82},{35,67},{51,83},{3... | collective-permute-start | bytes 294920 | tf_op jit(solution)/shard_map/ppermute | solution.py:479
  89.6 1.7 %collective-permute-start.26 = (f32[32,768]{1,0:T(8,128)S(1)}, f32[32,768]{1,0:T(8,128)S(1)}, u32[]{:S(2)}, u32[]{:S(2)}) collective-permute-start(f32[32,768]{1,0:T(8,128)S(1)} %hop.17), channel_id=1, source_target_pairs={{64,96},{80,112},{65,97},{81,113},{66,98},{82,114},{67,99},{83,115... | collective-permute-start | bytes 294920 | tf_op jit(solution)/shard_map/ppermute | solution.py:479
  90.7 1.7 %collective-permute-start.21 = (f32[32,768]{1,0:T(8,128)S(1)}, f32[32,768]{1,0:T(8,128)S(1)}, u32[]{:S(2)}, u32[]{:S(2)}) collective-permute-start(f32[32,768]{1,0:T(8,128)S(1)} %hop.13), channel_id=1, source_target_pairs={{64,96},{80,112},{65,97},{81,113},{66,98},{82,114},{67,99},{83,115... | collective-permute-start | bytes 294920 | tf_op jit(solution)/shard_map/ppermute | solution.py:479
  91.7 1.7 %collective-permute-start.30 = (f32[32,768]{1,0:T(8,128)S(1)}, f32[32,768]{1,0:T(8,128)S(1)}, u32[]{:S(2)}, u32[]{:S(2)}) collective-permute-start(f32[32,768]{1,0:T(8,128)S(1)} %hop.18), channel_id=1, source_target_pairs={{96,144},{112,128},{97,145},{113,129},{98,146},{114,130},{99,147},... | collective-permute-start | bytes 294920 | tf_op jit(solution)/shard_map/ppermute | solution.py:479
  92.8 1.7 %collective-permute-start.22 = (f32[32,768]{1,0:T(8,128)S(1)}, f32[32,768]{1,0:T(8,128)S(1)}, u32[]{:S(2)}, u32[]{:S(2)}) collective-permute-start(f32[32,768]{1,0:T(8,128)S(1)} %hop.14), channel_id=1, source_target_pairs={{96,144},{112,128},{97,145},{113,129},{98,146},{114,130},{99,147},... | collective-permute-start | bytes 294920 | tf_op jit(solution)/shard_map/ppermute | solution.py:479
  93.8 5.8 %collective-permute-start.31 = (f32[32,768]{1,0:T(8,128)S(1)}, f32[32,768]{1,0:T(8,128)S(1)}, u32[]{:S(2)}, u32[]{:S(2)}) collective-permute-start(f32[32,768]{1,0:T(8,128)S(1)} %hop.21), channel_id=1, source_target_pairs={{128,160},{144,176},{129,161},{145,177},{130,162},{146,178},{131,1... | collective-permute-start | bytes 294920 | tf_op jit(solution)/shard_map/ppermute | solution.py:479
  94.8 6.4 %collective-permute-start.23 = (f32[32,768]{1,0:T(8,128)S(1)}, f32[32,768]{1,0:T(8,128)S(1)}, u32[]{:S(2)}, u32[]{:S(2)}) collective-permute-start(f32[32,768]{1,0:T(8,128)S(1)} %hop.15), channel_id=1, source_target_pairs={{128,160},{144,176},{129,161},{145,177},{130,162},{146,178},{131,1... | collective-permute-start | bytes 294920 | tf_op jit(solution)/shard_map/ppermute | solution.py:479
  100.0 18.9 %collective-permute-start.32 = (f32[32,768]{1,0:T(8,128)S(1)}, f32[32,768]{1,0:T(8,128)S(1)}, u32[]{:S(2)}, u32[]{:S(2)}) collective-permute-start(f32[32,768]{1,0:T(8,128)S(1)} %hop.22), channel_id=1, source_target_pairs={{160,192},{176,208},{161,193},{177,209},{162,194},{178,210},{163,1... | collective-permute-start | bytes 294920 | tf_op jit(solution)/shard_map/ppermute | solution.py:479
  101.7 20.0 %collective-permute-start.28 = (f32[32,768]{1,0:T(8,128)S(1)}, f32[32,768]{1,0:T(8,128)S(1)}, u32[]{:S(2)}, u32[]{:S(2)}) collective-permute-start(f32[32,768]{1,0:T(8,128)S(1)} %hop.19), channel_id=1, source_target_pairs={{160,192},{176,208},{161,193},{177,209},{162,194},{178,210},{163,1... | collective-permute-start | bytes 294920 | tf_op jit(solution)/shard_map/ppermute | solution.py:479
  119.3 4.0 %collective-permute-start.33 = (f32[32,768]{1,0:T(8,128)S(1)}, f32[32,768]{1,0:T(8,128)S(1)}, u32[]{:S(2)}, u32[]{:S(2)}) collective-permute-start(f32[32,768]{1,0:T(8,128)S(1)} %hop.23), channel_id=1, source_target_pairs={{192,224},{208,240},{193,225},{209,241},{194,226},{210,242},{195,2... | collective-permute-start | bytes 294920 | tf_op jit(solution)/shard_map/ppermute | solution.py:479
  122.0 3.3 %collective-permute-start.29 = (f32[32,768]{1,0:T(8,128)S(1)}, f32[32,768]{1,0:T(8,128)S(1)}, u32[]{:S(2)}, u32[]{:S(2)}) collective-permute-start(f32[32,768]{1,0:T(8,128)S(1)} %hop.20), channel_id=1, source_target_pairs={{192,224},{208,240},{193,225},{209,241},{194,226},{210,242},{195,2... | collective-permute-start | bytes 294920 | tf_op jit(solution)/shard_map/ppermute | solution.py:479
  126.8 4.3 %collective-permute-start.34 = (f32[64,512]{1,0:T(8,128)S(1)}, f32[64,512]{1,0:T(8,128)S(1)}, u32[]{:S(2)}, u32[]{:S(2)}) collective-permute-start(f32[64,512]{1,0:T(8,128)S(1)} %broadcast_select_fusion), channel_id=1, source_target_pairs={{0,16},{16,0},{1,17},{17,1},{2,18},{18,2},{3,19},{19,3},{4,20},{20... | collective-permute-start | bytes 393224 | tf_op jit(solution)/shard_map/ppermute | solution.py:497
  127.9 6.9 %collective-permute-start.35 = (f32[64,512]{1,0:T(8,128)S(1)}, f32[64,512]{1,0:T(8,128)S(1)}, u32[]{:S(2)}, u32[]{:S(2)}) collective-permute-start(f32[64,512]{1,0:T(8,128)S(1)} %get-tuple-element.84), channel_id=1, source_target_pairs={{32,16},{64,48},{96,80},{128,112},{160,144},{192,176},{224,208},{3... | collective-permute-start | bytes 393224 | tf_op jit(solution)/shard_map/ppermute | solution.py:495
  129.2 6.4 %collective-permute-start.36 = (f32[64,512]{1,0:T(8,128)S(1)}, f32[64,512]{1,0:T(8,128)S(1)}, u32[]{:S(2)}, u32[]{:S(2)}) collective-permute-start(f32[64,512]{1,0:T(8,128)S(1)} %get-tuple-element.84), channel_id=1, source_target_pairs={{48,16},{80,48},{112,80},{144,112},{176,144},{208,176},{240,208},{... | collective-permute-start | bytes 393224 | tf_op jit(solution)/shard_map/ppermute | solution.py:495

commit v3 on v2

--- a/solution.py
+++ b/solution.py
@@ -224,12 +224,12 @@
     )(ends, data, own, *parts)
 
 
-def merge_body(odd_ref, mine_ref, other_ref, keep_ref, got_ref, high_ref, low_ref, add_ref):
+def merge_add_body(odd_ref, mine_ref, other_ref, keep_ref, got_ref, add_ref):
     n = mine_ref.shape[1]
     odd = odd_ref[0] == 1
-    keep = keep_ref[...]
-    got = got_ref[...]
-    even_parts = [split(jnp.where(odd, other_ref[k], mine_ref[k])) for k in range(6)]
+    wide = slice(0, 3 * n)
+    keep = keep_ref[:, wide]
+    got = got_ref[:, wide]
     odd_parts = [split(jnp.where(odd, mine_ref[k], other_ref[k])) for k in range(6)]
     odd_add = jnp.where(odd, keep, got)
     add_parts = split(jnp.where(odd, got, keep))
@@ -239,6 +239,27 @@
             columns = slice(j * n, (j + 1) * n)
             total = total + dot3((add_parts[0][:, columns], add_parts[1][:, columns]), odd_parts[PAIRS.index((j, s))])
         add_ref[:, s * n : (s + 1) * n] = total
+
+
+def merge_add(odd, mine, other, keep, got):
+    n = mine.shape[1]
+    vmem = pl.BlockSpec(memory_space=pltpu.VMEM)
+    return pl.pallas_call(
+        merge_add_body,
+        out_shape=jax.ShapeDtypeStruct((keep.shape[0], 3 * n), jnp.float32),
+        in_specs=[pl.BlockSpec(memory_space=pltpu.SMEM)] + [vmem] * 4,
+        out_specs=vmem,
+        compiler_params=pltpu.CompilerParams(vmem_limit_bytes=16 * 1024 * 1024),
+        interpret=INTERPRET,
+        name="merge_add",
+    )(odd, mine, other, keep, got)
+
+
+def merge_map_body(odd_ref, mine_ref, other_ref, high_ref, low_ref):
+    odd = odd_ref[0] == 1
+    even_parts = [split(jnp.where(odd, other_ref[k], mine_ref[k])) for k in range(6)]
+    odd_parts = [split(jnp.where(odd, mine_ref[k], other_ref[k])) for k in range(6)]
+    for s in range(3):
         for k in range(s + 1):
             total = None
             for j in range(k, s + 1):
@@ -247,20 +268,18 @@
             high_ref[PAIRS.index((k, s))], low_ref[PAIRS.index((k, s))] = split(total)
 
 
-def merge(odd, mine, other, keep, got):
-    n = mine.shape[1]
-    half = keep.shape[0]
-    vmem = pl.BlockSpec(memory_space=pltpu.VMEM)
-    packed = jax.ShapeDtypeStruct((6, n, n), jnp.bfloat16)
-    return pl.pallas_call(
-        merge_body,
-        out_shape=(packed, packed, jax.ShapeDtypeStruct((half, 3 * n), jnp.float32)),
-        in_specs=[pl.BlockSpec(memory_space=pltpu.SMEM)] + [vmem] * 4,
-        out_specs=(vmem,) * 3,
-        compiler_params=pltpu.CompilerParams(vmem_limit_bytes=20 * 1024 * 1024),
-        interpret=INTERPRET,
-        name="merge",
-    )(odd, mine, other, keep, got)
+def merge_map(odd, mine, other):
+    vmem = pl.BlockSpec(memory_space=pltpu.VMEM)
+    packed = jax.ShapeDtypeStruct(mine.shape, jnp.bfloat16)
+    return pl.pallas_call(
+        merge_map_body,
+        out_shape=(packed, packed),
+        in_specs=[pl.BlockSpec(memory_space=pltpu.SMEM)] + [vmem] * 2,
+        out_specs=(vmem,) * 2,
+        compiler_params=pltpu.CompilerParams(vmem_limit_bytes=16 * 1024 * 1024),
+        interpret=INTERPRET,
+        name="merge_map",
+    )(odd, mine, other)
 
 
 def hop_body(state_ref, high_ref, low_ref, add_ref, out_ref):
@@ -389,6 +408,32 @@
     )(state, high, low, add)
 
 
+def close_body(places_ref, got_ref, hand0_ref, hand1_ref, even_ref, odd_ref, out_ref):
+    odd, last, flipped, flips_next = [places_ref[k] == 1 for k in range(4)]
+    got = got_ref[...]
+    for_even = even_ref[...]
+    for_odd = odd_ref[...]
+    near = jnp.where(flips_next, hand1_ref[...], hand0_ref[...])
+    far = jnp.where(flips_next, hand0_ref[...], hand1_ref[...])
+    upper = jnp.where(odd, jnp.where(last, for_odd, near), jnp.where(flipped, got, for_even))
+    lower = jnp.where(odd, jnp.where(last, got, far), jnp.where(flipped, for_even, got))
+    out_ref[...] = jnp.concatenate([upper, lower], axis=0).T
+
+
+def close(places, got, hand0, hand1, for_even, for_odd):
+    half, m = got.shape
+    vmem = pl.BlockSpec(memory_space=pltpu.VMEM)
+    return pl.pallas_call(
+        close_body,
+        out_shape=jax.ShapeDtypeStruct((m, 2 * half), jnp.float32),
+        in_specs=[pl.BlockSpec(memory_space=pltpu.SMEM)] + [vmem] * 5,
+        out_specs=vmem,
+        compiler_params=pltpu.CompilerParams(vmem_limit_bytes=8 * 1024 * 1024),
+        interpret=INTERPRET,
+        name="close",
+    )(places, got, hand0, hand1, for_even, for_odd)
+
+
 def ring(value, axis, step):
     count = lax.axis_size(axis)
     return lax.ppermute(value, axis, [(k, (k + step) % count) for k in range(count)])
@@ -423,8 +468,9 @@
     index_b = jnp.stack([*at, one, held]).astype(jnp.int32)
     ends = jnp.stack([is_first, is_last]).astype(jnp.int32)
     odd = is_odd.astype(jnp.int32).reshape(1)
-    local, is_last, is_odd, flipped, flips_next, takes_second, on_last, index_a, index_b, ends, odd = lax.optimization_barrier(
-        (local, is_last, is_odd, flipped, flips_next, takes_second, on_last, index_a, index_b, ends, odd)
+    places = jnp.stack([is_odd, on_last, flipped, flips_next]).astype(jnp.int32)
+    local, is_last, is_odd, takes_second, places, index_a, index_b, ends, odd = lax.optimization_barrier(
+        (local, is_last, is_odd, takes_second, places, index_a, index_b, ends, odd)
     )
     n = eigenvectors.shape[0] // 2
     stay = jnp.stack([local[0, 1], local[1, 0], local[1, 1], local[2, 0]])
@@ -468,8 +514,9 @@
     other = lax.ppermute(step, "core", swap)
     got = lax.ppermute(give, "core", swap)
     rest, other, got = lax.optimization_barrier((rest, other, got))
-    high, low, chip_add = merge(odd, step, other, keep[:, : 3 * n], got[:, : 3 * n])
+    chip_add = merge_add(odd, step, other, keep, got)
     other_rest = lax.ppermute(rest, "core", swap)
+    high, low = merge_map(odd, step, other)
 
     sub = half // SUBS
     adds = [chip_add[k * sub : (k + 1) * sub] for k in range(SUBS)]
@@ -478,7 +525,9 @@
         turn = 1 if hop == middle else 0
         return lax.ppermute(value, ROW, [(2 * hop - 2 + side, 2 * hop + (side ^ turn)) for side in range(2)])
 
-    arrived = [[onward(part, 1)] for part in adds]
+    arrived = []
+    for k in range(SUBS):
+        arrived.append([onward(adds[k], 1)])
     for hop in range(2, chips):
         for k in range(SUBS):
             sent = hop_on(arrived[k][-1], high, low, adds[k])
@@ -495,11 +544,7 @@
         handed.append(lax.ppermute(for_prior, ROW, pairs))
     for_even, for_odd = finish_own(state, *ended)
     got = lax.ppermute(jnp.where(is_odd, for_even, for_odd), "core", swap)
-    got, *handed = lax.optimization_barrier((got, *handed))
-    near, far = jnp.where(flips_next, handed[1], handed[0]), jnp.where(flips_next, handed[0], handed[1])
-    upper = jnp.where(is_odd, jnp.where(on_last, for_odd, near), jnp.where(flipped, got, for_even))
-    lower = jnp.where(is_odd, jnp.where(on_last, got, far), jnp.where(flipped, for_even, got))
-    return jnp.concatenate([upper, lower], axis=0).T
+    return close(places, got, *handed, for_even, for_odd)
 
 
 def solution(mesh):

time: 137 us -> 136 us (level)
  Pallas kernels: 31.1 us -> 32.8 us
    pallas_call x1 -> x3, Pallas kernels: 1.68 us -> 3.42 us  [the longest x1 1.41 us: close(): pl.pallas_call(close_body, out_shape=jax.ShapeDtypeStruct((m, 2 * half),...]
  transfers between devices with their start and end apart: 37 -> 37, of which waited for: 11 -> 11; matrix products, arithmetic and copies ran while one was open for 1% -> 1% of each run, Pallas kernels for 18% -> 19%
where the time goes in v3:
time: 136 us
  starting transfers between devices  55.3 us (41%)
  waiting for transfers between devices  45.2 us (33%)
  Pallas kernels  32.8 us (24%)
    ppermute x14, waiting for transfers between devices, ring(): lax.ppermute(value, axis, [(k, (k + step) % count) for k in range(count)])  19.5 us
    ppermute x14, starting transfers between devices, ring(): lax.ppermute(value, axis, [(k, (k + step) % count) for k in range(count)])  18.7 us
    ppermute x14, waiting for transfers between devices, onward(): lax.ppermute(value, ROW, [(2 * hop - 2 + side, 2 * hop + (side ^ turn)) f...  17.7 us
    pallas_call x2, Pallas kernels, prepare(): pl.pallas_call(functools.partial(prepare_body, outer_y), out_shape=(out,...  15.1 us
    ppermute x14, starting transfers between devices, onward(): lax.ppermute(value, ROW, [(2 * hop - 2 + side, 2 * hop + (side ^ turn)) f...  11.8 us
    ppermute x3, starting transfers between devices, shifted(): lax.ppermute(value, ROW, [(k, k + step) for k in range(max(0, -step), min...  10.6 us
    ppermute x1, starting transfers between devices, shards(): other = lax.ppermute(step, 'core', swap)  9.48 us
    ppermute x2, waiting for transfers between devices, shards(): handed.append(lax.ppermute(for_prior, ROW, pairs))  4.45 us
  transfers between devices with their start and end apart: 37, of which 11 were waited for; matrix products, arithmetic and copies ran while one was open for 1% of the time, Pallas kernels for 19%

profile of v3, /device:TPU:45, one launch (start us, length us, event | category | flops | bytes accessed | tf_op | source)
XLA Modules:
  0.0 136.0 jit_solution(13846555801183164039)
XLA Ops:
  0.3 0.9 slice_bitcast_fusion.3
  1.2 3.1 %collective-permute-start.7 = (f32[4,16,512]{2,1,0:T(8,128)S(1)}, f32[4,16,512]{2,1,0:T(8,128)S(1)}, u32[]{:S(2)}, u32[]{:S(2)}) collective-permute-start(f32[4,16,512]{2,1,0:T(8,128)S(1)} %pad_maximum_fusion.2), channel_id=1, source_target_pairs={{0,1},{1,2},{2,3},{3,0},{4,5},{5,6},{6,7},{7,4},{8,9},{9,10},{10,1... | collective-permute-start | bytes 393224 | tf_op jit(solution)/shard_map/ppermute | solution.py:439
  4.3 2.2 %collective-permute-start.6 = (f32[4,16,512]{2,1,0:T(8,128)S(1)}, f32[4,16,512]{2,1,0:T(8,128)S(1)}, u32[]{:S(2)}, u32[]{:S(2)}) collective-permute-start(f32[4,16,512]{2,1,0:T(8,128)S(1)} %pad_maximum_fusion.2), channel_id=1, source_target_pairs={{0,3},{1,0},{2,1},{3,2},{4,7},{5,4},{6,5},{7,6},{8,11},{9,8},{10,9... | collective-permute-start | bytes 393224 | tf_op jit(solution)/shard_map/ppermute | solution.py:439
  6.5 6.2 %collective-permute-done.7 = f32[4,16,512]{2,1,0:T(8,128)S(1)} collective-permute-done((f32[4,16,512]{2,1,0:T(8,128)S(1)}, f32[4,16,512]{2,1,0:T(8,128)S(1)}, u32[]{:S(2)}, u32[]{:S(2)}) %collective-permute-start.7) | collective-permute-done | bytes 131104 | tf_op jit(solution)/shard_map/ppermute | solution.py:439
  12.9 2.7 %collective-permute-start = (f32[16,512]{1,0:T(8,128)S(1)}, f32[16,512]{1,0:T(8,128)S(1)}, u32[]{:S(2)}, u32[]{:S(2)}) collective-permute-start(f32[16,512]{1,0:T(8,128)S(1)} %get-tuple-element.85), channel_id=1, source_target_pairs={{16,0},{32,16},{48,32},{64,48},{80,64},{96,80},{112,96},{128,112},... | collective-permute-start | bytes 98312 | tf_op jit(solution)/shard_map/ppermute | solution.py:444
  15.6 2.9 %collective-permute-start.1 = (f32[16,512]{1,0:T(8,128)S(1)}, f32[16,512]{1,0:T(8,128)S(1)}, u32[]{:S(2)}, u32[]{:S(2)}) collective-permute-start(f32[16,512]{1,0:T(8,128)S(1)} %get-tuple-element.86), channel_id=1, source_target_pairs={{0,16},{16,32},{32,48},{48,64},{64,80},{80,96},{96,112},{112,128},... | collective-permute-start | bytes 98312 | tf_op jit(solution)/shard_map/ppermute | solution.py:444
  18.5 1.7 %collective-permute-done.8 = f32[4,16,512]{2,1,0:T(8,128)S(1)} collective-permute-done((f32[4,16,512]{2,1,0:T(8,128)S(1)}, f32[4,16,512]{2,1,0:T(8,128)S(1)}, u32[]{:S(2)}, u32[]{:S(2)}) %collective-permute-start.8) | collective-permute-done | bytes 131104 | tf_op jit(solution)/shard_map/ppermute | solution.py:439
  20.2 1.3 collective-permute-start.10
  21.8 0.8 select_bitcast_fusion
  22.5 1.6 %collective-permute-start.2 = (f32[2,16,512]{2,1,0:T(8,128)S(1)}, f32[2,16,512]{2,1,0:T(8,128)S(1)}, u32[]{:S(2)}, u32[]{:S(2)}) collective-permute-start(f32[2,16,512]{2,1,0:T(8,128)S(1)} %pad_maximum_fusion.3), channel_id=1, source_target_pairs={{0,12},{4,0},{8,4},{12,8},{1,13},{5,1},{9,5},{13,9},{2,14},{6,2},{... | collective-permute-start | bytes 196616 | tf_op jit(solution)/shard_map/ppermute | solution.py:439
  24.1 0.9 collective-permute-start.3
  25.1 1.6 %collective-permute-start.4 = (f32[2,16,512]{2,1,0:T(8,128)S(1)}, f32[2,16,512]{2,1,0:T(8,128)S(1)}, u32[]{:S(2)}, u32[]{:S(2)}) collective-permute-start(f32[2,16,512]{2,1,0:T(8,128)S(1)} %pad_maximum_fusion.3), channel_id=1, source_target_pairs={{0,4},{4,8},{8,12},{12,0},{1,5},{5,9},{9,13},{13,1},{2,6},{6,10},{... | collective-permute-start | bytes 196616 | tf_op jit(solution)/shard_map/ppermute | solution.py:439
  26.7 7.8 %collective-permute-done.2 = f32[2,16,512]{2,1,0:T(8,128)S(1)} collective-permute-done((f32[2,16,512]{2,1,0:T(8,128)S(1)}, f32[2,16,512]{2,1,0:T(8,128)S(1)}, u32[]{:S(2)}, u32[]{:S(2)}) %collective-permute-start.2) | collective-permute-done | bytes 65568 | tf_op jit(solution)/shard_map/ppermute | solution.py:439
  34.5 1.8 %collective-permute-done.3 = f32[2,16,512]{2,1,0:T(8,128)S(1)} collective-permute-done((f32[2,16,512]{2,1,0:T(8,128)S(1)}, f32[2,16,512]{2,1,0:T(8,128)S(1)}, u32[]{:S(2)}, u32[]{:S(2)}) %collective-permute-start.3) | collective-permute-done | bytes 65568 | tf_op jit(solution)/shard_map/ppermute | solution.py:439
  36.4 3.5 %collective-permute-start.13 = (f32[2,64,512]{2,1,0:T(8,128)S(1)}, f32[2,64,512]{2,1,0:T(8,128)S(1)}, u32[]{:S(2)}, u32[]{:S(2)}) collective-permute-start(f32[2,64,512]{2,1,0:T(8,128)S(1)} %pad_maximum_fusion.1.near_ref), channel_id=1, source_target_pairs={{0,3},{1,0},{2,1},{3,2},{4,7},{5,4},{6,5},{7,6},{8,11},{9,8},{10,9... | collective-permute-start | bytes 786440 | tf_op jit(solution)/shard_map/ppermute | solution.py:439
  40.0 1.5 %collective-permute-start.14 = (f32[4,32,512]{2,1,0:T(8,128)S(1)}, f32[4,32,512]{2,1,0:T(8,128)S(1)}, u32[]{:S(2)}, u32[]{:S(2)}) collective-permute-start(f32[4,32,512]{2,1,0:T(8,128)S(1)} %slice.67), channel_id=1, source_target_pairs={{0,12},{4,0},{8,4},{12,8},{1,13},{5,1},{9,5},{13,9},{2,14},{6,2},{... | collective-permute-start | bytes 786440 | tf_op jit(solution)/shard_map/ppermute | solution.py:439
  41.5 5.1 %collective-permute-start.5 = (f32[256,128]{1,0:T(8,128)S(1)}, f32[256,128]{1,0:T(8,128)S(1)}, u32[]{:S(2)}, u32[]{:S(2)}) collective-permute-start(f32[256,128]{1,0:T(8,128)S(1)} %slice.50), channel_id=1, source_target_pairs={{16,0},{32,16},{48,32},{64,48},{80,64},{96,80},{112,96},{128,112},... | collective-permute-start | bytes 393224 | tf_op jit(solution)/shard_map/ppermute | solution.py:444
  46.6 1.9 %collective-permute-done.12.before_ref = f32[2,64,512]{2,1,0:T(8,128)S(1)} collective-permute-done((f32[2,64,512]{2,1,0:T(8,128)S(1)}, f32[2,64,512]{2,1,0:T(8,128)S(1)}, u32[]{:S(2)}, u32[]{:S(2)}) %collective-permute-start.12) | collective-permute-done | bytes 262176 | tf_op jit(solution)/shard_map/ppermute | solution.py:439
  48.5 1.5 %collective-permute-start.16 = (f32[2,32,512]{2,1,0:T(8,128)S(1)}, f32[2,32,512]{2,1,0:T(8,128)S(1)}, u32[]{:S(2)}, u32[]{:S(2)}) collective-permute-start(f32[2,32,512]{2,1,0:T(8,128)S(1)} %slice.68), channel_id=1, source_target_pairs={{0,3},{1,0},{2,1},{3,2},{4,7},{5,4},{6,5},{7,6},{8,11},{9,8},{10,9... | collective-permute-start | bytes 393224 | tf_op jit(solution)/shard_map/ppermute | solution.py:439
  50.0 1.0 collective-permute-start.15
  51.0 9.2 %prepare.2 = (bf16[4,512,512]{2,1,0:T(8,128)(2,1)S(1)}, bf16[4,512,512]{2,1,0:T(8,128)(2,1)S(1)}) custom-call(s32[6]{0:T(128)S(1)} %stack.63.index_ref, f32[4,64,512]{2,1,0:T(8,128)S(1)} %pad_maximum_fusion.near_ref, f32[4,64,512]{2,1,0:T(8,128)S(1)} %collective-permute-done.9.after_ref, f32[4,64,512]{2,1,0:T(8,128)S(1)} %collective-permute-done.10.before_ref, ...), custom_call_target="tpu_custom_call" | custom-call | flops 2000000000 | bytes 1000000 | tf_op jit(solution)/shard_map/prepare/pallas_call | solution.py:117
  60.2 5.9 %prepare.3 = (bf16[2,512,512]{2,1,0:T(8,128)(2,1)S(1)}, bf16[2,512,512]{2,1,0:T(8,128)(2,1)S(1)}) custom-call(s32[4]{0:T(128)S(1)} %pad_add_fusion.index_ref, f32[2,64,512]{2,1,0:T(8,128)S(1)} %pad_maximum_fusion.1.near_ref, f32[2,64,512]{2,1,0:T(8,128)S(1)} %collective-permute-done.13.after_ref, f32[2,64,512]{2,1,0:T(8,128)S(1)} %collective-permute-done.12.before_ref, ...), custom_call_target="tpu_custom_call" | custom-call | flops 2000000000 | bytes 1000000 | tf_op jit(solution)/shard_map/prepare/pallas_call | solution.py:117
  66.1 4.4 %operate.1 = (f32[6,256,256]{2,1,0:T(8,128)S(1)}, f32[768,1024]{1,0:T(8,128)S(1)}, f32[128,1792]{1,0:T(8,128)S(1)}) custom-call(s32[2]{0:T(128)S(1)} %add_convert_fusion.1.ends_ref, f32[256,128]{1,0:T(8,128)S(1)} %collective-permute-done.5.data_ref, f32[512,128]{1,0:T(8,128)S(1)} %copy-done, bf16[4,512,512]{2,1,0:T(8,128)(2,1)S(1)} %get-tuple-element.52.ah, ...), custom_call_target="tpu_custom_call" | custom-call | tf_op jit(solution)/shard_map/operate/pallas_call | solution.py:212
  70.5 9.5 %collective-permute-start.17 = (f32[6,256,256]{2,1,0:T(8,128)S(1)}, f32[6,256,256]{2,1,0:T(8,128)S(1)}, u32[]{:S(2)}, u32[]{:S(2)}) collective-permute-start(f32[6,256,256]{2,1,0:T(8,128)S(1)} %get-tuple-element.58.mine_ref), channel_id=1, source_target_pairs={{0,16},{16,0},{1,17},{17,1},{2,18},{18,2},{3,19},{19,3},{4,20},{20... | collective-permute-start | bytes 4718600 | tf_op jit(solution)/shard_map/ppermute | solution.py:514
  80.2 3.5 %collective-permute-done.18.got_ref = f32[64,1792]{1,0:T(8,128)S(1)} collective-permute-done((f32[64,1792]{1,0:T(8,128)S(1)}, f32[64,1792]{1,0:T(8,128)S(1)}, u32[]{:S(2)}, u32[]{:S(2)}) %collective-permute-start.18) | collective-permute-done | bytes 458784 | tf_op jit(solution)/shard_map/ppermute | solution.py:515
  83.7 0.4 collective-permute-start.27
  84.1 0.7 merge_add.1
  84.8 0.7 collective-permute-start.24
  85.5 0.7 collective-permute-start.19
  86.1 1.3 merge_map.1
  87.5 0.4 hop.16
  87.9 0.7 collective-permute-start.25
  88.9 0.7 collective-permute-start.20
  89.9 0.7 collective-permute-start.26
  90.6 0.4 hop.13
  91.0 0.7 collective-permute-start.21
  91.7 0.4 hop.18
  92.0 0.7 collective-permute-start.30
  92.7 0.4 hop.14
  93.1 0.7 collective-permute-start.22
  93.8 0.4 hop.21
  94.1 0.7 collective-permute-start.31
  94.8 0.4 hop.15
  95.2 0.7 collective-permute-start.23
  95.8 4.1 %ending.1 = (bf16[768,1536]{1,0:T(8,128)(2,1)S(1)}, bf16[768,1536]{1,0:T(8,128)(2,1)S(1)}, f32[64,1536]{1,0:T(8,128)S(1)}) custom-call(s32[1]{0:T(128)S(6)} %reshape.9.odd_ref, f32[6,256,256]{2,1,0:T(8,128)S(1)} %get-tuple-element.58.mine_ref, f32[6,256,256]{2,1,0:T(8,128)S(1)} %collective-permute-done.17.other_ref, ...), custom_call_target="tpu_custom_call" | custom-call | tf_op jit(solution)/shard_map/ending/pallas_call | solution.py:346
  100.0 0.4 hop.22
  100.3 1.3 collective-permute-start.32
  101.6 0.4 hop.19
  102.0 1.3 collective-permute-start.28
  103.3 14.6 %collective-permute-done.32.state_ref.refs_12_ = f32[32,768]{1,0:T(8,128)S(1)} collective-permute-done((f32[32,768]{1,0:T(8,128)S(1)}, f32[32,768]{1,0:T(8,128)S(1)}, u32[]{:S(2)}, u32[]{:S(2)}) %collective-permute-start.32) | collective-permute-done | bytes 98336 | tf_op jit(solution)/shard_map/ppermute | solution.py:526
  117.9 0.4 hop.23
  118.3 1.3 collective-permute-start.33
  119.6 1.1 collective-permute-done.28.state_ref.refs_5_
  120.6 0.4 hop.20
  121.0 1.3 collective-permute-start.29
  122.3 2.0 %collective-permute-done.29.refs_6_ = f32[32,768]{1,0:T(8,128)S(1)} collective-permute-done((f32[32,768]{1,0:T(8,128)S(1)}, f32[32,768]{1,0:T(8,128)S(1)}, u32[]{:S(2)}, u32[]{:S(2)}) %collective-permute-start.29) | collective-permute-done | bytes 98336 | tf_op jit(solution)/shard_map/ppermute | solution.py:526
  124.3 0.5 finish.1
  124.9 0.9 finish_own.1
  125.8 1.1 collective-permute-start.34
  126.9 1.3 collective-permute-start.35
  128.2 1.9 %collective-permute-start.36 = (f32[64,512]{1,0:T(8,128)S(1)}, f32[64,512]{1,0:T(8,128)S(1)}, u32[]{:S(2)}, u32[]{:S(2)}) collective-permute-start(f32[64,512]{1,0:T(8,128)S(1)} %get-tuple-element.76), channel_id=1, source_target_pairs={{48,16},{80,48},{112,80},{144,112},{176,144},{208,176},{240,208},{... | collective-permute-start | bytes 393224 | tf_op jit(solution)/shard_map/ppermute | solution.py:544
  130.1 3.7 %collective-permute-done.35.hand0_ref = f32[64,512]{1,0:T(8,128)S(1)} collective-permute-done((f32[64,512]{1,0:T(8,128)S(1)}, f32[64,512]{1,0:T(8,128)S(1)}, u32[]{:S(2)}, u32[]{:S(2)}) %collective-permute-start.35) | collective-permute-done | bytes 131104 | tf_op jit(solution)/shard_map/ppermute | solution.py:544
  133.8 0.7 collective-permute-done.36.hand1_ref
  134.6 1.4 %close.1 = f32[512,128]{1,0:T(8,128)} custom-call(s32[4]{0:T(128)S(1)} %add_convert_fusion.places_ref, f32[64,512]{1,0:T(8,128)S(1)} %collective-permute-done.34.got_ref, f32[64,512]{1,0:T(8,128)S(1)} %collective-permute-done.35.hand0_ref, f32[64,512]{1,0:T(8,128)S(1)} %collective-permute-done.36.hand1_ref, f32[64,512]{1,0:T(8,128)S(1)} %get-tuple-element.74.even_ref, ...), custom_call_target="tpu_custom_call" | custom-call | tf_op jit(solution)/shard_map/close/pallas_call | solution.py:426
  (51 shorter events, 2.0 us)
Async XLA Ops:
  0.0 41.5 %copy-start = (f32[512,128]{1,0:T(8,128)S(1)}, f32[512,128]{1,0:T(8,128)}, u32[]{:S(2)}) copy-start(f32[512,128]{1,0:T(8,128)} %own_ref.1) | copy-start | bytes 786436
  1.2 11.5 %collective-permute-start.7 = (f32[4,16,512]{2,1,0:T(8,128)S(1)}, f32[4,16,512]{2,1,0:T(8,128)S(1)}, u32[]{:S(2)}, u32[]{:S(2)}) collective-permute-start(f32[4,16,512]{2,1,0:T(8,128)S(1)} %pad_maximum_fusion.2), channel_id=1, source_target_pairs={{0,1},{1,2},{2,3},{3,0},{4,5},{5,6},{6,7},{7,4},{8,9},{9,10},{10,1... | collective-permute-start | bytes 393224 | tf_op jit(solution)/shard_map/ppermute | solution.py:439
  4.3 14.2 %collective-permute-start.6 = (f32[4,16,512]{2,1,0:T(8,128)S(1)}, f32[4,16,512]{2,1,0:T(8,128)S(1)}, u32[]{:S(2)}, u32[]{:S(2)}) collective-permute-start(f32[4,16,512]{2,1,0:T(8,128)S(1)} %pad_maximum_fusion.2), channel_id=1, source_target_pairs={{0,3},{1,0},{2,1},{3,2},{4,7},{5,4},{6,5},{7,6},{8,11},{9,8},{10,9... | collective-permute-start | bytes 393224 | tf_op jit(solution)/shard_map/ppermute | solution.py:439
  12.7 7.5 %collective-permute-start.8 = (f32[4,16,512]{2,1,0:T(8,128)S(1)}, f32[4,16,512]{2,1,0:T(8,128)S(1)}, u32[]{:S(2)}, u32[]{:S(2)}) collective-permute-start(f32[4,16,512]{2,1,0:T(8,128)S(1)} %collective-permute-done.7), channel_id=1, source_target_pairs={{0,1},{1,2},{2,3},{3,0},{4,5},{5,6},{6,7},{7,4},{8,9},{9,10},{10,1... | collective-permute-start | bytes 393224 | tf_op jit(solution)/shard_map/ppermute | solution.py:439
  12.9 8.8 %collective-permute-start = (f32[16,512]{1,0:T(8,128)S(1)}, f32[16,512]{1,0:T(8,128)S(1)}, u32[]{:S(2)}, u32[]{:S(2)}) collective-permute-start(f32[16,512]{1,0:T(8,128)S(1)} %get-tuple-element.85), channel_id=1, source_target_pairs={{16,0},{32,16},{48,32},{64,48},{80,64},{96,80},{112,96},{128,112},... | collective-permute-start | bytes 98312 | tf_op jit(solution)/shard_map/ppermute | solution.py:444
  15.6 6.9 %collective-permute-start.1 = (f32[16,512]{1,0:T(8,128)S(1)}, f32[16,512]{1,0:T(8,128)S(1)}, u32[]{:S(2)}, u32[]{:S(2)}) collective-permute-start(f32[16,512]{1,0:T(8,128)S(1)} %get-tuple-element.86), channel_id=1, source_target_pairs={{0,16},{16,32},{32,48},{48,64},{64,80},{80,96},{96,112},{112,128},... | collective-permute-start | bytes 98312 | tf_op jit(solution)/shard_map/ppermute | solution.py:444
  20.2 19.6 %collective-permute-start.10 = (f32[4,64,512]{2,1,0:T(8,128)S(1)}, f32[4,64,512]{2,1,0:T(8,128)S(1)}, u32[]{:S(2)}, u32[]{:S(2)}) collective-permute-start(f32[4,64,512]{2,1,0:T(8,128)S(1)} %pad_maximum_fusion.near_ref), channel_id=1, source_target_pairs={{0,4},{4,8},{8,12},{12,0},{1,5},{5,9},{9,13},{13,1},{2,6},{6,10},{... | collective-permute-start | bytes 1572872 | tf_op jit(solution)/shard_map/ppermute | solution.py:439
  21.5 18.4 %collective-permute-start.9 = (f32[4,64,512]{2,1,0:T(8,128)S(1)}, f32[4,64,512]{2,1,0:T(8,128)S(1)}, u32[]{:S(2)}, u32[]{:S(2)}) collective-permute-start(f32[4,64,512]{2,1,0:T(8,128)S(1)} %pad_maximum_fusion.near_ref), channel_id=1, source_target_pairs={{0,12},{4,0},{8,4},{12,8},{1,13},{5,1},{9,5},{13,9},{2,14},{6,2},{... | collective-permute-start | bytes 1572872 | tf_op jit(solution)/shard_map/ppermute | solution.py:439
  22.5 12.0 %collective-permute-start.2 = (f32[2,16,512]{2,1,0:T(8,128)S(1)}, f32[2,16,512]{2,1,0:T(8,128)S(1)}, u32[]{:S(2)}, u32[]{:S(2)}) collective-permute-start(f32[2,16,512]{2,1,0:T(8,128)S(1)} %pad_maximum_fusion.3), channel_id=1, source_target_pairs={{0,12},{4,0},{8,4},{12,8},{1,13},{5,1},{9,5},{13,9},{2,14},{6,2},{... | collective-permute-start | bytes 196616 | tf_op jit(solution)/shard_map/ppermute | solution.py:439
  24.1 12.2 %collective-permute-start.3 = (f32[2,16,512]{2,1,0:T(8,128)S(1)}, f32[2,16,512]{2,1,0:T(8,128)S(1)}, u32[]{:S(2)}, u32[]{:S(2)}) collective-permute-start(f32[2,16,512]{2,1,0:T(8,128)S(1)} %pad_maximum_fusion.3), channel_id=1, source_target_pairs={{0,8},{4,12},{8,0},{12,4},{1,9},{5,13},{9,1},{13,5},{2,10},{6,14},... | collective-permute-start | bytes 196616 | tf_op jit(solution)/shard_map/ppermute | solution.py:439
  25.1 11.3 %collective-permute-start.4 = (f32[2,16,512]{2,1,0:T(8,128)S(1)}, f32[2,16,512]{2,1,0:T(8,128)S(1)}, u32[]{:S(2)}, u32[]{:S(2)}) collective-permute-start(f32[2,16,512]{2,1,0:T(8,128)S(1)} %pad_maximum_fusion.3), channel_id=1, source_target_pairs={{0,4},{4,8},{8,12},{12,0},{1,5},{5,9},{9,13},{13,1},{2,6},{6,10},{... | collective-permute-start | bytes 196616 | tf_op jit(solution)/shard_map/ppermute | solution.py:439
  36.4 10.2 %collective-permute-start.13 = (f32[2,64,512]{2,1,0:T(8,128)S(1)}, f32[2,64,512]{2,1,0:T(8,128)S(1)}, u32[]{:S(2)}, u32[]{:S(2)}) collective-permute-start(f32[2,64,512]{2,1,0:T(8,128)S(1)} %pad_maximum_fusion.1.near_ref), channel_id=1, source_target_pairs={{0,3},{1,0},{2,1},{3,2},{4,7},{5,4},{6,5},{7,6},{8,11},{9,8},{10,9... | collective-permute-start | bytes 786440 | tf_op jit(solution)/shard_map/ppermute | solution.py:439
  39.8 8.7 %collective-permute-start.12 = (f32[2,64,512]{2,1,0:T(8,128)S(1)}, f32[2,64,512]{2,1,0:T(8,128)S(1)}, u32[]{:S(2)}, u32[]{:S(2)}) collective-permute-start(f32[2,64,512]{2,1,0:T(8,128)S(1)} %pad_maximum_fusion.1.near_ref), channel_id=1, source_target_pairs={{0,1},{1,2},{2,3},{3,0},{4,5},{5,6},{6,7},{7,4},{8,9},{9,10},{10,1... | collective-permute-start | bytes 786440 | tf_op jit(solution)/shard_map/ppermute | solution.py:439
  39.9 11.1 %collective-permute-start.11 = (f32[4,32,512]{2,1,0:T(8,128)S(1)}, f32[4,32,512]{2,1,0:T(8,128)S(1)}, u32[]{:S(2)}, u32[]{:S(2)}) collective-permute-start(f32[4,32,512]{2,1,0:T(8,128)S(1)} %slice.65), channel_id=1, source_target_pairs={{0,4},{4,8},{8,12},{12,0},{1,5},{5,9},{9,13},{13,1},{2,6},{6,10},{... | collective-permute-start | bytes 786440 | tf_op jit(solution)/shard_map/ppermute | solution.py:439
  40.0 11.0 %collective-permute-start.14 = (f32[4,32,512]{2,1,0:T(8,128)S(1)}, f32[4,32,512]{2,1,0:T(8,128)S(1)}, u32[]{:S(2)}, u32[]{:S(2)}) collective-permute-start(f32[4,32,512]{2,1,0:T(8,128)S(1)} %slice.67), channel_id=1, source_target_pairs={{0,12},{4,0},{8,4},{12,8},{1,13},{5,1},{9,5},{13,9},{2,14},{6,2},{... | collective-permute-start | bytes 786440 | tf_op jit(solution)/shard_map/ppermute | solution.py:439
  41.5 24.6 %collective-permute-start.5 = (f32[256,128]{1,0:T(8,128)S(1)}, f32[256,128]{1,0:T(8,128)S(1)}, u32[]{:S(2)}, u32[]{:S(2)}) collective-permute-start(f32[256,128]{1,0:T(8,128)S(1)} %slice.50), channel_id=1, source_target_pairs={{16,0},{32,16},{48,32},{64,48},{80,64},{96,80},{112,96},{128,112},... | collective-permute-start | bytes 393224 | tf_op jit(solution)/shard_map/ppermute | solution.py:444
  48.5 11.6 %collective-permute-start.16 = (f32[2,32,512]{2,1,0:T(8,128)S(1)}, f32[2,32,512]{2,1,0:T(8,128)S(1)}, u32[]{:S(2)}, u32[]{:S(2)}) collective-permute-start(f32[2,32,512]{2,1,0:T(8,128)S(1)} %slice.68), channel_id=1, source_target_pairs={{0,3},{1,0},{2,1},{3,2},{4,7},{5,4},{6,5},{7,6},{8,11},{9,8},{10,9... | collective-permute-start | bytes 393224 | tf_op jit(solution)/shard_map/ppermute | solution.py:439
  50.0 10.2 %collective-permute-start.15 = (f32[2,32,512]{2,1,0:T(8,128)S(1)}, f32[2,32,512]{2,1,0:T(8,128)S(1)}, u32[]{:S(2)}, u32[]{:S(2)}) collective-permute-start(f32[2,32,512]{2,1,0:T(8,128)S(1)} %slice.66), channel_id=1, source_target_pairs={{0,1},{1,2},{2,3},{3,0},{4,5},{5,6},{6,7},{7,4},{8,9},{9,10},{10,1... | collective-permute-start | bytes 393224 | tf_op jit(solution)/shard_map/ppermute | solution.py:439
  70.5 13.2 %collective-permute-start.17 = (f32[6,256,256]{2,1,0:T(8,128)S(1)}, f32[6,256,256]{2,1,0:T(8,128)S(1)}, u32[]{:S(2)}, u32[]{:S(2)}) collective-permute-start(f32[6,256,256]{2,1,0:T(8,128)S(1)} %get-tuple-element.58.mine_ref), channel_id=1, source_target_pairs={{0,16},{16,0},{1,17},{17,1},{2,18},{18,2},{3,19},{19,3},{4,20},{20... | collective-permute-start | bytes 4718600 | tf_op jit(solution)/shard_map/ppermute | solution.py:514
  80.1 3.6 %collective-permute-start.18 = (f32[64,1792]{1,0:T(8,128)S(1)}, f32[64,1792]{1,0:T(8,128)S(1)}, u32[]{:S(2)}, u32[]{:S(2)}) collective-permute-start(f32[64,1792]{1,0:T(8,128)S(1)} %get-tuple-element.78), channel_id=1, source_target_pairs={{0,16},{16,0},{1,17},{17,1},{2,18},{18,2},{3,19},{19,3},{4,20},{20... | collective-permute-start | bytes 1376264 | tf_op jit(solution)/shard_map/ppermute | solution.py:515
  83.7 12.1 %collective-permute-start.27 = (f32[768,1024]{1,0:T(8,128)S(1)}, f32[768,1024]{1,0:T(8,128)S(1)}, u32[]{:S(2)}, u32[]{:S(2)}) collective-permute-start(f32[768,1024]{1,0:T(8,128)S(1)} %get-tuple-element.67.rest_ref), channel_id=1, source_target_pairs={{0,16},{16,0},{1,17},{17,1},{2,18},{18,2},{3,19},{19,3},{4,20},{20... | collective-permute-start | bytes 9437192 | tf_op jit(solution)/shard_map/ppermute | solution.py:518
  84.8 2.7 %collective-permute-start.24 = (f32[32,768]{1,0:T(8,128)S(1)}, f32[32,768]{1,0:T(8,128)S(1)}, u32[]{:S(2)}, u32[]{:S(2)}) collective-permute-start(f32[32,768]{1,0:T(8,128)S(1)} %get-tuple-element.79.add_ref), channel_id=1, source_target_pairs={{0,32},{16,48},{1,33},{17,49},{2,34},{18,50},{3,35},{19,51},{4,36}... | collective-permute-start | bytes 294920 | tf_op jit(solution)/shard_map/ppermute | solution.py:526
  85.5 3.1 %collective-permute-start.19 = (f32[32,768]{1,0:T(8,128)S(1)}, f32[32,768]{1,0:T(8,128)S(1)}, u32[]{:S(2)}, u32[]{:S(2)}) collective-permute-start(f32[32,768]{1,0:T(8,128)S(1)} %get-tuple-element.80.add_ref), channel_id=1, source_target_pairs={{0,32},{16,48},{1,33},{17,49},{2,34},{18,50},{3,35},{19,51},{4,36}... | collective-permute-start | bytes 294920 | tf_op jit(solution)/shard_map/ppermute | solution.py:526
  87.9 1.7 %collective-permute-start.25 = (f32[32,768]{1,0:T(8,128)S(1)}, f32[32,768]{1,0:T(8,128)S(1)}, u32[]{:S(2)}, u32[]{:S(2)}) collective-permute-start(f32[32,768]{1,0:T(8,128)S(1)} %hop.16), channel_id=1, source_target_pairs={{32,64},{48,80},{33,65},{49,81},{34,66},{50,82},{35,67},{51,83},{3... | collective-permute-start | bytes 294920 | tf_op jit(solution)/shard_map/ppermute | solution.py:526
  88.9 1.7 %collective-permute-start.20 = (f32[32,768]{1,0:T(8,128)S(1)}, f32[32,768]{1,0:T(8,128)S(1)}, u32[]{:S(2)}, u32[]{:S(2)}) collective-permute-start(f32[32,768]{1,0:T(8,128)S(1)} %hop.12), channel_id=1, source_target_pairs={{32,64},{48,80},{33,65},{49,81},{34,66},{50,82},{35,67},{51,83},{3... | collective-permute-start | bytes 294920 | tf_op jit(solution)/shard_map/ppermute | solution.py:526
  89.9 1.7 %collective-permute-start.26 = (f32[32,768]{1,0:T(8,128)S(1)}, f32[32,768]{1,0:T(8,128)S(1)}, u32[]{:S(2)}, u32[]{:S(2)}) collective-permute-start(f32[32,768]{1,0:T(8,128)S(1)} %hop.17), channel_id=1, source_target_pairs={{64,96},{80,112},{65,97},{81,113},{66,98},{82,114},{67,99},{83,115... | collective-permute-start | bytes 294920 | tf_op jit(solution)/shard_map/ppermute | solution.py:526
  91.0 1.7 %collective-permute-start.21 = (f32[32,768]{1,0:T(8,128)S(1)}, f32[32,768]{1,0:T(8,128)S(1)}, u32[]{:S(2)}, u32[]{:S(2)}) collective-permute-start(f32[32,768]{1,0:T(8,128)S(1)} %hop.13), channel_id=1, source_target_pairs={{64,96},{80,112},{65,97},{81,113},{66,98},{82,114},{67,99},{83,115... | collective-permute-start | bytes 294920 | tf_op jit(solution)/shard_map/ppermute | solution.py:526
  92.0 1.7 %collective-permute-start.30 = (f32[32,768]{1,0:T(8,128)S(1)}, f32[32,768]{1,0:T(8,128)S(1)}, u32[]{:S(2)}, u32[]{:S(2)}) collective-permute-start(f32[32,768]{1,0:T(8,128)S(1)} %hop.18), channel_id=1, source_target_pairs={{96,144},{112,128},{97,145},{113,129},{98,146},{114,130},{99,147},... | collective-permute-start | bytes 294920 | tf_op jit(solution)/shard_map/ppermute | solution.py:526
  93.1 1.7 %collective-permute-start.22 = (f32[32,768]{1,0:T(8,128)S(1)}, f32[32,768]{1,0:T(8,128)S(1)}, u32[]{:S(2)}, u32[]{:S(2)}) collective-permute-start(f32[32,768]{1,0:T(8,128)S(1)} %hop.14), channel_id=1, source_target_pairs={{96,144},{112,128},{97,145},{113,129},{98,146},{114,130},{99,147},... | collective-permute-start | bytes 294920 | tf_op jit(solution)/shard_map/ppermute | solution.py:526
  94.1 5.8 %collective-permute-start.31 = (f32[32,768]{1,0:T(8,128)S(1)}, f32[32,768]{1,0:T(8,128)S(1)}, u32[]{:S(2)}, u32[]{:S(2)}) collective-permute-start(f32[32,768]{1,0:T(8,128)S(1)} %hop.21), channel_id=1, source_target_pairs={{128,160},{144,176},{129,161},{145,177},{130,162},{146,178},{131,1... | collective-permute-start | bytes 294920 | tf_op jit(solution)/shard_map/ppermute | solution.py:526
  95.2 6.5 %collective-permute-start.23 = (f32[32,768]{1,0:T(8,128)S(1)}, f32[32,768]{1,0:T(8,128)S(1)}, u32[]{:S(2)}, u32[]{:S(2)}) collective-permute-start(f32[32,768]{1,0:T(8,128)S(1)} %hop.15), channel_id=1, source_target_pairs={{128,160},{144,176},{129,161},{145,177},{130,162},{146,178},{131,1... | collective-permute-start | bytes 294920 | tf_op jit(solution)/shard_map/ppermute | solution.py:526
  100.3 17.6 %collective-permute-start.32 = (f32[32,768]{1,0:T(8,128)S(1)}, f32[32,768]{1,0:T(8,128)S(1)}, u32[]{:S(2)}, u32[]{:S(2)}) collective-permute-start(f32[32,768]{1,0:T(8,128)S(1)} %hop.22), channel_id=1, source_target_pairs={{160,192},{176,208},{161,193},{177,209},{162,194},{178,210},{163,1... | collective-permute-start | bytes 294920 | tf_op jit(solution)/shard_map/ppermute | solution.py:526
  102.0 18.6 %collective-permute-start.28 = (f32[32,768]{1,0:T(8,128)S(1)}, f32[32,768]{1,0:T(8,128)S(1)}, u32[]{:S(2)}, u32[]{:S(2)}) collective-permute-start(f32[32,768]{1,0:T(8,128)S(1)} %hop.19), channel_id=1, source_target_pairs={{160,192},{176,208},{161,193},{177,209},{162,194},{178,210},{163,1... | collective-permute-start | bytes 294920 | tf_op jit(solution)/shard_map/ppermute | solution.py:526
  118.3 4.0 %collective-permute-start.33 = (f32[32,768]{1,0:T(8,128)S(1)}, f32[32,768]{1,0:T(8,128)S(1)}, u32[]{:S(2)}, u32[]{:S(2)}) collective-permute-start(f32[32,768]{1,0:T(8,128)S(1)} %hop.23), channel_id=1, source_target_pairs={{192,224},{208,240},{193,225},{209,241},{194,226},{210,242},{195,2... | collective-permute-start | bytes 294920 | tf_op jit(solution)/shard_map/ppermute | solution.py:526
  121.0 3.3 %collective-permute-start.29 = (f32[32,768]{1,0:T(8,128)S(1)}, f32[32,768]{1,0:T(8,128)S(1)}, u32[]{:S(2)}, u32[]{:S(2)}) collective-permute-start(f32[32,768]{1,0:T(8,128)S(1)} %hop.20), channel_id=1, source_target_pairs={{192,224},{208,240},{193,225},{209,241},{194,226},{210,242},{195,2... | collective-permute-start | bytes 294920 | tf_op jit(solution)/shard_map/ppermute | solution.py:526
  125.8 4.3 %collective-permute-start.34 = (f32[64,512]{1,0:T(8,128)S(1)}, f32[64,512]{1,0:T(8,128)S(1)}, u32[]{:S(2)}, u32[]{:S(2)}) collective-permute-start(f32[64,512]{1,0:T(8,128)S(1)} %broadcast_select_fusion), channel_id=1, source_target_pairs={{0,16},{16,0},{1,17},{17,1},{2,18},{18,2},{3,19},{19,3},{4,20},{20... | collective-permute-start | bytes 393224 | tf_op jit(solution)/shard_map/ppermute | solution.py:546
  126.9 6.9 %collective-permute-start.35 = (f32[64,512]{1,0:T(8,128)S(1)}, f32[64,512]{1,0:T(8,128)S(1)}, u32[]{:S(2)}, u32[]{:S(2)}) collective-permute-start(f32[64,512]{1,0:T(8,128)S(1)} %get-tuple-element.76), channel_id=1, source_target_pairs={{32,16},{64,48},{96,80},{128,112},{160,144},{192,176},{224,208},{3... | collective-permute-start | bytes 393224 | tf_op jit(solution)/shard_map/ppermute | solution.py:544
  128.2 6.4 %collective-permute-start.36 = (f32[64,512]{1,0:T(8,128)S(1)}, f32[64,512]{1,0:T(8,128)S(1)}, u32[]{:S(2)}, u32[]{:S(2)}) collective-permute-start(f32[64,512]{1,0:T(8,128)S(1)} %get-tuple-element.76), channel_id=1, source_target_pairs={{48,16},{80,48},{112,80},{144,112},{176,144},{208,176},{240,208},{... | collective-permute-start | bytes 393224 | tf_op jit(solution)/shard_map/ppermute | solution.py:544

commit v4 on v3

--- a/solution.py
+++ b/solution.py
@@ -311,7 +311,7 @@
     )(state, high, low, add)
 
 
-def ending_body(odd_ref, mine_ref, other_ref, rest_ref, other_rest_ref, keep_ref, got_ref, high_ref, low_ref, add_ref):
+def ending_body(odd_ref, mine_ref, other_ref, rest_ref, other_rest_ref, keep_ref, got_ref, keep_late_ref, got_late_ref, high_ref, low_ref, add_ref):
     n = mine_ref.shape[1]
     odd = odd_ref[0] == 1
     for k in range(3):
@@ -331,27 +331,27 @@
         rows = slice(k * n, (k + 1) * n)
         high_ref[rows, 2 * n :], low_ref[rows, 2 * n :] = split(total)
     even_add = jnp.where(odd, got_ref[...], keep_ref[...])
-    odd_add = jnp.where(odd, keep_ref[...], got_ref[...])
-    total = odd_add[:, 3 * n :]
+    even_late = jnp.where(odd, got_late_ref[...], keep_late_ref[...])
+    total = jnp.where(odd, keep_late_ref[...], got_late_ref[...])
     for j in range(3):
         total = total + dot3(split(even_add[:, j * n : (j + 1) * n]), odd_parts[j])
-    add_ref[:, : 2 * n] = even_add[:, 3 * n : 5 * n]
+    add_ref[:, : 2 * n] = even_late[:, : 2 * n]
     add_ref[:, 2 * n :] = total
 
 
-def ending(odd, mine, other, rest, other_rest, keep, got):
+def ending(odd, mine, other, rest, other_rest, *adds):
     n = mine.shape[1]
     vmem = pl.BlockSpec(memory_space=pltpu.VMEM)
     wide = jax.ShapeDtypeStruct((3 * n, 6 * n), jnp.bfloat16)
     return pl.pallas_call(
         ending_body,
-        out_shape=(wide, wide, jax.ShapeDtypeStruct((keep.shape[0], 6 * n), jnp.float32)),
-        in_specs=[pl.BlockSpec(memory_space=pltpu.SMEM)] + [vmem] * 6,
+        out_shape=(wide, wide, jax.ShapeDtypeStruct((adds[0].shape[0], 6 * n), jnp.float32)),
+        in_specs=[pl.BlockSpec(memory_space=pltpu.SMEM)] + [vmem] * 8,
         out_specs=(vmem,) * 3,
         compiler_params=pltpu.CompilerParams(vmem_limit_bytes=16 * 1024 * 1024),
         interpret=INTERPRET,
         name="ending",
-    )(odd, mine, other, rest, other_rest, keep, got)
+    )(odd, mine, other, rest, other_rest, *adds)
 
 
 def finish_body(*refs):
@@ -509,13 +509,15 @@
     swap = [(0, 1), (1, 0)]
     half = add.shape[0] // 2
     halves = add.reshape(2, half, 7 * n)
-    keep = jnp.where(takes_second, halves[1], halves[0])
-    give = jnp.where(takes_second, halves[0], halves[1])
+    mine, theirs = jnp.where(takes_second, halves[1], halves[0]), jnp.where(takes_second, halves[0], halves[1])
+    keep, keep_late = mine[:, : 3 * n], mine[:, 3 * n :]
+    give, give_late = theirs[:, : 3 * n], theirs[:, 3 * n :]
     other = lax.ppermute(step, "core", swap)
     got = lax.ppermute(give, "core", swap)
-    rest, other, got = lax.optimization_barrier((rest, other, got))
+    rest, give_late, other, got = lax.optimization_barrier((rest, give_late, other, got))
     chip_add = merge_add(odd, step, other, keep, got)
     other_rest = lax.ppermute(rest, "core", swap)
+    got_late = lax.ppermute(give_late, "core", swap)
     high, low = merge_map(odd, step, other)
 
     sub = half // SUBS
@@ -533,7 +535,7 @@
             sent = hop_on(arrived[k][-1], high, low, adds[k])
             arrived[k].append(onward(sent, hop))
         if hop == 4:
-            ended = ending(odd, step, other, after_these(rest, [sent]), other_rest, keep, got)
+            ended = ending(odd, step, other, after_these(rest, [sent]), other_rest, keep, got, keep_late, got_late)
         if hop == 5:
             for values in arrived:
                 values[-1] = after_these(values[-1], ended)

time: 136 us -> 136 us (level)
  transfers between devices with their start and end apart: 37 -> 38, of which waited for: 11 -> 11; matrix products, arithmetic and copies ran while one was open for 1% -> 1% of each run, Pallas kernels for 19% -> 19%
where the time goes in v4:
time: 136 us
  starting transfers between devices  55.6 us (41%)
  waiting for transfers between devices  44.5 us (33%)
  Pallas kernels  32.8 us (24%)
    ppermute x14, waiting for transfers between devices, ring(): lax.ppermute(value, axis, [(k, (k + step) % count) for k in range(count)])  19.5 us
    ppermute x14, starting transfers between devices, ring(): lax.ppermute(value, axis, [(k, (k + step) % count) for k in range(count)])  18.7 us
    ppermute x14, waiting for transfers between devices, onward(): lax.ppermute(value, ROW, [(2 * hop - 2 + side, 2 * hop + (side ^ turn)) f...  17.5 us
    pallas_call x2, Pallas kernels, prepare(): pl.pallas_call(functools.partial(prepare_body, outer_y), out_shape=(out,...  15.1 us
    ppermute x14, starting transfers between devices, onward(): lax.ppermute(value, ROW, [(2 * hop - 2 + side, 2 * hop + (side ^ turn)) f...  11.8 us
    ppermute x3, starting transfers between devices, shifted(): lax.ppermute(value, ROW, [(k, k + step) for k in range(max(0, -step), min...  10.6 us
    ppermute x1, starting transfers between devices, shards(): other = lax.ppermute(step, 'core', swap)  9.48 us
    ppermute x2, waiting for transfers between devices, shards(): handed.append(lax.ppermute(for_prior, ROW, pairs))  4.45 us
  transfers between devices with their start and end apart: 38, of which 11 were waited for; matrix products, arithmetic and copies ran while one was open for 1% of the time, Pallas kernels for 19%

profile of v4, /device:TPU:45, one launch (start us, length us, event | category | flops | bytes accessed | tf_op | source)
XLA Modules:
  0.0 135.6 jit_solution(855998821482871007)
XLA Ops:
  0.3 0.9 slice_bitcast_fusion.3
  1.2 3.1 %collective-permute-start.7 = (f32[4,16,512]{2,1,0:T(8,128)S(1)}, f32[4,16,512]{2,1,0:T(8,128)S(1)}, u32[]{:S(2)}, u32[]{:S(2)}) collective-permute-start(f32[4,16,512]{2,1,0:T(8,128)S(1)} %pad_maximum_fusion.2), channel_id=1, source_target_pairs={{0,1},{1,2},{2,3},{3,0},{4,5},{5,6},{6,7},{7,4},{8,9},{9,10},{10,1... | collective-permute-start | bytes 393224 | tf_op jit(solution)/shard_map/ppermute | solution.py:439
  4.3 2.2 %collective-permute-start.6 = (f32[4,16,512]{2,1,0:T(8,128)S(1)}, f32[4,16,512]{2,1,0:T(8,128)S(1)}, u32[]{:S(2)}, u32[]{:S(2)}) collective-permute-start(f32[4,16,512]{2,1,0:T(8,128)S(1)} %pad_maximum_fusion.2), channel_id=1, source_target_pairs={{0,3},{1,0},{2,1},{3,2},{4,7},{5,4},{6,5},{7,6},{8,11},{9,8},{10,9... | collective-permute-start | bytes 393224 | tf_op jit(solution)/shard_map/ppermute | solution.py:439
  6.5 6.2 %collective-permute-done.7 = f32[4,16,512]{2,1,0:T(8,128)S(1)} collective-permute-done((f32[4,16,512]{2,1,0:T(8,128)S(1)}, f32[4,16,512]{2,1,0:T(8,128)S(1)}, u32[]{:S(2)}, u32[]{:S(2)}) %collective-permute-start.7) | collective-permute-done | bytes 131104 | tf_op jit(solution)/shard_map/ppermute | solution.py:439
  12.9 2.7 %collective-permute-start = (f32[16,512]{1,0:T(8,128)S(1)}, f32[16,512]{1,0:T(8,128)S(1)}, u32[]{:S(2)}, u32[]{:S(2)}) collective-permute-start(f32[16,512]{1,0:T(8,128)S(1)} %get-tuple-element.87), channel_id=1, source_target_pairs={{16,0},{32,16},{48,32},{64,48},{80,64},{96,80},{112,96},{128,112},... | collective-permute-start | bytes 98312 | tf_op jit(solution)/shard_map/ppermute | solution.py:444
  15.6 2.9 %collective-permute-start.1 = (f32[16,512]{1,0:T(8,128)S(1)}, f32[16,512]{1,0:T(8,128)S(1)}, u32[]{:S(2)}, u32[]{:S(2)}) collective-permute-start(f32[16,512]{1,0:T(8,128)S(1)} %get-tuple-element.88), channel_id=1, source_target_pairs={{0,16},{16,32},{32,48},{48,64},{64,80},{80,96},{96,112},{112,128},... | collective-permute-start | bytes 98312 | tf_op jit(solution)/shard_map/ppermute | solution.py:444
  18.5 1.7 %collective-permute-done.8 = f32[4,16,512]{2,1,0:T(8,128)S(1)} collective-permute-done((f32[4,16,512]{2,1,0:T(8,128)S(1)}, f32[4,16,512]{2,1,0:T(8,128)S(1)}, u32[]{:S(2)}, u32[]{:S(2)}) %collective-permute-start.8) | collective-permute-done | bytes 131104 | tf_op jit(solution)/shard_map/ppermute | solution.py:439
  20.2 1.3 collective-permute-start.10
  21.8 0.8 select_bitcast_fusion
  22.5 1.6 %collective-permute-start.2 = (f32[2,16,512]{2,1,0:T(8,128)S(1)}, f32[2,16,512]{2,1,0:T(8,128)S(1)}, u32[]{:S(2)}, u32[]{:S(2)}) collective-permute-start(f32[2,16,512]{2,1,0:T(8,128)S(1)} %pad_maximum_fusion.3), channel_id=1, source_target_pairs={{0,12},{4,0},{8,4},{12,8},{1,13},{5,1},{9,5},{13,9},{2,14},{6,2},{... | collective-permute-start | bytes 196616 | tf_op jit(solution)/shard_map/ppermute | solution.py:439
  24.1 0.9 collective-permute-start.3
  25.1 1.6 %collective-permute-start.4 = (f32[2,16,512]{2,1,0:T(8,128)S(1)}, f32[2,16,512]{2,1,0:T(8,128)S(1)}, u32[]{:S(2)}, u32[]{:S(2)}) collective-permute-start(f32[2,16,512]{2,1,0:T(8,128)S(1)} %pad_maximum_fusion.3), channel_id=1, source_target_pairs={{0,4},{4,8},{8,12},{12,0},{1,5},{5,9},{9,13},{13,1},{2,6},{6,10},{... | collective-permute-start | bytes 196616 | tf_op jit(solution)/shard_map/ppermute | solution.py:439
  26.7 7.8 %collective-permute-done.2 = f32[2,16,512]{2,1,0:T(8,128)S(1)} collective-permute-done((f32[2,16,512]{2,1,0:T(8,128)S(1)}, f32[2,16,512]{2,1,0:T(8,128)S(1)}, u32[]{:S(2)}, u32[]{:S(2)}) %collective-permute-start.2) | collective-permute-done | bytes 65568 | tf_op jit(solution)/shard_map/ppermute | solution.py:439
  34.5 1.8 %collective-permute-done.3 = f32[2,16,512]{2,1,0:T(8,128)S(1)} collective-permute-done((f32[2,16,512]{2,1,0:T(8,128)S(1)}, f32[2,16,512]{2,1,0:T(8,128)S(1)}, u32[]{:S(2)}, u32[]{:S(2)}) %collective-permute-start.3) | collective-permute-done | bytes 65568 | tf_op jit(solution)/shard_map/ppermute | solution.py:439
  36.4 3.5 %collective-permute-start.13 = (f32[2,64,512]{2,1,0:T(8,128)S(1)}, f32[2,64,512]{2,1,0:T(8,128)S(1)}, u32[]{:S(2)}, u32[]{:S(2)}) collective-permute-start(f32[2,64,512]{2,1,0:T(8,128)S(1)} %pad_maximum_fusion.1.near_ref), channel_id=1, source_target_pairs={{0,3},{1,0},{2,1},{3,2},{4,7},{5,4},{6,5},{7,6},{8,11},{9,8},{10,9... | collective-permute-start | bytes 786440 | tf_op jit(solution)/shard_map/ppermute | solution.py:439
  40.0 1.5 %collective-permute-start.14 = (f32[4,32,512]{2,1,0:T(8,128)S(1)}, f32[4,32,512]{2,1,0:T(8,128)S(1)}, u32[]{:S(2)}, u32[]{:S(2)}) collective-permute-start(f32[4,32,512]{2,1,0:T(8,128)S(1)} %slice.83), channel_id=1, source_target_pairs={{0,12},{4,0},{8,4},{12,8},{1,13},{5,1},{9,5},{13,9},{2,14},{6,2},{... | collective-permute-start | bytes 786440 | tf_op jit(solution)/shard_map/ppermute | solution.py:439
  41.5 5.1 %collective-permute-start.5 = (f32[256,128]{1,0:T(8,128)S(1)}, f32[256,128]{1,0:T(8,128)S(1)}, u32[]{:S(2)}, u32[]{:S(2)}) collective-permute-start(f32[256,128]{1,0:T(8,128)S(1)} %slice.62), channel_id=1, source_target_pairs={{16,0},{32,16},{48,32},{64,48},{80,64},{96,80},{112,96},{128,112},... | collective-permute-start | bytes 393224 | tf_op jit(solution)/shard_map/ppermute | solution.py:444
  46.6 1.9 %collective-permute-done.12.before_ref = f32[2,64,512]{2,1,0:T(8,128)S(1)} collective-permute-done((f32[2,64,512]{2,1,0:T(8,128)S(1)}, f32[2,64,512]{2,1,0:T(8,128)S(1)}, u32[]{:S(2)}, u32[]{:S(2)}) %collective-permute-start.12) | collective-permute-done | bytes 262176 | tf_op jit(solution)/shard_map/ppermute | solution.py:439
  48.5 1.5 %collective-permute-start.16 = (f32[2,32,512]{2,1,0:T(8,128)S(1)}, f32[2,32,512]{2,1,0:T(8,128)S(1)}, u32[]{:S(2)}, u32[]{:S(2)}) collective-permute-start(f32[2,32,512]{2,1,0:T(8,128)S(1)} %slice.84), channel_id=1, source_target_pairs={{0,3},{1,0},{2,1},{3,2},{4,7},{5,4},{6,5},{7,6},{8,11},{9,8},{10,9... | collective-permute-start | bytes 393224 | tf_op jit(solution)/shard_map/ppermute | solution.py:439
  50.0 1.0 collective-permute-start.15
  51.0 9.2 %prepare.2 = (bf16[4,512,512]{2,1,0:T(8,128)(2,1)S(1)}, bf16[4,512,512]{2,1,0:T(8,128)(2,1)S(1)}) custom-call(s32[6]{0:T(128)S(1)} %stack.63.index_ref, f32[4,64,512]{2,1,0:T(8,128)S(1)} %pad_maximum_fusion.near_ref, f32[4,64,512]{2,1,0:T(8,128)S(1)} %collective-permute-done.9.after_ref, f32[4,64,512]{2,1,0:T(8,128)S(1)} %collective-permute-done.10.before_ref, ...), custom_call_target="tpu_custom_call" | custom-call | flops 2000000000 | bytes 1000000 | tf_op jit(solution)/shard_map/prepare/pallas_call | solution.py:117
  60.2 5.9 %prepare.3 = (bf16[2,512,512]{2,1,0:T(8,128)(2,1)S(1)}, bf16[2,512,512]{2,1,0:T(8,128)(2,1)S(1)}) custom-call(s32[4]{0:T(128)S(1)} %pad_add_fusion.index_ref, f32[2,64,512]{2,1,0:T(8,128)S(1)} %pad_maximum_fusion.1.near_ref, f32[2,64,512]{2,1,0:T(8,128)S(1)} %collective-permute-done.13.after_ref, f32[2,64,512]{2,1,0:T(8,128)S(1)} %collective-permute-done.12.before_ref, ...), custom_call_target="tpu_custom_call" | custom-call | flops 2000000000 | bytes 1000000 | tf_op jit(solution)/shard_map/prepare/pallas_call | solution.py:117
  66.1 4.4 %operate.1 = (f32[6,256,256]{2,1,0:T(8,128)S(1)}, f32[768,1024]{1,0:T(8,128)S(1)}, f32[128,1792]{1,0:T(8,128)S(1)}) custom-call(s32[2]{0:T(128)S(1)} %add_convert_fusion.1.ends_ref, f32[256,128]{1,0:T(8,128)S(1)} %collective-permute-done.5.data_ref, f32[512,128]{1,0:T(8,128)S(1)} %copy-done, bf16[4,512,512]{2,1,0:T(8,128)(2,1)S(1)} %get-tuple-element.53.ah, ...), custom_call_target="tpu_custom_call" | custom-call | tf_op jit(solution)/shard_map/operate/pallas_call | solution.py:212
  70.5 9.5 %collective-permute-start.17 = (f32[6,256,256]{2,1,0:T(8,128)S(1)}, f32[6,256,256]{2,1,0:T(8,128)S(1)}, u32[]{:S(2)}, u32[]{:S(2)}) collective-permute-start(f32[6,256,256]{2,1,0:T(8,128)S(1)} %get-tuple-element.59.mine_ref), channel_id=1, source_target_pairs={{0,16},{16,0},{1,17},{17,1},{2,18},{18,2},{3,19},{19,3},{4,20},{20... | collective-permute-start | bytes 4718600 | tf_op jit(solution)/shard_map/ppermute | solution.py:515
  80.2 3.1 %collective-permute-done.18.got_ref = f32[64,768]{1,0:T(8,128)S(1)} collective-permute-done((f32[64,768]{1,0:T(8,128)S(1)}, f32[64,768]{1,0:T(8,128)S(1)}, u32[]{:S(2)}, u32[]{:S(2)}) %collective-permute-start.18) | collective-permute-done | bytes 196640 | tf_op jit(solution)/shard_map/ppermute | solution.py:516
  83.3 0.4 collective-permute-start.27
  83.7 0.7 merge_add.1
  84.4 0.7 collective-permute-start.24
  85.1 0.7 collective-permute-start.19
  85.8 1.3 merge_map.1
  87.1 0.4 hop.16
  87.5 0.7 collective-permute-start.25
  88.2 0.4 hop.12
  88.5 0.7 collective-permute-start.20
  89.6 0.7 collective-permute-start.26
  90.3 0.4 hop.13
  90.6 0.7 collective-permute-start.21
  91.9 0.7 collective-permute-start.31
  92.6 0.4 hop.14
  92.9 0.7 collective-permute-start.22
  93.6 0.4 hop.21
  94.0 0.7 collective-permute-start.32
  94.6 0.4 hop.15
  95.0 0.7 collective-permute-start.23
  95.7 4.1 %ending.1 = (bf16[768,1536]{1,0:T(8,128)(2,1)S(1)}, bf16[768,1536]{1,0:T(8,128)(2,1)S(1)}, f32[64,1536]{1,0:T(8,128)S(1)}) custom-call(s32[1]{0:T(128)S(6)} %reshape.9.odd_ref, f32[6,256,256]{2,1,0:T(8,128)S(1)} %get-tuple-element.59.mine_ref, f32[6,256,256]{2,1,0:T(8,128)S(1)} %collective-permute-done.17.other_ref, ...), custom_call_target="tpu_custom_call" | custom-call | tf_op jit(solution)/shard_map/ending/pallas_call | solution.py:346
  99.9 0.4 hop.22
  100.2 1.3 collective-permute-start.33
  101.5 0.4 hop.19
  101.9 1.3 collective-permute-start.29
  103.2 14.4 %collective-permute-done.33.state_ref.refs_12_ = f32[32,768]{1,0:T(8,128)S(1)} collective-permute-done((f32[32,768]{1,0:T(8,128)S(1)}, f32[32,768]{1,0:T(8,128)S(1)}, u32[]{:S(2)}, u32[]{:S(2)}) %collective-permute-start.33) | collective-permute-done | bytes 98336 | tf_op jit(solution)/shard_map/ppermute | solution.py:528
  117.6 0.4 hop.23
  117.9 1.3 collective-permute-start.34
  119.2 1.1 collective-permute-done.29.state_ref.refs_5_
  120.3 0.4 hop.20
  120.7 1.3 collective-permute-start.30
  122.0 2.0 %collective-permute-done.30.refs_6_ = f32[32,768]{1,0:T(8,128)S(1)} collective-permute-done((f32[32,768]{1,0:T(8,128)S(1)}, f32[32,768]{1,0:T(8,128)S(1)}, u32[]{:S(2)}, u32[]{:S(2)}) %collective-permute-start.30) | collective-permute-done | bytes 98336 | tf_op jit(solution)/shard_map/ppermute | solution.py:528
  124.0 0.5 finish.1
  124.5 0.9 finish_own.1
  125.5 1.1 collective-permute-start.35
  126.5 1.3 collective-permute-start.36
  127.8 1.9 %collective-permute-start.37 = (f32[64,512]{1,0:T(8,128)S(1)}, f32[64,512]{1,0:T(8,128)S(1)}, u32[]{:S(2)}, u32[]{:S(2)}) collective-permute-start(f32[64,512]{1,0:T(8,128)S(1)} %get-tuple-element.78), channel_id=1, source_target_pairs={{48,16},{80,48},{112,80},{144,112},{176,144},{208,176},{240,208},{... | collective-permute-start | bytes 393224 | tf_op jit(solution)/shard_map/ppermute | solution.py:546
  129.7 3.7 %collective-permute-done.36.hand0_ref = f32[64,512]{1,0:T(8,128)S(1)} collective-permute-done((f32[64,512]{1,0:T(8,128)S(1)}, f32[64,512]{1,0:T(8,128)S(1)}, u32[]{:S(2)}, u32[]{:S(2)}) %collective-permute-start.36) | collective-permute-done | bytes 131104 | tf_op jit(solution)/shard_map/ppermute | solution.py:546
  133.5 0.7 collective-permute-done.37.hand1_ref
  134.2 1.4 %close.1 = f32[512,128]{1,0:T(8,128)} custom-call(s32[4]{0:T(128)S(1)} %add_convert_fusion.places_ref, f32[64,512]{1,0:T(8,128)S(1)} %collective-permute-done.35.got_ref, f32[64,512]{1,0:T(8,128)S(1)} %collective-permute-done.36.hand0_ref, f32[64,512]{1,0:T(8,128)S(1)} %collective-permute-done.37.hand1_ref, f32[64,512]{1,0:T(8,128)S(1)} %get-tuple-element.76.even_ref, ...), custom_call_target="tpu_custom_call" | custom-call | tf_op jit(solution)/shard_map/close/pallas_call | solution.py:426
  (57 shorter events, 2.3 us)
Async XLA Ops:
  0.0 41.5 %copy-start = (f32[512,128]{1,0:T(8,128)S(1)}, f32[512,128]{1,0:T(8,128)}, u32[]{:S(2)}) copy-start(f32[512,128]{1,0:T(8,128)} %own_ref.1) | copy-start | bytes 786436
  1.2 11.5 %collective-permute-start.7 = (f32[4,16,512]{2,1,0:T(8,128)S(1)}, f32[4,16,512]{2,1,0:T(8,128)S(1)}, u32[]{:S(2)}, u32[]{:S(2)}) collective-permute-start(f32[4,16,512]{2,1,0:T(8,128)S(1)} %pad_maximum_fusion.2), channel_id=1, source_target_pairs={{0,1},{1,2},{2,3},{3,0},{4,5},{5,6},{6,7},{7,4},{8,9},{9,10},{10,1... | collective-permute-start | bytes 393224 | tf_op jit(solution)/shard_map/ppermute | solution.py:439
  4.3 14.2 %collective-permute-start.6 = (f32[4,16,512]{2,1,0:T(8,128)S(1)}, f32[4,16,512]{2,1,0:T(8,128)S(1)}, u32[]{:S(2)}, u32[]{:S(2)}) collective-permute-start(f32[4,16,512]{2,1,0:T(8,128)S(1)} %pad_maximum_fusion.2), channel_id=1, source_target_pairs={{0,3},{1,0},{2,1},{3,2},{4,7},{5,4},{6,5},{7,6},{8,11},{9,8},{10,9... | collective-permute-start | bytes 393224 | tf_op jit(solution)/shard_map/ppermute | solution.py:439
  12.7 7.5 %collective-permute-start.8 = (f32[4,16,512]{2,1,0:T(8,128)S(1)}, f32[4,16,512]{2,1,0:T(8,128)S(1)}, u32[]{:S(2)}, u32[]{:S(2)}) collective-permute-start(f32[4,16,512]{2,1,0:T(8,128)S(1)} %collective-permute-done.7), channel_id=1, source_target_pairs={{0,1},{1,2},{2,3},{3,0},{4,5},{5,6},{6,7},{7,4},{8,9},{9,10},{10,1... | collective-permute-start | bytes 393224 | tf_op jit(solution)/shard_map/ppermute | solution.py:439
  12.9 8.8 %collective-permute-start = (f32[16,512]{1,0:T(8,128)S(1)}, f32[16,512]{1,0:T(8,128)S(1)}, u32[]{:S(2)}, u32[]{:S(2)}) collective-permute-start(f32[16,512]{1,0:T(8,128)S(1)} %get-tuple-element.87), channel_id=1, source_target_pairs={{16,0},{32,16},{48,32},{64,48},{80,64},{96,80},{112,96},{128,112},... | collective-permute-start | bytes 98312 | tf_op jit(solution)/shard_map/ppermute | solution.py:444
  15.6 6.9 %collective-permute-start.1 = (f32[16,512]{1,0:T(8,128)S(1)}, f32[16,512]{1,0:T(8,128)S(1)}, u32[]{:S(2)}, u32[]{:S(2)}) collective-permute-start(f32[16,512]{1,0:T(8,128)S(1)} %get-tuple-element.88), channel_id=1, source_target_pairs={{0,16},{16,32},{32,48},{48,64},{64,80},{80,96},{96,112},{112,128},... | collective-permute-start | bytes 98312 | tf_op jit(solution)/shard_map/ppermute | solution.py:444
  20.2 19.6 %collective-permute-start.10 = (f32[4,64,512]{2,1,0:T(8,128)S(1)}, f32[4,64,512]{2,1,0:T(8,128)S(1)}, u32[]{:S(2)}, u32[]{:S(2)}) collective-permute-start(f32[4,64,512]{2,1,0:T(8,128)S(1)} %pad_maximum_fusion.near_ref), channel_id=1, source_target_pairs={{0,4},{4,8},{8,12},{12,0},{1,5},{5,9},{9,13},{13,1},{2,6},{6,10},{... | collective-permute-start | bytes 1572872 | tf_op jit(solution)/shard_map/ppermute | solution.py:439
  21.5 18.4 %collective-permute-start.9 = (f32[4,64,512]{2,1,0:T(8,128)S(1)}, f32[4,64,512]{2,1,0:T(8,128)S(1)}, u32[]{:S(2)}, u32[]{:S(2)}) collective-permute-start(f32[4,64,512]{2,1,0:T(8,128)S(1)} %pad_maximum_fusion.near_ref), channel_id=1, source_target_pairs={{0,12},{4,0},{8,4},{12,8},{1,13},{5,1},{9,5},{13,9},{2,14},{6,2},{... | collective-permute-start | bytes 1572872 | tf_op jit(solution)/shard_map/ppermute | solution.py:439
  22.5 12.0 %collective-permute-start.2 = (f32[2,16,512]{2,1,0:T(8,128)S(1)}, f32[2,16,512]{2,1,0:T(8,128)S(1)}, u32[]{:S(2)}, u32[]{:S(2)}) collective-permute-start(f32[2,16,512]{2,1,0:T(8,128)S(1)} %pad_maximum_fusion.3), channel_id=1, source_target_pairs={{0,12},{4,0},{8,4},{12,8},{1,13},{5,1},{9,5},{13,9},{2,14},{6,2},{... | collective-permute-start | bytes 196616 | tf_op jit(solution)/shard_map/ppermute | solution.py:439
  24.1 12.2 %collective-permute-start.3 = (f32[2,16,512]{2,1,0:T(8,128)S(1)}, f32[2,16,512]{2,1,0:T(8,128)S(1)}, u32[]{:S(2)}, u32[]{:S(2)}) collective-permute-start(f32[2,16,512]{2,1,0:T(8,128)S(1)} %pad_maximum_fusion.3), channel_id=1, source_target_pairs={{0,8},{4,12},{8,0},{12,4},{1,9},{5,13},{9,1},{13,5},{2,10},{6,14},... | collective-permute-start | bytes 196616 | tf_op jit(solution)/shard_map/ppermute | solution.py:439
  25.1 11.3 %collective-permute-start.4 = (f32[2,16,512]{2,1,0:T(8,128)S(1)}, f32[2,16,512]{2,1,0:T(8,128)S(1)}, u32[]{:S(2)}, u32[]{:S(2)}) collective-permute-start(f32[2,16,512]{2,1,0:T(8,128)S(1)} %pad_maximum_fusion.3), channel_id=1, source_target_pairs={{0,4},{4,8},{8,12},{12,0},{1,5},{5,9},{9,13},{13,1},{2,6},{6,10},{... | collective-permute-start | bytes 196616 | tf_op jit(solution)/shard_map/ppermute | solution.py:439
  36.4 10.2 %collective-permute-start.13 = (f32[2,64,512]{2,1,0:T(8,128)S(1)}, f32[2,64,512]{2,1,0:T(8,128)S(1)}, u32[]{:S(2)}, u32[]{:S(2)}) collective-permute-start(f32[2,64,512]{2,1,0:T(8,128)S(1)} %pad_maximum_fusion.1.near_ref), channel_id=1, source_target_pairs={{0,3},{1,0},{2,1},{3,2},{4,7},{5,4},{6,5},{7,6},{8,11},{9,8},{10,9... | collective-permute-start | bytes 786440 | tf_op jit(solution)/shard_map/ppermute | solution.py:439
  39.8 8.7 %collective-permute-start.12 = (f32[2,64,512]{2,1,0:T(8,128)S(1)}, f32[2,64,512]{2,1,0:T(8,128)S(1)}, u32[]{:S(2)}, u32[]{:S(2)}) collective-permute-start(f32[2,64,512]{2,1,0:T(8,128)S(1)} %pad_maximum_fusion.1.near_ref), channel_id=1, source_target_pairs={{0,1},{1,2},{2,3},{3,0},{4,5},{5,6},{6,7},{7,4},{8,9},{9,10},{10,1... | collective-permute-start | bytes 786440 | tf_op jit(solution)/shard_map/ppermute | solution.py:439
  39.9 11.1 %collective-permute-start.11 = (f32[4,32,512]{2,1,0:T(8,128)S(1)}, f32[4,32,512]{2,1,0:T(8,128)S(1)}, u32[]{:S(2)}, u32[]{:S(2)}) collective-permute-start(f32[4,32,512]{2,1,0:T(8,128)S(1)} %slice.81), channel_id=1, source_target_pairs={{0,4},{4,8},{8,12},{12,0},{1,5},{5,9},{9,13},{13,1},{2,6},{6,10},{... | collective-permute-start | bytes 786440 | tf_op jit(solution)/shard_map/ppermute | solution.py:439
  40.0 11.0 %collective-permute-start.14 = (f32[4,32,512]{2,1,0:T(8,128)S(1)}, f32[4,32,512]{2,1,0:T(8,128)S(1)}, u32[]{:S(2)}, u32[]{:S(2)}) collective-permute-start(f32[4,32,512]{2,1,0:T(8,128)S(1)} %slice.83), channel_id=1, source_target_pairs={{0,12},{4,0},{8,4},{12,8},{1,13},{5,1},{9,5},{13,9},{2,14},{6,2},{... | collective-permute-start | bytes 786440 | tf_op jit(solution)/shard_map/ppermute | solution.py:439
  41.5 24.6 %collective-permute-start.5 = (f32[256,128]{1,0:T(8,128)S(1)}, f32[256,128]{1,0:T(8,128)S(1)}, u32[]{:S(2)}, u32[]{:S(2)}) collective-permute-start(f32[256,128]{1,0:T(8,128)S(1)} %slice.62), channel_id=1, source_target_pairs={{16,0},{32,16},{48,32},{64,48},{80,64},{96,80},{112,96},{128,112},... | collective-permute-start | bytes 393224 | tf_op jit(solution)/shard_map/ppermute | solution.py:444
  48.5 11.6 %collective-permute-start.16 = (f32[2,32,512]{2,1,0:T(8,128)S(1)}, f32[2,32,512]{2,1,0:T(8,128)S(1)}, u32[]{:S(2)}, u32[]{:S(2)}) collective-permute-start(f32[2,32,512]{2,1,0:T(8,128)S(1)} %slice.84), channel_id=1, source_target_pairs={{0,3},{1,0},{2,1},{3,2},{4,7},{5,4},{6,5},{7,6},{8,11},{9,8},{10,9... | collective-permute-start | bytes 393224 | tf_op jit(solution)/shard_map/ppermute | solution.py:439
  50.0 10.2 %collective-permute-start.15 = (f32[2,32,512]{2,1,0:T(8,128)S(1)}, f32[2,32,512]{2,1,0:T(8,128)S(1)}, u32[]{:S(2)}, u32[]{:S(2)}) collective-permute-start(f32[2,32,512]{2,1,0:T(8,128)S(1)} %slice.82), channel_id=1, source_target_pairs={{0,1},{1,2},{2,3},{3,0},{4,5},{5,6},{6,7},{7,4},{8,9},{9,10},{10,1... | collective-permute-start | bytes 393224 | tf_op jit(solution)/shard_map/ppermute | solution.py:439
  70.5 12.8 %collective-permute-start.17 = (f32[6,256,256]{2,1,0:T(8,128)S(1)}, f32[6,256,256]{2,1,0:T(8,128)S(1)}, u32[]{:S(2)}, u32[]{:S(2)}) collective-permute-start(f32[6,256,256]{2,1,0:T(8,128)S(1)} %get-tuple-element.59.mine_ref), channel_id=1, source_target_pairs={{0,16},{16,0},{1,17},{17,1},{2,18},{18,2},{3,19},{19,3},{4,20},{20... | collective-permute-start | bytes 4718600 | tf_op jit(solution)/shard_map/ppermute | solution.py:515
  80.1 3.2 %collective-permute-start.18 = (f32[64,768]{1,0:T(8,128)S(1)}, f32[64,768]{1,0:T(8,128)S(1)}, u32[]{:S(2)}, u32[]{:S(2)}) collective-permute-start(f32[64,768]{1,0:T(8,128)S(1)} %slice.86), channel_id=1, source_target_pairs={{0,16},{16,0},{1,17},{17,1},{2,18},{18,2},{3,19},{19,3},{4,20},{20... | collective-permute-start | bytes 589832 | tf_op jit(solution)/shard_map/ppermute | solution.py:516
  83.3 12.4 %collective-permute-start.27 = (f32[768,1024]{1,0:T(8,128)S(1)}, f32[768,1024]{1,0:T(8,128)S(1)}, u32[]{:S(2)}, u32[]{:S(2)}) collective-permute-start(f32[768,1024]{1,0:T(8,128)S(1)} %get-tuple-element.68.rest_ref), channel_id=1, source_target_pairs={{0,16},{16,0},{1,17},{17,1},{2,18},{18,2},{3,19},{19,3},{4,20},{20... | collective-permute-start | bytes 9437192 | tf_op jit(solution)/shard_map/ppermute | solution.py:519
  84.4 2.7 %collective-permute-start.24 = (f32[32,768]{1,0:T(8,128)S(1)}, f32[32,768]{1,0:T(8,128)S(1)}, u32[]{:S(2)}, u32[]{:S(2)}) collective-permute-start(f32[32,768]{1,0:T(8,128)S(1)} %get-tuple-element.81.add_ref), channel_id=1, source_target_pairs={{0,32},{16,48},{1,33},{17,49},{2,34},{18,50},{3,35},{19,51},{4,36}... | collective-permute-start | bytes 294920 | tf_op jit(solution)/shard_map/ppermute | solution.py:528
  85.1 3.1 %collective-permute-start.19 = (f32[32,768]{1,0:T(8,128)S(1)}, f32[32,768]{1,0:T(8,128)S(1)}, u32[]{:S(2)}, u32[]{:S(2)}) collective-permute-start(f32[32,768]{1,0:T(8,128)S(1)} %get-tuple-element.82.add_ref), channel_id=1, source_target_pairs={{0,32},{16,48},{1,33},{17,49},{2,34},{18,50},{3,35},{19,51},{4,36}... | collective-permute-start | bytes 294920 | tf_op jit(solution)/shard_map/ppermute | solution.py:528
  87.5 1.7 %collective-permute-start.25 = (f32[32,768]{1,0:T(8,128)S(1)}, f32[32,768]{1,0:T(8,128)S(1)}, u32[]{:S(2)}, u32[]{:S(2)}) collective-permute-start(f32[32,768]{1,0:T(8,128)S(1)} %hop.16), channel_id=1, source_target_pairs={{32,64},{48,80},{33,65},{49,81},{34,66},{50,82},{35,67},{51,83},{3... | collective-permute-start | bytes 294920 | tf_op jit(solution)/shard_map/ppermute | solution.py:528
  88.5 1.7 %collective-permute-start.20 = (f32[32,768]{1,0:T(8,128)S(1)}, f32[32,768]{1,0:T(8,128)S(1)}, u32[]{:S(2)}, u32[]{:S(2)}) collective-permute-start(f32[32,768]{1,0:T(8,128)S(1)} %hop.12), channel_id=1, source_target_pairs={{32,64},{48,80},{33,65},{49,81},{34,66},{50,82},{35,67},{51,83},{3... | collective-permute-start | bytes 294920 | tf_op jit(solution)/shard_map/ppermute | solution.py:528
  89.6 1.9 %collective-permute-start.26 = (f32[32,768]{1,0:T(8,128)S(1)}, f32[32,768]{1,0:T(8,128)S(1)}, u32[]{:S(2)}, u32[]{:S(2)}) collective-permute-start(f32[32,768]{1,0:T(8,128)S(1)} %hop.17), channel_id=1, source_target_pairs={{64,96},{80,112},{65,97},{81,113},{66,98},{82,114},{67,99},{83,115... | collective-permute-start | bytes 294920 | tf_op jit(solution)/shard_map/ppermute | solution.py:528
  90.6 1.9 %collective-permute-start.21 = (f32[32,768]{1,0:T(8,128)S(1)}, f32[32,768]{1,0:T(8,128)S(1)}, u32[]{:S(2)}, u32[]{:S(2)}) collective-permute-start(f32[32,768]{1,0:T(8,128)S(1)} %hop.13), channel_id=1, source_target_pairs={{64,96},{80,112},{65,97},{81,113},{66,98},{82,114},{67,99},{83,115... | collective-permute-start | bytes 294920 | tf_op jit(solution)/shard_map/ppermute | solution.py:528
  91.3 4.4 %collective-permute-start.28 = (f32[64,1024]{1,0:T(8,128)S(1)}, f32[64,1024]{1,0:T(8,128)S(1)}, u32[]{:S(2)}, u32[]{:S(2)}) collective-permute-start(f32[64,1024]{1,0:T(8,128)S(1)} %slice.85), channel_id=1, source_target_pairs={{0,16},{16,0},{1,17},{17,1},{2,18},{18,2},{3,19},{19,3},{4,20},{20... | collective-permute-start | bytes 786440 | tf_op jit(solution)/shard_map/ppermute | solution.py:520
  91.9 1.7 %collective-permute-start.31 = (f32[32,768]{1,0:T(8,128)S(1)}, f32[32,768]{1,0:T(8,128)S(1)}, u32[]{:S(2)}, u32[]{:S(2)}) collective-permute-start(f32[32,768]{1,0:T(8,128)S(1)} %hop.18), channel_id=1, source_target_pairs={{96,144},{112,128},{97,145},{113,129},{98,146},{114,130},{99,147},... | collective-permute-start | bytes 294920 | tf_op jit(solution)/shard_map/ppermute | solution.py:528
  92.9 1.7 %collective-permute-start.22 = (f32[32,768]{1,0:T(8,128)S(1)}, f32[32,768]{1,0:T(8,128)S(1)}, u32[]{:S(2)}, u32[]{:S(2)}) collective-permute-start(f32[32,768]{1,0:T(8,128)S(1)} %hop.14), channel_id=1, source_target_pairs={{96,144},{112,128},{97,145},{113,129},{98,146},{114,130},{99,147},... | collective-permute-start | bytes 294920 | tf_op jit(solution)/shard_map/ppermute | solution.py:528
  94.0 5.9 %collective-permute-start.32 = (f32[32,768]{1,0:T(8,128)S(1)}, f32[32,768]{1,0:T(8,128)S(1)}, u32[]{:S(2)}, u32[]{:S(2)}) collective-permute-start(f32[32,768]{1,0:T(8,128)S(1)} %hop.21), channel_id=1, source_target_pairs={{128,160},{144,176},{129,161},{145,177},{130,162},{146,178},{131,1... | collective-permute-start | bytes 294920 | tf_op jit(solution)/shard_map/ppermute | solution.py:528
  95.0 6.5 %collective-permute-start.23 = (f32[32,768]{1,0:T(8,128)S(1)}, f32[32,768]{1,0:T(8,128)S(1)}, u32[]{:S(2)}, u32[]{:S(2)}) collective-permute-start(f32[32,768]{1,0:T(8,128)S(1)} %hop.15), channel_id=1, source_target_pairs={{128,160},{144,176},{129,161},{145,177},{130,162},{146,178},{131,1... | collective-permute-start | bytes 294920 | tf_op jit(solution)/shard_map/ppermute | solution.py:528
  100.2 17.4 %collective-permute-start.33 = (f32[32,768]{1,0:T(8,128)S(1)}, f32[32,768]{1,0:T(8,128)S(1)}, u32[]{:S(2)}, u32[]{:S(2)}) collective-permute-start(f32[32,768]{1,0:T(8,128)S(1)} %hop.22), channel_id=1, source_target_pairs={{160,192},{176,208},{161,193},{177,209},{162,194},{178,210},{163,1... | collective-permute-start | bytes 294920 | tf_op jit(solution)/shard_map/ppermute | solution.py:528
  101.9 18.4 %collective-permute-start.29 = (f32[32,768]{1,0:T(8,128)S(1)}, f32[32,768]{1,0:T(8,128)S(1)}, u32[]{:S(2)}, u32[]{:S(2)}) collective-permute-start(f32[32,768]{1,0:T(8,128)S(1)} %hop.19), channel_id=1, source_target_pairs={{160,192},{176,208},{161,193},{177,209},{162,194},{178,210},{163,1... | collective-permute-start | bytes 294920 | tf_op jit(solution)/shard_map/ppermute | solution.py:528
  117.9 4.0 %collective-permute-start.34 = (f32[32,768]{1,0:T(8,128)S(1)}, f32[32,768]{1,0:T(8,128)S(1)}, u32[]{:S(2)}, u32[]{:S(2)}) collective-permute-start(f32[32,768]{1,0:T(8,128)S(1)} %hop.23), channel_id=1, source_target_pairs={{192,224},{208,240},{193,225},{209,241},{194,226},{210,242},{195,2... | collective-permute-start | bytes 294920 | tf_op jit(solution)/shard_map/ppermute | solution.py:528
  120.7 3.3 %collective-permute-start.30 = (f32[32,768]{1,0:T(8,128)S(1)}, f32[32,768]{1,0:T(8,128)S(1)}, u32[]{:S(2)}, u32[]{:S(2)}) collective-permute-start(f32[32,768]{1,0:T(8,128)S(1)} %hop.20), channel_id=1, source_target_pairs={{192,224},{208,240},{193,225},{209,241},{194,226},{210,242},{195,2... | collective-permute-start | bytes 294920 | tf_op jit(solution)/shard_map/ppermute | solution.py:528
  125.5 4.3 %collective-permute-start.35 = (f32[64,512]{1,0:T(8,128)S(1)}, f32[64,512]{1,0:T(8,128)S(1)}, u32[]{:S(2)}, u32[]{:S(2)}) collective-permute-start(f32[64,512]{1,0:T(8,128)S(1)} %broadcast_select_fusion), channel_id=1, source_target_pairs={{0,16},{16,0},{1,17},{17,1},{2,18},{18,2},{3,19},{19,3},{4,20},{20... | collective-permute-start | bytes 393224 | tf_op jit(solution)/shard_map/ppermute | solution.py:548
  126.5 6.9 %collective-permute-start.36 = (f32[64,512]{1,0:T(8,128)S(1)}, f32[64,512]{1,0:T(8,128)S(1)}, u32[]{:S(2)}, u32[]{:S(2)}) collective-permute-start(f32[64,512]{1,0:T(8,128)S(1)} %get-tuple-element.78), channel_id=1, source_target_pairs={{32,16},{64,48},{96,80},{128,112},{160,144},{192,176},{224,208},{3... | collective-permute-start | bytes 393224 | tf_op jit(solution)/shard_map/ppermute | solution.py:546
  127.8 6.4 %collective-permute-start.37 = (f32[64,512]{1,0:T(8,128)S(1)}, f32[64,512]{1,0:T(8,128)S(1)}, u32[]{:S(2)}, u32[]{:S(2)}) collective-permute-start(f32[64,512]{1,0:T(8,128)S(1)} %get-tuple-element.78), channel_id=1, source_target_pairs={{48,16},{80,48},{112,80},{144,112},{176,144},{208,176},{240,208},{... | collective-permute-start | bytes 393224 | tf_op jit(solution)/shard_map/ppermute | solution.py:546
